TPU v7x, 256 devices: a whole 4x4x8 slice. The times are simulated.
256 devices in a mesh: leaf: 64 (over y, z, core), grid: 4 (over x).
Axes of the slice: x: 4, y: 4, z: 8, core: 2. Of those that a mesh axis runs over, the one named last changes fastest.
Arguments:
- source_leaf: float32 [8, 32768], P(None, ('leaf', 'grid')), may hold values from -6 to 6
- block_leaf: float32 [32768, 128], P(('leaf', 'grid')), may hold values from -0.5 to 0.5
- expand_leaf: float32 [32768, 128], P(('leaf', 'grid')), may hold values from -0.5 to 0.5
- basis_leaf: float32 [32768, 256], P(('leaf', 'grid')), may hold values from -0.25 to 0.25
- pivot_leaf: float32 [32768], P(('leaf', 'grid')), may hold values from -2 to 2
- couple_leaf: float32 [65536, 128], P(('leaf', 'grid')), may hold values from -0.5 to 0.5
- ranks_leaf: int32 [64, 2], replicated, may hold values from 32 to 128
- targets_leaf: int32 [65536], P(('leaf', 'grid')), may hold values from 0 to 16383, as said below
- source_middle: float32 [8, 32768], P(None, ('leaf', 'grid')), may hold values from -6 to 6
- block_middle: float32 [32768, 128], P(('leaf', 'grid')), may hold values from -0.5 to 0.5
- expand_middle: float32 [32768, 128], P(('leaf', 'grid')), may hold values from -0.5 to 0.5
- basis_middle: float32 [32768, 256], P(('leaf', 'grid')), may hold values from -0.0625 to 0.0625
- pivot_middle: float32 [32768], P(('leaf', 'grid')), may hold values from -2 to 2
- couple_middle: float32 [32768, 128], P(('leaf', 'grid')), may hold values from -0.5 to 0.5
- ranks_middle: int32 [4, 2], replicated, may hold values from 32 to 128
- targets_middle: int32 [32768], P(('leaf', 'grid')), may hold values from 0 to 32767, as said below
- source_upper: float32 [8, 32768], P(None, ('leaf', 'grid')), may hold values from -6 to 6
- block_upper: float32 [32768, 128], P(('leaf', 'grid')), may hold values from -0.5 to 0.5
- expand_upper: float32 [32768, 128], P(('leaf', 'grid')), may hold values from -0.5 to 0.5
- basis_upper: float32 [32768, 256], P(('leaf', 'grid')), may hold values from -0.046875 to 0.046875
- pivot_upper: float32 [32768], P(('leaf', 'grid')), may hold values from -2 to 2
- couple_upper: float32 [32768, 128], P(('leaf', 'grid')), may hold values from -0.5 to 0.5
- ranks_upper: int32 [2, 2], replicated, may hold values from 32 to 128
- targets_upper: int32 [32768], P(('leaf', 'grid')), may hold values from 0 to 32767, as said below
- source_root: float32 [8, 32768], P(None, ('leaf', 'grid')), may hold values from -6 to 6
- block_root: float32 [32768, 128], P(('leaf', 'grid')), may hold values from -0.5 to 0.5
- expand_root: float32 [32768, 128], P(('leaf', 'grid')), may hold values from -0.5 to 0.5
- basis_root: float32 [32768, 256], P(('leaf', 'grid')), may hold values from -0.03125 to 0.03125
- pivot_root: float32 [32768], P(('leaf', 'grid')), may hold values from -2 to 2
- ranks_root: int32 [1, 2], replicated, may hold values from 32 to 128
Outputs:
- answer_leaf: float32 [8, 32768], P(None, ('leaf', 'grid'))
- answer_middle: float32 [8, 32768], P(None, ('leaf', 'grid'))
- answer_upper: float32 [8, 32768], P(None, ('leaf', 'grid'))
- answer_root: float32 [8, 32768], P(None, ('leaf', 'grid'))
Inputs may be any that keep to these rules, and one draw needn't show every extreme that they name: `targets_leaf`: within one leaf front the 1024 entries are distinct; each names a row of the parent front's row vector of 16384 rows. Split that vector's separator part and its update part each evenly, in order, over the parent's devices (leaf then grid); then the rows of one device name at most 4 rows held by any one of them, and exactly that many for some. `targets_middle`: within one middle front the entries are distinct; each names a row of the parent front's row vector of 32768 rows. Split likewise over the parent's devices, the rows of one device name at most 1 row held by any one of them, and exactly that many for some. `targets_upper`: within one upper front the entries are distinct; each names a row of the root separator. Split evenly in order over all devices, the rows of one device name at most 1 row held by any one of them, and exactly that many for some.
All inputs are finite; a program needn't handle non-finite values.
Results may differ from a plain program's by a relative error of at most 0.0003.
Values sent between devices are 32-bit elements; how exact they have to be, the bound alone decides.
No kernel may reach another device: no remote copies, remote signals or barrier semaphores. Data moves between devices by JAX's collectives and lax.ppermute only.
A program may use at most 128 MiB of HBM per device.

v0:
```python
import functools

import jax
import jax.numpy as jnp
from jax import lax
from jax.experimental import pallas as pl
from jax.experimental.pallas import tpu as pltpu
from jax.sharding import PartitionSpec as P

RHS = 8
LANES = 128
TILE = 128
SLOT = 32
SLOTS_LEAF = 4

F32 = jnp.float32
HIGHEST = lax.Precision.HIGHEST


def dot(a, b, ca, cb):
    return lax.dot_general(
        a, b, (((ca,), (cb,)), ((), ())), precision=HIGHEST, preferred_element_type=F32
    )


def mm(a, b):
    return dot(a, b, 1, 0)


def mmt(a, b):
    return dot(a, b, 1, 1)


def iota(shape, dim):
    return lax.broadcasted_iota(jnp.int32, shape, dim)


def masks(ranks_ref, groups):
    front = lax.axis_index("leaf") // groups
    pair = ranks_ref[pl.ds(front, 1), :]
    lane = iota((1, TILE), 1)
    mh = (lane < pair[:, 0:1]).astype(F32)
    mc = (lane < pair[:, 1:2]).astype(F32)
    return mh, mc


def spread(parts):
    n = parts[0][0].shape[1]
    rows = []
    for values, label in parts:
        rows.append(values)
        tail = SLOT - RHS
        if label is None:
            rows.append(jnp.zeros((tail, n), F32))
        else:
            at = iota((tail, n), 0)
            rows.append(jnp.where(at == 0, jnp.broadcast_to(label, (tail, n)), 0.0))
    left = LANES - SLOT * len(parts)
    if left:
        rows.append(jnp.zeros((left, n), F32))
    return jnp.concatenate(rows, axis=0)


def dest_onehot(dest, count):
    n = dest.shape[1]
    return (iota((count, n), 0) == jnp.broadcast_to(dest, (count, n))).astype(F32)


def split_target(targets, shift):
    piece = lax.shift_right_logical(targets, shift)
    within = jnp.bitwise_and(targets, (1 << shift) - 1)
    dest = lax.shift_right_logical(within, 7)
    label = piece * TILE + jnp.bitwise_and(within, TILE - 1)
    return dest, label.astype(F32)


def leaf_slots(onehot):
    n = onehot.shape[1]
    upper = (iota((n, n), 0) <= iota((n, n), 1)).astype(F32)
    order = lax.dot_general(
        onehot, upper, (((1,), (0,)), ((), ())), preferred_element_type=F32
    )
    return jnp.sum(order * onehot, axis=0, keepdims=True) - 1.0


def label_onehot(got, k, cols):
    count = got.shape[0]
    label = got[:, SLOT * k + RHS : SLOT * k + RHS + 1]
    at = iota((count, cols), 1).astype(F32)
    return (jnp.broadcast_to(label, (count, cols)) == at).astype(F32)


def received(got, slots, cols):
    turned = got.T
    total = None
    for k in range(slots):
        part = mm(turned[SLOT * k : SLOT * k + RHS, :], label_onehot(got, k, cols))
        total = part if total is None else total + part
    return total


def replies(got, rows, slots):
    total = None
    zero = jnp.zeros_like(rows)
    for k in range(slots):
        padded = spread([(rows if j == k else zero, None) for j in range(slots)])
        part = mmt(label_onehot(got, k, rows.shape[1]), padded)
        total = part if total is None else total + part
    return total


def sum_copies(ref, copies, rows):
    total = ref[0:rows, :]
    for i in range(1, copies):
        total = total + ref[rows * i : rows * (i + 1), :]
    return total


def start_kernel(
    src, w, p, q, tl, pm, qm, pu, qu, pr, pivr, first, y0, slot, cross
):
    b = src[...]
    y = mm(b, w[...])
    v = q[:, RANK_AT:]
    first[0:RHS, :] = mm(b, q[:, 0:RANK_AT])
    first[RHS : 2 * RHS, :] = mm(y, v)
    first[2 * RHS :, :] = dot(p[...], v, 0, 0)
    y0[...] = y
    dest, _ = split_target(tl[...], 13)
    slot[...] = leaf_slots(dest_onehot(dest, 64))
    cross[0:TILE, :] = dot(pm[...], qm[:, RANK_AT:], 0, 0)
    cross[TILE : 2 * TILE, :] = dot(pu[...], qu[:, RANK_AT:], 0, 0)
    scaled = pr[...].T * pivr[...]
    cross[2 * TILE :, :] = mm(scaled, pr[...])


RANK_AT = 128


def leaf_up_kernel(s0, s1, s2, s3, y0, p, piv, c, ranks, tl, slot, out, z_out, zp_out, k_out):
    total = (s0[...] + s1[...]) + (s2[...] + s3[...])
    mh, mc = masks(ranks, 1)
    k1 = total[2 * RHS :, :]
    hq = total[0:RHS, :] * mh
    wv = (total[RHS : 2 * RHS, :] + mm(hq, k1)) * mc
    e = -mmt(wv, c[...])
    dest, label = split_target(tl[...], 13)
    pick = dest_onehot(dest, 64)
    at = slot[...]
    parts = []
    for k in range(SLOTS_LEAF):
        on = (at == float(k)).astype(F32)
        parts.append((e * on, label * on))
    out[...] = mmt(pick, spread(parts))
    z = (y0[...] + mmt(hq, p[...])) * piv[...]
    z_out[...] = z
    zp_out[...] = mm(z, p[...])
    k_out[...] = k1


def enter_kernel(slots, has_update, got, src, w, q, part, y0, upd=None):
    g = got[...]
    cols = 2 * TILE if has_update else TILE
    inc = received(g, slots, cols)
    b = src[...] + inc[:, 0:TILE]
    y = mm(b, w[...])
    part[0:RHS, :] = mm(b, q[:, 0:RANK_AT])
    part[RHS:, :] = mm(y, q[:, RANK_AT:])
    y0[...] = y
    if has_update:
        upd[...] = inc[:, TILE:]


def enter_root_kernel(got, src, w, p, q, piv, part, y0):
    inc = received(got[...], 1, TILE)
    b = src[...] + inc
    y = mm(b, w[...])
    part[0:RHS, :] = mm(b, q[:, 0:RANK_AT])
    part[RHS:, :] = mm(y * piv[...], p[...])
    y0[...] = y


def up_kernel(copies, groups, shift, peers, red, y0, upd, p, piv, c, ranks, t, k1, out, z_out, zp_out):
    total = sum_copies(red, copies, 2 * RHS)
    mh, mc = masks(ranks, groups)
    hq = total[0:RHS, :] * mh
    wv = (total[RHS:, :] + mm(hq, k1[...])) * mc
    e = upd[...] - mmt(wv, c[...])
    dest, label = split_target(t[...], shift)
    out[...] = mmt(dest_onehot(dest, peers), spread([(e, label)]))
    z = (y0[...] + mmt(hq, p[...])) * piv[...]
    z_out[...] = z
    zp_out[...] = mm(z, p[...])


def root_kernel(copies, red, y0, w, p, q, piv, ranks, k2, got, answer, reply):
    total = sum_copies(red, copies, 2 * RHS)
    mh, _ = masks(ranks, 64)
    hq = total[0:RHS, :] * mh
    pr = (total[RHS:, :] + mm(hq, k2[...])) * mh
    r = (y0[...] + mmt(hq, p[...])) * piv[...]
    x = mmt(r, w[...]) + mmt(pr, q[:, 0:RANK_AT])
    answer[...] = x
    reply[...] = replies(got[...], x, 1)


def fetch_kernel(shift, peers, back, t, c, zp, part, xu_out):
    dest, _ = split_target(t[...], shift)
    turned = back[...].T
    xu = mm(turned[0:RHS, :], dest_onehot(dest, peers))
    part[0:RHS, :] = mm(xu, c[...])
    part[RHS:, :] = zp[...]
    xu_out[...] = xu


def fetch_leaf_kernel(back, t, slot, c, zp, part):
    dest, _ = split_target(t[...], 13)
    turned = back[...].T
    rows = jnp.concatenate(
        [turned[SLOT * k : SLOT * k + RHS, :] for k in range(SLOTS_LEAF)], axis=0
    )
    both = mm(rows, dest_onehot(dest, 64))
    at = slot[...]
    xu = None
    for k in range(SLOTS_LEAF):
        one = both[RHS * k : RHS * (k + 1), :] * (at == float(k)).astype(F32)
        xu = one if xu is None else xu + one
    part[0:RHS, :] = mm(xu, c[...])
    part[RHS:, :] = zp[...]


def solve(total, z, k1, w, q, mh, mc):
    s = total[0:RHS, :] * mc
    r = z - mmt(s, q[:, RANK_AT:])
    pr = (total[RHS:, :] - mmt(s, k1)) * mh
    return mmt(r, w) + mmt(pr, q[:, 0:RANK_AT])


def down_kernel(copies, groups, slots, red, z, k1, w, q, ranks, xu, got, answer, reply):
    total = sum_copies(red, copies, 2 * RHS)
    mh, mc = masks(ranks, groups)
    x = solve(total, z[...], k1[...], w[...], q[...], mh, mc)
    answer[...] = x
    reply[...] = replies(got[...], jnp.concatenate([x, xu[...]], axis=1), slots)


def leaf_kernel(s0, s1, s2, s3, z, k1, w, q, ranks, answer):
    total = (s0[...] + s1[...]) + (s2[...] + s3[...])
    mh, mc = masks(ranks, 1)
    answer[...] = solve(total, z[...], k1[...], w[...], q[...], mh, mc)


def run(kernel, shapes, *args):
    outs = [jax.ShapeDtypeStruct(s, F32) for s in shapes]
    name = getattr(kernel, "func", kernel).__name__
    single = len(outs) == 1
    return pl.pallas_call(
        kernel,
        out_shape=outs[0] if single else outs,
        name=name,
    )(*args)


def swap(value, axis, mask):
    pairs = [(s, s ^ mask) for s in range(lax.axis_size(axis))]
    return lax.ppermute(value, axis, pairs)


def four(value, axis, unit):
    return [value] + [swap(value, axis, unit * m) for m in (1, 2, 3)]


def add_four(values):
    return (values[0] + values[1]) + (values[2] + values[3])


def share(value, members):
    rows = value.shape[0]
    copies = jnp.broadcast_to(value, (members, *value.shape)).reshape(members * rows, LANES)
    size = lax.axis_size("leaf")
    groups = None
    if members < size:
        groups = [list(range(g, g + members)) for g in range(0, size, members)]
    return lax.all_to_all(
        copies, "leaf", split_axis=0, concat_axis=0, tiled=True, axis_index_groups=groups
    )


def route(messages, members):
    size = lax.axis_size("leaf") * lax.axis_size("grid")
    groups = None
    if members < size:
        groups = [list(range(g, g + members)) for g in range(0, size, members)]
    return lax.all_to_all(
        messages,
        ("leaf", "grid"),
        split_axis=0,
        concat_axis=0,
        tiled=True,
        axis_index_groups=groups,
    )


def shards(
    src_l, w_l, p_l, q_l, piv_l, c_l, ranks_l, t_l,
    src_m, w_m, p_m, q_m, piv_m, c_m, ranks_m, t_m,
    src_u, w_u, p_u, q_u, piv_u, c_u, ranks_u, t_u,
    src_r, w_r, p_r, q_r, piv_r, ranks_r,
):
    t_l, t_m, t_u = (t.reshape(1, -1) for t in (t_l, t_m, t_u))
    piv_l, piv_m, piv_u, piv_r = (v.reshape(1, -1) for v in (piv_l, piv_m, piv_u, piv_r))
    row = (RHS, TILE)
    pair = (2 * RHS, TILE)

    first, y_l, slot_l, cross = run(
        start_kernel,
        [(2 * RHS + TILE, TILE), row, (1, 2 * TILE), (3 * TILE, TILE)],
        src_l, w_l, p_l, q_l, t_l, p_m, q_m, p_u, q_u, p_r, piv_r,
    )
    for axis, mask in (("grid", 1), ("grid", 2), ("leaf", 1), ("leaf", 2), ("leaf", 4), ("leaf", 8)):
        cross = cross + swap(cross, axis, mask)
    k_m = cross[0:TILE]
    cross = cross[TILE:]
    cross = cross + swap(cross, "leaf", 16)
    k_u = cross[0:TILE]
    k_r = cross[TILE:]
    k_r = k_r + swap(k_r, "leaf", 32)

    out, z_l, zp_l, k_l = run(
        leaf_up_kernel,
        [(64, LANES), row, row, (TILE, TILE)],
        *four(first, "grid", 1), y_l, p_l, piv_l, c_l, ranks_l, t_l, slot_l,
    )
    got_m = route(out, 64)

    part, y_m, upd_m = run(
        functools.partial(enter_kernel, SLOTS_LEAF, True), [pair, row, row],
        got_m, src_m, w_m, q_m,
    )
    red = share(add_four(four(part, "grid", 1)), 16)
    out, z_m, zp_m = run(
        functools.partial(up_kernel, 16, 16, 14, 128), [(128, LANES), row, row],
        red, y_m, upd_m, p_m, piv_m, c_m, ranks_m, t_m, k_m,
    )
    got_u = route(out, 128)

    part, y_u, upd_u = run(
        functools.partial(enter_kernel, 1, True), [pair, row, row],
        got_u, src_u, w_u, q_u,
    )
    red = share(add_four(four(part, "grid", 1)), 32)
    out, z_u, zp_u = run(
        functools.partial(up_kernel, 32, 32, 15, 256), [(256, LANES), row, row],
        red, y_u, upd_u, p_u, piv_u, c_u, ranks_u, t_u, k_u,
    )
    got_r = route(out, 256)

    part, y_r = run(enter_root_kernel, [pair, row], got_r, src_r, w_r, p_r, q_r, piv_r)
    part = add_four(four(part, "grid", 1))
    red = share(add_four(four(part, "leaf", 16)), 16)
    x_r, out = run(
        functools.partial(root_kernel, 16), [row, (256, LANES)],
        red, y_r, w_r, p_r, q_r, piv_r, ranks_r, k_r, got_r,
    )

    back = route(out, 256)
    part, xu = run(
        functools.partial(fetch_kernel, 15, 256), [pair, row], back, t_u, c_u, zp_u
    )
    red = share(add_four(four(part, "grid", 1)), 32)
    x_u, out = run(
        functools.partial(down_kernel, 32, 32, 1), [row, (128, LANES)],
        red, z_u, k_u, w_u, q_u, ranks_u, xu, got_u,
    )

    back = route(out, 128)
    part, xu = run(
        functools.partial(fetch_kernel, 14, 128), [pair, row], back, t_m, c_m, zp_m
    )
    red = share(add_four(four(part, "grid", 1)), 16)
    x_m, out = run(
        functools.partial(down_kernel, 16, 16, SLOTS_LEAF), [row, (64, LANES)],
        red, z_m, k_m, w_m, q_m, ranks_m, xu, got_m,
    )

    back = route(out, 64)
    part = run(fetch_leaf_kernel, [pair], back, t_l, slot_l, c_l, zp_l)
    x_l = run(
        leaf_kernel, [row], *four(part, "grid", 1), z_l, k_l, w_l, q_l, ranks_l
    )
    return (x_l, x_m, x_u, x_r)


def solution(mesh):
    both = ("leaf", "grid")
    wide = P(None, both)
    tall = P(both, None)
    flat = P(both)
    level = (wide, tall, tall, tall, flat, tall, P(), flat)
    in_specs = level * 3 + (wide, tall, tall, tall, flat, P())
    return jax.shard_map(
        shards, mesh=mesh, in_specs=in_specs, out_specs=(wide,) * 4, check_vma=False
    )
```

profile of v0, /device:TPU:2, one launch (start us, length us, event | category | flops | bytes accessed | tf_op | source)
XLA Modules:
  0.0 309.2 jit_solution(15681631330647272793)
XLA Ops:
  0.6 2.5 start_kernel.1
  3.1 2.2 collective-permute-start.6
  5.4 4.6 %collective-permute-done.6 = f32[384,128]{1,0:T(8,128)S(1)} collective-permute-done((f32[384,128]{1,0:T(8,128)}, f32[384,128]{1,0:T(8,128)S(1)}, u32[]{:S(2)}, u32[]{:S(2)}) %collective-permute-start.6) | collective-permute-done | bytes 196640 | tf_op jit(solution)/shard_map/ppermute | solution.py:266
  10.0 1.0 add.81
  10.9 2.2 collective-permute-start.7
  13.1 5.0 %collective-permute-done.7 = f32[384,128]{1,0:T(8,128)S(1)} collective-permute-done((f32[384,128]{1,0:T(8,128)S(1)}, f32[384,128]{1,0:T(8,128)S(1)}, u32[]{:S(2)}, u32[]{:S(2)}) %collective-permute-start.7) | collective-permute-done | bytes 196640 | tf_op jit(solution)/shard_map/ppermute | solution.py:266
  18.3 1.4 collective-permute-done.8
  19.8 2.1 collective-permute-start.9
  21.9 1.5 collective-permute-start.2
  23.4 1.1 collective-permute-start.1
  24.5 1.5 collective-permute-start
  26.7 2.9 collective-permute-done.1.s2
  30.2 2.8 leaf_up_kernel.1
  33.0 20.0 %all_to_all.106 = f32[64,1,128]{2,1,0:T(1,128)} all-to-all(f32[64,1,128]{2,1,0:T(1,128)} %bitcast.54), channel_id=1, replica_groups={{0,1,2,3,4,5,6,7,8,9,10,11,12,13,14,15,16,17,18,19,20,21,22,23,24,25,26..., dimensions={0} | all-to-all | bytes 65536 | tf_op jit(solution)/shard_map/all_to_all | solution.py:294
  53.0 2.3 enter_kernel.2
  56.0 2.8 collective-permute-start.4
  60.2 1.1 collective-permute-done.4
  61.3 1.3 collective-permute-done.3
  63.3 3.5 %all-to-all-start.1 = ((f32[16,16,128]{2,1,0:T(8,128)}), f32[16,16,128]{2,1,0:T(8,128)S(1)}, u32[]{:S(2)}, u32[]{:S(2)}) async-start(f32[16,16,128]{2,1,0:T(8,128)} %broadcast_in_dim.15), calls=%async_computation.1 | async-start | bytes 262144 | tf_op jit(solution)/shard_map/all_to_all | solution.py:284
  66.9 3.1 %collective-permute-done.10 = f32[384,128]{1,0:T(8,128)S(1)} collective-permute-done((f32[384,128]{1,0:T(8,128)S(1)}, f32[384,128]{1,0:T(8,128)S(1)}, u32[]{:S(2)}, u32[]{:S(2)}) %collective-permute-start.10) | collective-permute-done | bytes 196640 | tf_op jit(solution)/shard_map/ppermute | solution.py:266
  70.0 2.8 collective-permute-start.11
  73.4 11.6 %collective-permute-done.11 = f32[384,128]{1,0:T(8,128)S(1)} collective-permute-done((f32[384,128]{1,0:T(8,128)S(1)}, f32[384,128]{1,0:T(8,128)S(1)}, u32[]{:S(2)}, u32[]{:S(2)}) %collective-permute-start.11) | collective-permute-done | bytes 196640 | tf_op jit(solution)/shard_map/ppermute | solution.py:266
  86.3 2.7 up_kernel.2
  89.0 18.2 %all_to_all.107 = f32[128,1,128]{2,1,0:T(1,128)} all-to-all(f32[128,1,128]{2,1,0:T(1,128)} %bitcast.53), channel_id=1, replica_groups={{0,1,2,3,4,5,6,7,8,9,10,11,12,13,14,15,16,17,18,19,20,21,22,23,24,25,26..., dimensions={0} | all-to-all | bytes 131072 | tf_op jit(solution)/shard_map/all_to_all | solution.py:294
  107.3 2.3 enter_kernel.3
  110.3 3.2 %collective-permute-start.13 = (f32[16,128]{1,0:T(8,128)}, f32[16,128]{1,0:T(8,128)S(1)}, u32[]{:S(2)}, u32[]{:S(2)}) collective-permute-start(f32[16,128]{1,0:T(8,128)} %get-tuple-element.45), channel_id=1, source_target_pairs={{0,2},{1,3},{2,0},{3,1},{4,6},{5,7},{6,4},{7,5},{8,10},{9,11},{10,... | collective-permute-start | bytes 24584 | tf_op jit(solution)/shard_map/ppermute | solution.py:266
  114.4 1.2 collective-permute-done.13
  115.6 1.7 collective-permute-done.12
  118.1 3.9 %all-to-all-start.3 = ((f32[32,16,128]{2,1,0:T(8,128)}), f32[32,16,128]{2,1,0:T(8,128)S(1)}, u32[]{:S(2)}, u32[]{:S(2)}) async-start(f32[32,16,128]{2,1,0:T(8,128)} %broadcast_in_dim.16), calls=%async_computation.3 | async-start | bytes 524288 | tf_op jit(solution)/shard_map/all_to_all | solution.py:284
  122.0 3.0 collective-permute-start.22
  125.0 3.0 collective-permute-done.22
  128.7 6.4 %all-to-all-done.3 = f32[32,16,128]{2,1,0:T(8,128)S(1)} async-done(((f32[32,16,128]{2,1,0:T(8,128)}), f32[32,16,128]{2,1,0:T(8,128)S(1)}, u32[]{:S(2)}, u32[]{:S(2)}) %all-to-all-start.3) | async-done | bytes 262176 | tf_op jit(solution)/shard_map/all_to_all | solution.py:284
  135.8 2.8 up_kernel.3
  138.6 19.9 %all_to_all.108 = f32[256,1,128]{2,1,0:T(1,128)} all-to-all(f32[256,1,128]{2,1,0:T(1,128)} %bitcast.49), channel_id=1, replica_groups=mesh['leaf'=64,'grid'=4] {'leaf','grid'}, dimensions={0} | all-to-all | bytes 262144 | tf_op jit(solution)/shard_map/all_to_all | solution.py:294
  158.5 2.4 enter_root_kernel.1
  160.9 3.6 %collective-permute-start.17 = (f32[16,128]{1,0:T(8,128)}, f32[16,128]{1,0:T(8,128)S(1)}, u32[]{:S(2)}, u32[]{:S(2)}) collective-permute-start(f32[16,128]{1,0:T(8,128)} %get-tuple-element.49), channel_id=1, source_target_pairs={{0,2},{1,3},{2,0},{3,1},{4,6},{5,7},{6,4},{7,5},{8,10},{9,11},{10,... | collective-permute-start | bytes 24584 | tf_op jit(solution)/shard_map/ppermute | solution.py:266
  165.0 1.5 collective-permute-done.17
  166.5 2.0 collective-permute-done.16
  169.2 0.8 collective-permute-start.21
  169.9 1.6 collective-permute-start.20
  171.5 1.7 collective-permute-start.19
  174.0 1.1 collective-permute-done.20
  175.2 11.9 %all_to_all.109 = f32[16,16,128]{2,1,0:T(8,128)} all-to-all(f32[16,16,128]{2,1,0:T(8,128)S(1)} %broadcast_in_dim.17), channel_id=1, replica_groups={{0,4,8,12,16,20,24,28,32,36,40,44,48,52,56,60},{64,68,72,76,80,84,88,92..., dimensions={0} | all-to-all | bytes 262144 | tf_op jit(solution)/shard_map/all_to_all | solution.py:284
  187.1 2.9 root_kernel.1
  190.0 20.3 %all_to_all.110 = f32[256,1,128]{2,1,0:T(1,128)} all-to-all(f32[256,1,128]{2,1,0:T(1,128)} %bitcast.50), channel_id=1, replica_groups=mesh['leaf'=64,'grid'=4] {'leaf','grid'}, dimensions={0} | all-to-all | bytes 262144 | tf_op jit(solution)/shard_map/all_to_all | solution.py:294
  210.3 2.0 fetch_kernel.2
  212.4 3.6 %collective-permute-start.24 = (f32[16,128]{1,0:T(8,128)}, f32[16,128]{1,0:T(8,128)S(1)}, u32[]{:S(2)}, u32[]{:S(2)}) collective-permute-start(f32[16,128]{1,0:T(8,128)} %get-tuple-element.53), channel_id=1, source_target_pairs={{0,2},{1,3},{2,0},{3,1},{4,6},{5,7},{6,4},{7,5},{8,10},{9,11},{10,... | collective-permute-start | bytes 24584 | tf_op jit(solution)/shard_map/ppermute | solution.py:266
  216.4 1.4 collective-permute-done.24
  217.9 2.0 collective-permute-done.23
  220.6 16.8 %all_to_all.111 = f32[32,16,128]{2,1,0:T(8,128)} all-to-all(f32[32,16,128]{2,1,0:T(8,128)S(1)} %broadcast_in_dim.18), channel_id=1, replica_groups={{0,4,8,12,16,20,24,28,32,36,40,44,48,52,56,60,64,68,72,76,80,84,88,92,9..., dimensions={0} | all-to-all | bytes 524288 | tf_op jit(solution)/shard_map/all_to_all | solution.py:284
  237.4 3.0 down_kernel.2
  240.4 16.1 %all_to_all.112 = f32[128,1,128]{2,1,0:T(1,128)} all-to-all(f32[128,1,128]{2,1,0:T(1,128)} %bitcast.52), channel_id=1, replica_groups={{0,1,2,3,4,5,6,7,8,9,10,11,12,13,14,15,16,17,18,19,20,21,22,23,24,25,26..., dimensions={0} | all-to-all | bytes 131072 | tf_op jit(solution)/shard_map/all_to_all | solution.py:294
  256.5 2.0 fetch_kernel.3
  259.2 3.3 %collective-permute-start.27 = (f32[16,128]{1,0:T(8,128)}, f32[16,128]{1,0:T(8,128)S(1)}, u32[]{:S(2)}, u32[]{:S(2)}) collective-permute-start(f32[16,128]{1,0:T(8,128)} %get-tuple-element.58), channel_id=1, source_target_pairs={{0,2},{1,3},{2,0},{3,1},{4,6},{5,7},{6,4},{7,5},{8,10},{9,11},{10,... | collective-permute-start | bytes 24584 | tf_op jit(solution)/shard_map/ppermute | solution.py:266
  262.6 2.0 collective-permute-done.27
  264.6 1.8 collective-permute-done.26
  267.1 11.9 %all_to_all.113 = f32[16,16,128]{2,1,0:T(8,128)} all-to-all(f32[16,16,128]{2,1,0:T(8,128)S(1)} %broadcast_in_dim.19), channel_id=1, replica_groups={{0,4,8,12,16,20,24,28,32,36,40,44,48,52,56,60},{64,68,72,76,80,84,88,92..., dimensions={0} | all-to-all | bytes 262144 | tf_op jit(solution)/shard_map/all_to_all | solution.py:284
  279.0 3.1 %down_kernel.3 = (f32[8,128]{1,0:T(8,128)}, f32[64,128]{1,0:T(8,128)}) custom-call(f32[256,128]{1,0:T(8,128)} %bitcast.42, f32[8,128]{1,0:T(8,128)} %get-tuple-element.59.z, f32[128,128]{1,0:T(8,128)} %slice.16.k1, f32[128,128]{1,0:T(8,128)} %w.14, f32[128,256]{1,0:T(8,128)} %q.14, s32[4,2]{1,0:T(4,128)} %copy.40.ranks, f32[8,128]{1,0:T(8,128)} %get-tuple-element.60.xu, ...), custom_call_target="tpu_custom_call" | custom-call | tf_op jit(solution)/shard_map/down_kernel/pallas_call | solution.py:257
  282.1 14.4 %all_to_all.114 = f32[64,1,128]{2,1,0:T(1,128)} all-to-all(f32[64,1,128]{2,1,0:T(1,128)} %bitcast.55), channel_id=1, replica_groups={{0,1,2,3,4,5,6,7,8,9,10,11,12,13,14,15,16,17,18,19,20,21,22,23,24,25,26..., dimensions={0} | all-to-all | bytes 65536 | tf_op jit(solution)/shard_map/all_to_all | solution.py:294
  296.5 1.9 fetch_leaf_kernel.1.s0
  299.1 3.1 collective-permute-start.30
  302.6 1.9 collective-permute-done.30.s2
  304.5 1.5 collective-permute-done.29.s1
  306.6 2.7 leaf_kernel.1
  (77 shorter events, 16.3 us)
Async XLA Ops:
  3.1 6.9 %collective-permute-start.6 = (f32[384,128]{1,0:T(8,128)}, f32[384,128]{1,0:T(8,128)S(1)}, u32[]{:S(2)}, u32[]{:S(2)}) collective-permute-start(f32[384,128]{1,0:T(8,128)} %get-tuple-element.43), channel_id=1, source_target_pairs={{0,1},{1,0},{2,3},{3,2},{4,5},{5,4},{6,7},{7,6},{8,9},{9,8},{10,11... | collective-permute-start | bytes 589832 | tf_op jit(solution)/shard_map/ppermute | solution.py:266
  10.9 7.3 %collective-permute-start.7 = (f32[384,128]{1,0:T(8,128)S(1)}, f32[384,128]{1,0:T(8,128)S(1)}, u32[]{:S(2)}, u32[]{:S(2)}) collective-permute-start(f32[384,128]{1,0:T(8,128)S(1)} %add.81), channel_id=1, source_target_pairs={{0,2},{1,3},{2,0},{3,1},{4,6},{5,7},{6,4},{7,5},{8,10},{9,11},{10,... | collective-permute-start | bytes 589832 | tf_op jit(solution)/shard_map/ppermute | solution.py:266
  18.2 3.7 %copy-start.2 = (f32[144,128]{1,0:T(8,128)S(1)}, f32[144,128]{1,0:T(8,128)}, u32[]{:S(2)}) copy-start(f32[144,128]{1,0:T(8,128)} %get-tuple-element.36.s0) | copy-start | bytes 221188
  18.2 1.5 collective-permute-start.8
  19.8 6.2 %copy-start.11 = (s32[64,2]{0,1:T(2,128)S(1)}, s32[64,2]{0,1:T(2,128)}, u32[]{:S(2)}) copy-start(s32[64,2]{0,1:T(2,128)} %param.36) | copy-start | bytes 1540
  19.8 39.6 %collective-permute-start.9 = (f32[384,128]{1,0:T(8,128)S(1)}, f32[384,128]{1,0:T(8,128)S(1)}, u32[]{:S(2)}, u32[]{:S(2)}) collective-permute-start(f32[384,128]{1,0:T(8,128)S(1)} %add.83), channel_id=1, source_target_pairs={{0,8},{4,12},{8,0},{12,4},{16,24},{20,28},{24,16},{28,20},{32,40},... | collective-permute-start | bytes 589832 | tf_op jit(solution)/shard_map/ppermute | solution.py:266
  21.9 4.8 %collective-permute-start.2 = (f32[144,128]{1,0:T(8,128)S(1)}, f32[144,128]{1,0:T(8,128)S(1)}, u32[]{:S(2)}, u32[]{:S(2)}) collective-permute-start(f32[144,128]{1,0:T(8,128)S(1)} %copy-done.2), channel_id=1, source_target_pairs={{0,3},{1,2},{2,1},{3,0},{4,7},{5,6},{6,5},{7,4},{8,11},{9,10},{10,... | collective-permute-start | bytes 221192 | tf_op jit(solution)/shard_map/ppermute | solution.py:266
  23.4 6.2 %collective-permute-start.1 = (f32[144,128]{1,0:T(8,128)S(1)}, f32[144,128]{1,0:T(8,128)S(1)}, u32[]{:S(2)}, u32[]{:S(2)}) collective-permute-start(f32[144,128]{1,0:T(8,128)S(1)} %copy-done.2), channel_id=1, source_target_pairs={{0,2},{1,3},{2,0},{3,1},{4,6},{5,7},{6,4},{7,5},{8,10},{9,11},{10,... | collective-permute-start | bytes 221192 | tf_op jit(solution)/shard_map/ppermute | solution.py:266
  24.5 5.1 %collective-permute-start = (f32[144,128]{1,0:T(8,128)S(1)}, f32[144,128]{1,0:T(8,128)S(1)}, u32[]{:S(2)}, u32[]{:S(2)}) collective-permute-start(f32[144,128]{1,0:T(8,128)S(1)} %copy-done.2), channel_id=1, source_target_pairs={{0,1},{1,0},{2,3},{3,2},{4,5},{5,4},{6,7},{7,6},{8,9},{9,8},{10,11... | collective-permute-start | bytes 221192 | tf_op jit(solution)/shard_map/ppermute | solution.py:266
  26.7 2.9 copy-start.3
  29.6 0.6 copy-start.4
  29.6 0.6 copy-start.5
  55.3 7.3 %copy-start.6 = (f32[16,128]{1,0:T(8,128)S(1)}, f32[16,128]{1,0:T(8,128)}, u32[]{:S(2)}) copy-start(f32[16,128]{1,0:T(8,128)} %get-tuple-element.40) | copy-start | bytes 24580
  55.3 4.9 %collective-permute-start.5 = (f32[16,128]{1,0:T(8,128)}, f32[16,128]{1,0:T(8,128)S(1)}, u32[]{:S(2)}, u32[]{:S(2)}) collective-permute-start(f32[16,128]{1,0:T(8,128)} %get-tuple-element.40), channel_id=1, source_target_pairs={{0,3},{1,2},{2,1},{3,0},{4,7},{5,6},{6,5},{7,4},{8,11},{9,10},{10,... | collective-permute-start | bytes 24584 | tf_op jit(solution)/shard_map/ppermute | solution.py:266
  56.0 5.4 %collective-permute-start.4 = (f32[16,128]{1,0:T(8,128)}, f32[16,128]{1,0:T(8,128)S(1)}, u32[]{:S(2)}, u32[]{:S(2)}) collective-permute-start(f32[16,128]{1,0:T(8,128)} %get-tuple-element.40), channel_id=1, source_target_pairs={{0,2},{1,3},{2,0},{3,1},{4,6},{5,7},{6,4},{7,5},{8,10},{9,11},{10,... | collective-permute-start | bytes 24584 | tf_op jit(solution)/shard_map/ppermute | solution.py:266
  58.8 3.9 %collective-permute-start.3 = (f32[16,128]{1,0:T(8,128)}, f32[16,128]{1,0:T(8,128)S(1)}, u32[]{:S(2)}, u32[]{:S(2)}) collective-permute-start(f32[16,128]{1,0:T(8,128)} %get-tuple-element.40), channel_id=1, source_target_pairs={{0,1},{1,0},{2,3},{3,2},{4,5},{5,4},{6,7},{7,6},{8,9},{9,8},{10,11... | collective-permute-start | bytes 24584 | tf_op jit(solution)/shard_map/ppermute | solution.py:266
  59.5 10.5 %collective-permute-start.10 = (f32[384,128]{1,0:T(8,128)S(1)}, f32[384,128]{1,0:T(8,128)S(1)}, u32[]{:S(2)}, u32[]{:S(2)}) collective-permute-start(f32[384,128]{1,0:T(8,128)S(1)} %add.84), channel_id=1, source_target_pairs={{0,16},{4,20},{8,24},{12,28},{16,0},{20,4},{24,8},{28,12},{32,48},... | collective-permute-start | bytes 589832 | tf_op jit(solution)/shard_map/ppermute | solution.py:266
  63.3 22.3 %all-to-all-start.1 = ((f32[16,16,128]{2,1,0:T(8,128)}), f32[16,16,128]{2,1,0:T(8,128)S(1)}, u32[]{:S(2)}, u32[]{:S(2)}) async-start(f32[16,16,128]{2,1,0:T(8,128)} %broadcast_in_dim.15), calls=%async_computation.1 | async-start | bytes 262144 | tf_op jit(solution)/shard_map/all_to_all | solution.py:284
  66.8 5.9 %copy-start.12 = (s32[4,2]{0,1:T(2,128)S(1)}, s32[4,2]{0,1:T(2,128)}, u32[]{:S(2)}) copy-start(s32[4,2]{0,1:T(2,128)} %param.44) | copy-start | bytes 100
  70.0 15.0 %collective-permute-start.11 = (f32[384,128]{1,0:T(8,128)S(1)}, f32[384,128]{1,0:T(8,128)S(1)}, u32[]{:S(2)}, u32[]{:S(2)}) collective-permute-start(f32[384,128]{1,0:T(8,128)S(1)} %add.85), channel_id=1, source_target_pairs={{0,32},{4,36},{8,40},{12,44},{16,48},{20,52},{24,56},{28,60},{32,0... | collective-permute-start | bytes 589832 | tf_op jit(solution)/shard_map/ppermute | solution.py:266
  85.7 0.7 copy-start.1
  109.5 7.8 %copy-start.7 = (f32[16,128]{1,0:T(8,128)S(1)}, f32[16,128]{1,0:T(8,128)}, u32[]{:S(2)}) copy-start(f32[16,128]{1,0:T(8,128)} %get-tuple-element.45) | copy-start | bytes 24580
  109.5 4.8 %collective-permute-start.14 = (f32[16,128]{1,0:T(8,128)}, f32[16,128]{1,0:T(8,128)S(1)}, u32[]{:S(2)}, u32[]{:S(2)}) collective-permute-start(f32[16,128]{1,0:T(8,128)} %get-tuple-element.45), channel_id=1, source_target_pairs={{0,3},{1,2},{2,1},{3,0},{4,7},{5,6},{6,5},{7,4},{8,11},{9,10},{10,... | collective-permute-start | bytes 24584 | tf_op jit(solution)/shard_map/ppermute | solution.py:266
  110.3 5.4 %collective-permute-start.13 = (f32[16,128]{1,0:T(8,128)}, f32[16,128]{1,0:T(8,128)S(1)}, u32[]{:S(2)}, u32[]{:S(2)}) collective-permute-start(f32[16,128]{1,0:T(8,128)} %get-tuple-element.45), channel_id=1, source_target_pairs={{0,2},{1,3},{2,0},{3,1},{4,6},{5,7},{6,4},{7,5},{8,10},{9,11},{10,... | collective-permute-start | bytes 24584 | tf_op jit(solution)/shard_map/ppermute | solution.py:266
  113.5 3.9 %collective-permute-start.12 = (f32[16,128]{1,0:T(8,128)}, f32[16,128]{1,0:T(8,128)S(1)}, u32[]{:S(2)}, u32[]{:S(2)}) collective-permute-start(f32[16,128]{1,0:T(8,128)} %get-tuple-element.45), channel_id=1, source_target_pairs={{0,1},{1,0},{2,3},{3,2},{4,5},{5,4},{6,7},{7,6},{8,9},{9,8},{10,11... | collective-permute-start | bytes 24584 | tf_op jit(solution)/shard_map/ppermute | solution.py:266
  113.7 8.3 %collective-permute-start.15 = (f32[256,128]{1,0:T(8,128)S(1)}, f32[256,128]{1,0:T(8,128)S(1)}, u32[]{:S(2)}, u32[]{:S(2)}) collective-permute-start(f32[256,128]{1,0:T(8,128)S(1)} %slice.17), channel_id=1, source_target_pairs={{0,64},{4,68},{8,72},{12,76},{16,80},{20,84},{24,88},{28,92},{32,9... | collective-permute-start | bytes 393224 | tf_op jit(solution)/shard_map/ppermute | solution.py:266
  118.1 17.0 %all-to-all-start.3 = ((f32[32,16,128]{2,1,0:T(8,128)}), f32[32,16,128]{2,1,0:T(8,128)S(1)}, u32[]{:S(2)}, u32[]{:S(2)}) async-start(f32[32,16,128]{2,1,0:T(8,128)} %broadcast_in_dim.16), calls=%async_computation.3 | async-start | bytes 524288 | tf_op jit(solution)/shard_map/all_to_all | solution.py:284
  122.0 6.0 %collective-permute-start.22 = (f32[128,128]{1,0:T(8,128)S(1)}, f32[128,128]{1,0:T(8,128)S(1)}, u32[]{:S(2)}, u32[]{:S(2)}) collective-permute-start(f32[128,128]{1,0:T(8,128)S(1)} %slice.19), channel_id=1, source_target_pairs={{0,128},{4,132},{8,136},{12,140},{16,144},{20,148},{24,152},{28,15... | collective-permute-start | bytes 196616 | tf_op jit(solution)/shard_map/ppermute | solution.py:266
  135.1 0.7 copy-start
  160.9 4.1 %collective-permute-start.18 = (f32[16,128]{1,0:T(8,128)}, f32[16,128]{1,0:T(8,128)S(1)}, u32[]{:S(2)}, u32[]{:S(2)}) collective-permute-start(f32[16,128]{1,0:T(8,128)} %get-tuple-element.49), channel_id=1, source_target_pairs={{0,3},{1,2},{2,1},{3,0},{4,7},{5,6},{6,5},{7,4},{8,11},{9,10},{10,... | collective-permute-start | bytes 24584 | tf_op jit(solution)/shard_map/ppermute | solution.py:266
  160.9 5.5 %collective-permute-start.17 = (f32[16,128]{1,0:T(8,128)}, f32[16,128]{1,0:T(8,128)S(1)}, u32[]{:S(2)}, u32[]{:S(2)}) collective-permute-start(f32[16,128]{1,0:T(8,128)} %get-tuple-element.49), channel_id=1, source_target_pairs={{0,2},{1,3},{2,0},{3,1},{4,6},{5,7},{6,4},{7,5},{8,10},{9,11},{10,... | collective-permute-start | bytes 24584 | tf_op jit(solution)/shard_map/ppermute | solution.py:266
  164.6 3.9 %collective-permute-start.16 = (f32[16,128]{1,0:T(8,128)}, f32[16,128]{1,0:T(8,128)S(1)}, u32[]{:S(2)}, u32[]{:S(2)}) collective-permute-start(f32[16,128]{1,0:T(8,128)} %get-tuple-element.49), channel_id=1, source_target_pairs={{0,1},{1,0},{2,3},{3,2},{4,5},{5,4},{6,7},{7,6},{8,9},{9,8},{10,11... | collective-permute-start | bytes 24584 | tf_op jit(solution)/shard_map/ppermute | solution.py:266
  169.2 4.9 %collective-permute-start.21 = (f32[16,128]{1,0:T(8,128)S(1)}, f32[16,128]{1,0:T(8,128)S(1)}, u32[]{:S(2)}, u32[]{:S(2)}) collective-permute-start(f32[16,128]{1,0:T(8,128)S(1)} %add_add_fusion.3), channel_id=1, source_target_pairs={{0,192},{4,196},{8,200},{12,204},{16,208},{20,212},{24,216},{28,22... | collective-permute-start | bytes 24584 | tf_op jit(solution)/shard_map/ppermute | solution.py:266
  169.9 5.2 %collective-permute-start.20 = (f32[16,128]{1,0:T(8,128)S(1)}, f32[16,128]{1,0:T(8,128)S(1)}, u32[]{:S(2)}, u32[]{:S(2)}) collective-permute-start(f32[16,128]{1,0:T(8,128)S(1)} %add_add_fusion.3), channel_id=1, source_target_pairs={{0,128},{4,132},{8,136},{12,140},{16,144},{20,148},{24,152},{28,15... | collective-permute-start | bytes 24584 | tf_op jit(solution)/shard_map/ppermute | solution.py:266
  171.5 3.7 %collective-permute-start.19 = (f32[16,128]{1,0:T(8,128)S(1)}, f32[16,128]{1,0:T(8,128)S(1)}, u32[]{:S(2)}, u32[]{:S(2)}) collective-permute-start(f32[16,128]{1,0:T(8,128)S(1)} %add_add_fusion.3), channel_id=1, source_target_pairs={{0,64},{4,68},{8,72},{12,76},{16,80},{20,84},{24,88},{28,92},{32,9... | collective-permute-start | bytes 24584 | tf_op jit(solution)/shard_map/ppermute | solution.py:266
  212.3 4.1 %collective-permute-start.25 = (f32[16,128]{1,0:T(8,128)}, f32[16,128]{1,0:T(8,128)S(1)}, u32[]{:S(2)}, u32[]{:S(2)}) collective-permute-start(f32[16,128]{1,0:T(8,128)} %get-tuple-element.53), channel_id=1, source_target_pairs={{0,3},{1,2},{2,1},{3,0},{4,7},{5,6},{6,5},{7,4},{8,11},{9,10},{10,... | collective-permute-start | bytes 24584 | tf_op jit(solution)/shard_map/ppermute | solution.py:266
  212.4 5.5 %collective-permute-start.24 = (f32[16,128]{1,0:T(8,128)}, f32[16,128]{1,0:T(8,128)S(1)}, u32[]{:S(2)}, u32[]{:S(2)}) collective-permute-start(f32[16,128]{1,0:T(8,128)} %get-tuple-element.53), channel_id=1, source_target_pairs={{0,2},{1,3},{2,0},{3,1},{4,6},{5,7},{6,4},{7,5},{8,10},{9,11},{10,... | collective-permute-start | bytes 24584 | tf_op jit(solution)/shard_map/ppermute | solution.py:266
  216.0 3.9 %collective-permute-start.23 = (f32[16,128]{1,0:T(8,128)}, f32[16,128]{1,0:T(8,128)S(1)}, u32[]{:S(2)}, u32[]{:S(2)}) collective-permute-start(f32[16,128]{1,0:T(8,128)} %get-tuple-element.53), channel_id=1, source_target_pairs={{0,1},{1,0},{2,3},{3,2},{4,5},{5,4},{6,7},{7,6},{8,9},{9,8},{10,11... | collective-permute-start | bytes 24584 | tf_op jit(solution)/shard_map/ppermute | solution.py:266
  258.5 4.1 %collective-permute-start.28 = (f32[16,128]{1,0:T(8,128)}, f32[16,128]{1,0:T(8,128)S(1)}, u32[]{:S(2)}, u32[]{:S(2)}) collective-permute-start(f32[16,128]{1,0:T(8,128)} %get-tuple-element.58), channel_id=1, source_target_pairs={{0,3},{1,2},{2,1},{3,0},{4,7},{5,6},{6,5},{7,4},{8,11},{9,10},{10,... | collective-permute-start | bytes 24584 | tf_op jit(solution)/shard_map/ppermute | solution.py:266
  259.2 5.4 %collective-permute-start.27 = (f32[16,128]{1,0:T(8,128)}, f32[16,128]{1,0:T(8,128)S(1)}, u32[]{:S(2)}, u32[]{:S(2)}) collective-permute-start(f32[16,128]{1,0:T(8,128)} %get-tuple-element.58), channel_id=1, source_target_pairs={{0,2},{1,3},{2,0},{3,1},{4,6},{5,7},{6,4},{7,5},{8,10},{9,11},{10,... | collective-permute-start | bytes 24584 | tf_op jit(solution)/shard_map/ppermute | solution.py:266
  262.5 3.9 %collective-permute-start.26 = (f32[16,128]{1,0:T(8,128)}, f32[16,128]{1,0:T(8,128)S(1)}, u32[]{:S(2)}, u32[]{:S(2)}) collective-permute-start(f32[16,128]{1,0:T(8,128)} %get-tuple-element.58), channel_id=1, source_target_pairs={{0,1},{1,0},{2,3},{3,2},{4,5},{5,4},{6,7},{7,6},{8,9},{9,8},{10,11... | collective-permute-start | bytes 24584 | tf_op jit(solution)/shard_map/ppermute | solution.py:266
  298.5 4.1 %collective-permute-start.31 = (f32[16,128]{1,0:T(8,128)}, f32[16,128]{1,0:T(8,128)S(1)}, u32[]{:S(2)}, u32[]{:S(2)}) collective-permute-start(f32[16,128]{1,0:T(8,128)} %fetch_leaf_kernel.1.s0), channel_id=1, source_target_pairs={{0,3},{1,2},{2,1},{3,0},{4,7},{5,6},{6,5},{7,4},{8,11},{9,10},{10,... | collective-permute-start | bytes 24584 | tf_op jit(solution)/shard_map/ppermute | solution.py:266
  299.1 5.4 %collective-permute-start.30 = (f32[16,128]{1,0:T(8,128)}, f32[16,128]{1,0:T(8,128)S(1)}, u32[]{:S(2)}, u32[]{:S(2)}) collective-permute-start(f32[16,128]{1,0:T(8,128)} %fetch_leaf_kernel.1.s0), channel_id=1, source_target_pairs={{0,2},{1,3},{2,0},{3,1},{4,6},{5,7},{6,4},{7,5},{8,10},{9,11},{10,... | collective-permute-start | bytes 24584 | tf_op jit(solution)/shard_map/ppermute | solution.py:266
  302.1 3.9 %collective-permute-start.29 = (f32[16,128]{1,0:T(8,128)}, f32[16,128]{1,0:T(8,128)S(1)}, u32[]{:S(2)}, u32[]{:S(2)}) collective-permute-start(f32[16,128]{1,0:T(8,128)} %fetch_leaf_kernel.1.s0), channel_id=1, source_target_pairs={{0,1},{1,0},{2,3},{3,2},{4,5},{5,4},{6,7},{7,6},{8,9},{9,8},{10,11... | collective-permute-start | bytes 24584 | tf_op jit(solution)/shard_map/ppermute | solution.py:266
  302.6 3.4 %copy-start.8 = (f32[16,128]{1,0:T(8,128)}, f32[16,128]{1,0:T(8,128)S(1)}, u32[]{:S(2)}) copy-start(f32[16,128]{1,0:T(8,128)S(1)} %collective-permute-done.31.s3) | copy-start | bytes 24580
  304.4 1.6 copy-start.9
  306.0 0.6 copy-start.10
where the time goes:
time: 310 us; the launch traced here: 309 us
  blocking collectives  150 us (48%)
  waiting for transfers between devices  59.6 us (19%)
  starting transfers between devices  54 us (17%)
  Pallas kernels  35.3 us (11%)
  local copies, waits for them, and re-layouts  6.06 us (2%)
  other arithmetic  3.86 us (1%)
    all_to_all x6, blocking collectives, route(): lax.all_to_all(messages, ('leaf', 'grid'), split_axis=0, concat_axis=0, t...  109 us
    ppermute x32, waiting for transfers between devices, swap(): return lax.ppermute(value, axis, pairs)  53.1 us
    ppermute x32, starting transfers between devices, swap(): return lax.ppermute(value, axis, pairs)  46.6 us
    all_to_all x3, blocking collectives, share(): lax.all_to_all(copies, 'leaf', split_axis=0, concat_axis=0, tiled=True, a...  40.7 us
    pallas_call x14, Pallas kernels, run(): pl.pallas_call(kernel, out_shape=outs[0] if single else outs, name=name)  35.3 us
    all_to_all x2, starting transfers between devices, share(): lax.all_to_all(copies, 'leaf', split_axis=0, concat_axis=0, tiled=True, a...  7.38 us
    all_to_all x2, waiting for transfers between devices, share(): lax.all_to_all(copies, 'leaf', split_axis=0, concat_axis=0, tiled=True, a...  6.44 us
  transfers between devices with their start and end apart: 34, of which 23 were waited for; matrix products, arithmetic and copies ran while one was open for 1% of the time, Pallas kernels for 2%

commit v1 on v0

v1 whole, which is shorter than its diff:
```python
import functools

import jax
import jax.numpy as jnp
from jax import lax
from jax.experimental import pallas as pl
from jax.experimental.pallas import tpu as pltpu
from jax.sharding import PartitionSpec as P

RHS = 8
LANES = 128
TILE = 128
HOLD = 8
SLOT = 16
SLOTS_LEAF = 4

SRC, WAT, QAT, VAT, MISC, CAT, PAT, END = 0, 8, 136, 264, 392, 400, 528, 656
RMISC, RPAT, REND = 264, 272, 400

F32 = jnp.float32
BF16 = jnp.bfloat16


def iota(shape, dim):
    return lax.broadcasted_iota(jnp.int32, shape, dim)


def raw(a, b, ca, cb):
    return lax.dot_general(a, b, (((ca,), (cb,)), ((), ())), preferred_element_type=F32)


def halves(a):
    high = a.astype(BF16)
    low = (a - high.astype(F32)).astype(BF16)
    return high, low


def stacked(a):
    high = a.astype(BF16).astype(F32)
    return jnp.concatenate([high, a - high], axis=0).astype(BF16)


def fold(total):
    rows = total.shape[0] // 2
    return total[0:rows] + total[rows:]


def dot(a, b, ca, cb):
    high, low = halves(b)
    both = stacked(a)
    return fold(raw(both, high, ca, cb) + raw(both, low, ca, cb))


def mm(a, b):
    return dot(a, b, 1, 0)


def mmt(a, b):
    return dot(a, b, 1, 1)


def cross_product(a, b):
    return lax.dot_general(
        a,
        b,
        (((0,), (0,)), ((), ())),
        precision=lax.Precision.HIGHEST,
        preferred_element_type=F32,
    )


def cross(a, b):
    a_high, a_low = halves(a)
    b_high, b_low = halves(b)
    return (raw(a_low, b_high, 0, 0) + raw(a_high, b_low, 0, 0)) + raw(a_high, b_high, 0, 0)


def masks(ranks_ref, groups):
    front = lax.axis_index("leaf") // groups
    pair = ranks_ref[pl.ds(front, 1), :]
    lane = iota((1, TILE), 1)
    mh = (lane < pair[:, 0:1]).astype(F32)
    mc = (lane < pair[:, 1:2]).astype(F32)
    return mh, mc


def split_target(targets, shift):
    piece = lax.shift_right_logical(targets, shift)
    within = jnp.bitwise_and(targets, (1 << shift) - 1)
    dest = lax.shift_right_logical(within, 7)
    label = piece * TILE + jnp.bitwise_and(within, TILE - 1)
    return dest, label.astype(F32)


def row_onehot(at, count):
    n = at.shape[1]
    if at.dtype == jnp.int32:
        rows = iota((count, n), 0)
    else:
        rows = iota((count, n), 0).astype(F32)
    return (rows == jnp.broadcast_to(at, (count, n))).astype(F32)


def leaf_slots(onehot):
    n = onehot.shape[1]
    upper = (iota((n, n), 0) <= iota((n, n), 1)).astype(BF16)
    order = raw(onehot.astype(BF16), upper, 1, 0)
    return jnp.sum(order * onehot, axis=0, keepdims=True) - 1.0


def label_rows(label):
    n = label.shape[1]
    return jnp.where(iota((SLOT - RHS, n), 0) == 0, jnp.broadcast_to(label, (SLOT - RHS, n)), 0.0)


def fill(rows, n):
    used = sum(r.shape[0] for r in rows)
    if used < LANES:
        rows = rows + [jnp.zeros((LANES - used, n), F32)]
    return jnp.concatenate(rows, axis=0)


def block_mask(n):
    own = jnp.bitwise_and(iota((HOLD * RHS, n), 1), HOLD - 1)
    return (lax.shift_right_logical(iota((HOLD * RHS, n), 0), 3) == own).astype(F32)


def received(turned, slots, cols):
    n = turned.shape[1]
    mask = block_mask(n)
    total = None
    for k in range(slots):
        values = turned[SLOT * k : SLOT * k + RHS, :]
        label = turned[SLOT * k + RHS : SLOT * k + RHS + 1, :]
        spread = jnp.concatenate([values] * HOLD, axis=0) * mask
        part = raw(stacked(spread), row_onehot(label, cols).astype(BF16), 1, 1)
        total = part if total is None else total + part
    return fold(total)


def replies(turned, slots, rows):
    n = turned.shape[1]
    mask = block_mask(n)
    both = stacked(rows)
    out = []
    for k in range(slots):
        label = turned[SLOT * k + RHS : SLOT * k + RHS + 1, :]
        found = fold(raw(both, row_onehot(label, rows.shape[1]).astype(BF16), 1, 0)) * mask
        one = found[0:RHS]
        for j in range(1, HOLD):
            one = one + found[RHS * j : RHS * (j + 1)]
        out += [one, jnp.zeros((SLOT - RHS, n), F32)]
    return fill(out, n).T


def messages(blocks, targets, shift, count):
    out = []
    for b in range(HOLD):
        dest, label = split_target(targets[b : b + 1], shift)
        one = jnp.concatenate([blocks[b], label_rows(label)], axis=0)
        out.append(fold(raw(stacked(one), row_onehot(dest, count).astype(BF16), 1, 1)))
    return fill(out, count).T


def fetched(back, targets, shift):
    turned = back.T
    count = turned.shape[1]
    out = []
    for b in range(HOLD):
        dest, _ = split_target(targets[b : b + 1], shift)
        values = turned[SLOT * b : SLOT * b + RHS, :]
        out.append(fold(raw(stacked(values), row_onehot(dest, count).astype(BF16), 1, 0)))
    return out


def lanes(blocks):
    return jnp.concatenate(blocks, axis=1)


def tall(blocks):
    return jnp.concatenate(blocks, axis=0)


def cut_lanes(value):
    return [value[:, TILE * b : TILE * (b + 1)] for b in range(HOLD)]


def cut_tall(value):
    return [value[RHS * b : RHS * (b + 1)] for b in range(HOLD)]


def own_number():
    core = jnp.bitwise_and(lax.axis_index("leaf"), 1)
    return core * 4 + lax.axis_index("grid")


def numbers():
    core = jnp.bitwise_and(lax.axis_index("leaf"), 1)
    at = lax.axis_index("grid")
    out = []
    for c in (core, 1 - core):
        for step in (0, 3, 1, 2):
            out.append(c * 4 + jnp.bitwise_and(at + step, 3))
    return out


class Held:
    def __init__(self, bufs, base, low, high, scratch, sems):
        self.low = low
        self.scratch = scratch
        self.copies = []
        for i, (buf, at) in enumerate(zip(bufs, numbers())):
            copy = pltpu.make_async_copy(
                buf.at[pl.ds(base + low, high - low)], scratch.at[at], sems.at[i]
            )
            copy.start()
            self.copies.append(copy)

    def wait(self):
        for copy in self.copies:
            copy.wait()

    def one(self, b, at, rows=TILE):
        return self.scratch[b, at - self.low : at - self.low + rows, :]

    def all(self, at):
        return self.scratch[:, at - self.low : at - self.low + TILE, :].reshape(
            HOLD * TILE, TILE
        )

    def misc(self, at, row):
        return jnp.concatenate([self.one(b, at + row, 1) for b in range(HOLD)], axis=0)


def by_tiles(blocks, held, at, turned=False):
    return [
        dot(blocks[b], held.one(b, at), 1, 1 if turned else 0) for b in range(HOLD)
    ]


def split_refs(refs, n_in, n_out):
    bufs = refs[0:HOLD]
    ins = refs[HOLD : HOLD + n_in]
    outs = refs[HOLD + n_in : HOLD + n_in + n_out]
    scratch, sems = refs[HOLD + n_in + n_out :]
    return bufs, ins, outs, scratch, sems


def leaf_start_kernel(src, w, p, q, tl, first, y0, slot):
    b = src[...]
    y = mm(b, w[...])
    v = q[:, TILE:]
    first[0:RHS, :] = mm(b, q[:, 0:TILE])
    first[RHS : 2 * RHS, :] = mm(y, v)
    first[2 * RHS :, :] = cross_product(p[...], v)
    y0[...] = y
    dest, _ = split_target(tl[...], 13)
    slot[...] = leaf_slots(row_onehot(dest, 64))


def pack_kernel(*refs):
    (sm, wm, pm, qm, vm, cm, tm), rest = refs[0:7], refs[7:]
    (su, wu, pu, qu, vu, cu, tu), rest = rest[0:7], rest[7:]
    (sr, wr, pr, qr, vr), rest = rest[0:5], rest[5:]
    pack_m, pack_u = rest
    for pack, s, wt, pt, qt, vt, ct, t in (
        (pack_m, sm, wm, pm, qm, vm, cm, tm),
        (pack_u, su, wu, pu, qu, vu, cu, tu),
    ):
        pack[SRC:WAT, :] = s[...]
        pack[WAT:QAT, :] = wt[...]
        pack[QAT:VAT, :] = qt[:, 0:TILE]
        pack[VAT:MISC, :] = qt[:, TILE:]
        at = iota((8, TILE), 0)
        pack[MISC:CAT, :] = jnp.where(
            at == 0,
            jnp.broadcast_to(vt[...], (8, TILE)),
            jnp.broadcast_to(t[...].astype(F32), (8, TILE)),
        )
        pack[CAT:PAT, :] = ct[...]
        pack[PAT:END, :] = pt[...]
    pack_u[END + SRC : END + WAT, :] = sr[...]
    pack_u[END + WAT : END + QAT, :] = wr[...]
    pack_u[END + QAT : END + RMISC, :] = qr[:, 0:TILE]
    pack_u[END + RMISC : END + RPAT, :] = jnp.broadcast_to(vr[...], (8, TILE))
    pack_u[END + RPAT : END + REND, :] = pr[...]


def cross_kernel(*refs):
    bufs, (), (k1, k2), scratch, sems = split_refs(refs, 0, 2)
    upper = Held(bufs, 0, VAT, END, scratch.at[:, 0 : END - VAT, :], sems.at[0])
    root = Held(bufs, END, RMISC, REND, scratch.at[:, END - VAT :, :], sems.at[1])
    upper.wait()
    k1[...] = cross(upper.all(PAT), upper.all(VAT))
    root.wait()
    total = None
    for b in range(HOLD):
        p = root.one(b, RPAT)
        part = mm(p.T * root.one(b, RMISC, 1), p)
        total = part if total is None else total + part
    k2[...] = total


def leaf_up_kernel(
    s0, s1, s2, s3, y0, p, piv, c, ranks, tl, slot, out, z_out, zp_out, k_out
):
    total = (s0[...] + s1[...]) + (s2[...] + s3[...])
    mh, mc = masks(ranks, 1)
    k1 = total[2 * RHS :, :]
    hq = total[0:RHS, :] * mh
    wv = (total[RHS : 2 * RHS, :] + mm(hq, k1)) * mc
    e = -mmt(wv, c[...])
    dest, label = split_target(tl[...], 13)
    both = jnp.concatenate([e, label_rows(label)], axis=0)
    at = slot[...]
    parts = jnp.concatenate(
        [both * (at == float(k)).astype(F32) for k in range(SLOTS_LEAF)], axis=0
    )
    sent = fold(raw(stacked(parts), row_onehot(dest, 64).astype(BF16), 1, 1))
    sent = fill([sent], 64).T
    for place in range(HOLD):
        part = sent[HOLD * place : HOLD * (place + 1), :]
        for copy in range(HOLD):
            low = (place * HOLD + copy) * HOLD
            out[low : low + HOLD, :] = part
    z = (y0[...] + mmt(hq, p[...])) * piv[...]
    z_out[...] = z
    zp_out[...] = mm(z, p[...])
    k_out[...] = k1


def write_copies(ref, value):
    rows = value.shape[0]
    for i in range(ref.shape[0] // rows):
        ref[rows * i : rows * (i + 1), :] = value


def write_shares(ref, members, value, parts):
    step = ref.shape[0] // members
    rows = step - parts.shape[0] // min(members, 16)
    each = step - rows
    common = value.shape[0] == rows
    for i in range(members):
        low = step * i
        ref[low : low + rows, :] = value if common else value[rows * i : rows * (i + 1)]
        at = each * (i % 16)
        ref[low + rows : low + step, :] = parts[at : at + each]


def sum_rows(ref, step, low, high):
    total = ref[low:high, :]
    for i in range(1, ref.shape[0] // step):
        total = total + ref[step * i + low : step * i + high, :]
    return total


def stack_rows(ref, step, low, high, count):
    return jnp.concatenate(
        [ref[step * i + low : step * i + high, :] for i in range(count)], axis=0
    )


def enter_middle_kernel(*refs):
    bufs, (got,), (part, y_out, upd_out), scratch, sems = split_refs(refs, 1, 3)
    held = Held(bufs, 0, SRC, VAT, scratch, sems)
    inc = received(got[...].T, SLOTS_LEAF, 2 * TILE)
    held.wait()
    b = [held.one(j, SRC, RHS) + inc[RHS * j : RHS * (j + 1), 0:TILE] for j in range(HOLD)]
    write_copies(part, mm(lanes(b), held.all(QAT)))
    y_out[...] = lanes(by_tiles(b, held, WAT))
    upd_out[...] = inc[:, TILE:]


def middle_kernel(*refs):
    bufs, (red, y0, ranks), (part, z_out, zp_out), scratch, sems = split_refs(refs, 3, 3)
    held = Held(bufs, 0, VAT, END, scratch, sems)
    mh, _ = masks(ranks, 16)
    hq = sum_rows(red, RHS, 0, RHS) * mh
    held.wait()
    p, v = held.all(PAT), held.all(VAT)
    y = y0[...] + mmt(hq, p)
    write_shares(part, 8, mm(y, v), cross(p, v))
    z = y * lanes([held.one(b, MISC, 1) for b in range(HOLD)])
    z_out[...] = z
    zp_out[...] = mm(z, p)


def middle_up_kernel(*refs):
    bufs, (red, upd, ranks, k1), (out, k_out), scratch, sems = split_refs(refs, 4, 2)
    held = Held(bufs, 0, MISC, PAT, scratch, sems)
    _, mc = masks(ranks, 16)
    total = sum_rows(red, 3 * RHS, 0, 3 * RHS)
    k_out[...] = total[RHS:, :]
    wv = total[0:RHS, :] * mc
    held.wait()
    e = cut_lanes(mmt(wv, held.all(CAT)))
    upds = cut_tall(upd[...])
    targets = held.misc(MISC, 1).astype(jnp.int32)
    sent = messages([u - v for u, v in zip(upds, e)], targets, 14, 128)
    write_shares(out, 16, sent, k1[...])


def enter_upper_kernel(*refs):
    bufs, (got,), (part, y_out, upd_out), scratch, sems = split_refs(refs, 1, 3)
    held = Held(bufs, 0, SRC, MISC, scratch, sems)
    k1 = sum_rows(got, 2 * RHS, RHS, 2 * RHS)
    inc = received(stack_rows(got, 2 * RHS, 0, RHS, 16).T, HOLD, 2 * TILE)
    held.wait()
    b = [held.one(j, SRC, RHS) + inc[RHS * j : RHS * (j + 1), 0:TILE] for j in range(HOLD)]
    y = lanes(by_tiles(b, held, WAT))
    write_copies(part, tall([mm(lanes(b), held.all(QAT)), mm(y, held.all(VAT)), k1]))
    y_out[...] = y
    upd_out[...] = inc[:, TILE:]


def upper_up_kernel(*refs):
    bufs, ins, outs, scratch, sems = split_refs(refs, 5, 4)
    red, y0, upd, ranks, k2 = ins
    out, z_out, zp_out, k_out = outs
    held = Held(bufs, 0, MISC, END, scratch, sems)
    total = sum_rows(red, 3 * RHS, 0, 2 * RHS)
    k1 = stack_rows(red, 3 * RHS, 2 * RHS, 3 * RHS, 16)
    k_out[...] = k1
    mh, mc = masks(ranks, 32)
    hq = total[0:RHS, :] * mh
    wv = (total[RHS:, :] + mm(hq, k1)) * mc
    held.wait()
    e = cut_lanes(mmt(wv, held.all(CAT)))
    upds = cut_tall(upd[...])
    targets = held.misc(MISC, 1).astype(jnp.int32)
    sent = messages([u - v for u, v in zip(upds, e)], targets, 15, 256)
    write_shares(out, 32, sent, k2[...])
    y = y0[...] + mmt(hq, held.all(PAT))
    z = y * lanes([held.one(b, MISC, 1) for b in range(HOLD)])
    z_out[...] = z
    zp_out[...] = mm(z, held.all(PAT))


def enter_root_kernel(*refs):
    bufs, (got,), (part, y_out), scratch, sems = split_refs(refs, 1, 2)
    held = Held(bufs, END, SRC, REND, scratch, sems)
    k2 = sum_rows(got, 2 * RHS, RHS, 2 * RHS)
    inc = received(stack_rows(got, 2 * RHS, 0, RHS, 32).T, HOLD, TILE)
    held.wait()
    b = [held.one(j, SRC, RHS) + inc[RHS * j : RHS * (j + 1)] for j in range(HOLD)]
    y = lanes(by_tiles(b, held, WAT))
    z = y * lanes([held.one(j, RMISC, 1) for j in range(HOLD)])
    write_copies(part, tall([mm(lanes(b), held.all(QAT)), mm(z, held.all(RPAT)), k2]))
    y_out[...] = y


def own_block(blocks):
    me = own_number()
    out = blocks[0]
    for b in range(1, HOLD):
        out = jnp.where(me == b, blocks[b], out)
    return out


def root_kernel(*refs):
    bufs, (red, y0, ranks, got), (answer, reply), scratch, sems = split_refs(refs, 4, 2)
    held = Held(bufs, END, WAT, REND, scratch, sems)
    total = sum_rows(red, 3 * RHS, 0, 2 * RHS)
    k2 = stack_rows(red, 3 * RHS, 2 * RHS, 3 * RHS, 16)
    mh, _ = masks(ranks, 64)
    hq = total[0:RHS, :] * mh
    pr = (total[RHS:, :] + mm(hq, k2)) * mh
    turned = stack_rows(got, 2 * RHS, 0, RHS, 32).T
    held.wait()
    r = y0[...] + mmt(hq, held.all(RPAT))
    r = r * lanes([held.one(j, RMISC, 1) for j in range(HOLD)])
    x = by_tiles(cut_lanes(r), held, WAT, True)
    low = cut_lanes(mmt(pr, held.all(QAT)))
    x = [u + v for u, v in zip(x, low)]
    answer[...] = own_block(x)
    reply[...] = replies(turned, HOLD, tall(x))


def fetch_kernel(shift, with_cross, *refs):
    n_in = 3 if with_cross else 2
    bufs, ins, (part, xu_out), scratch, sems = split_refs(refs, n_in, 2)
    back, zp = ins[0:2]
    held = Held(bufs, 0, MISC, PAT, scratch, sems)
    held.wait()
    targets = held.misc(MISC, 1).astype(jnp.int32)
    xu = fetched(back[...], targets, shift)
    write_copies(
        part, tall([mm(lanes(xu), held.all(CAT))] + [ref[...] for ref in ins[1:]])
    )
    xu_out[...] = tall(xu)


def solve_held(total, z, k1, held, mh, mc):
    s = total[0:RHS, :] * mc
    r = z - mmt(s, held.all(VAT))
    pr = (total[RHS:, :] - mmt(s, k1)) * mh
    x = by_tiles(cut_lanes(r), held, WAT, True)
    low = cut_lanes(mmt(pr, held.all(QAT)))
    return [u + v for u, v in zip(x, low)]


def down_kernel(groups, *refs):
    middle = groups == 16
    n_in = 5 if middle else 6
    bufs, ins, (answer, reply), scratch, sems = split_refs(refs, n_in, 2)
    red, z, ranks, xu, got = ins[0:5]
    held = Held(bufs, 0, WAT, MISC, scratch, sems)
    mh, mc = masks(ranks, groups)
    if middle:
        total = sum_rows(red, 4 * RHS, 0, 2 * RHS)
        k1 = stack_rows(red, 4 * RHS, 2 * RHS, 4 * RHS, 8)
        me = own_number()
        rows = [
            got[pl.ds(pl.multiple_of((HOLD * i + me) * HOLD, HOLD), HOLD), :]
            for i in range(HOLD)
        ]
        turned, slots = tall(rows).T, SLOTS_LEAF
    else:
        total = sum_rows(red, 2 * RHS, 0, 2 * RHS)
        k1 = ins[5][...]
        turned, slots = stack_rows(got, 2 * RHS, 0, RHS, 16).T, HOLD
    held.wait()
    x = solve_held(total, z[...], k1, held, mh, mc)
    answer[...] = own_block(x)
    reply[...] = replies(turned, slots, jnp.concatenate([tall(x), xu[...]], axis=1))


def fetch_leaf_kernel(back, t, slot, c, zp, part):
    dest, _ = split_target(t[...], 13)
    turned = back[...].T
    rows = tall([turned[SLOT * k : SLOT * k + RHS, :] for k in range(SLOTS_LEAF)])
    both = fold(raw(stacked(rows), row_onehot(dest, 64).astype(BF16), 1, 0))
    at = slot[...]
    xu = None
    for k in range(SLOTS_LEAF):
        one = both[RHS * k : RHS * (k + 1), :] * (at == float(k)).astype(F32)
        xu = one if xu is None else xu + one
    part[0:RHS, :] = mm(xu, c[...])
    part[RHS:, :] = zp[...]


def leaf_kernel(s0, s1, s2, s3, z, k1, w, q, ranks, answer):
    total = (s0[...] + s1[...]) + (s2[...] + s3[...])
    mh, mc = masks(ranks, 1)
    s = total[0:RHS, :] * mc
    r = z[...] - mmt(s, q[:, TILE:])
    pr = (total[RHS:, :] - mmt(s, k1[...])) * mh
    answer[...] = mmt(r, w[...]) + mmt(pr, q[:, 0:TILE])


def run(kernel, shapes, *args, held=None, rows=0, twice=False):
    outs = [jax.ShapeDtypeStruct(s, F32) for s in shapes]
    name = getattr(kernel, "func", kernel).__name__
    options = {}
    if held is not None:
        args = tuple(held) + args
        space = pl.BlockSpec(memory_space=pl.ANY)
        options["in_specs"] = [space] * HOLD + [
            pl.BlockSpec(memory_space=pltpu.VMEM) for _ in args[HOLD:]
        ]
        options["scratch_shapes"] = [
            pltpu.VMEM((HOLD, rows, TILE), F32),
            pltpu.SemaphoreType.DMA((2, HOLD) if twice else (HOLD,)),
        ]
    single = len(outs) == 1
    return pl.pallas_call(
        kernel, out_shape=outs[0] if single else outs, name=name, **options
    )(*args)


def swap(value, axis, mask):
    pairs = [(s, s ^ mask) for s in range(lax.axis_size(axis))]
    return lax.ppermute(value, axis, pairs)


def shift(value, step):
    size = lax.axis_size("grid")
    return lax.ppermute(value, "grid", [(s, (s + step) % size) for s in range(size)])


def four(value, axis, unit):
    return [value] + [swap(value, axis, unit * m) for m in (1, 2, 3)]


def add_four(values):
    return (values[0] + values[1]) + (values[2] + values[3])


def together(*values):
    return lax.optimization_barrier(values)


def between(value, members):
    size = lax.axis_size("leaf")
    groups = [
        [start + core + 2 * i for i in range(members)]
        for start in range(0, size, 2 * members)
        for core in range(2)
    ]
    return lax.all_to_all(
        value, "leaf", split_axis=0, concat_axis=0, tiled=True, axis_index_groups=groups
    )


def route_leaf(value):
    size = lax.axis_size("leaf") * lax.axis_size("grid")
    groups = [list(range(g, g + 64)) for g in range(0, size, 64)]
    return lax.all_to_all(
        value,
        ("leaf", "grid"),
        split_axis=0,
        concat_axis=0,
        tiled=True,
        axis_index_groups=groups,
    )


def shards(
    src_l, w_l, p_l, q_l, piv_l, c_l, ranks_l, t_l,
    src_m, w_m, p_m, q_m, piv_m, c_m, ranks_m, t_m,
    src_u, w_u, p_u, q_u, piv_u, c_u, ranks_u, t_u,
    src_r, w_r, p_r, q_r, piv_r, ranks_r,
):
    t_l, t_m, t_u = (t.reshape(1, -1) for t in (t_l, t_m, t_u))
    piv_l, piv_m, piv_u, piv_r = (v.reshape(1, -1) for v in (piv_l, piv_m, piv_u, piv_r))
    row = (RHS, TILE)
    pair = (2 * RHS, TILE)
    flat = (RHS, HOLD * TILE)
    high = (HOLD * RHS, TILE)

    first, y_l, slot_l = run(
        leaf_start_kernel, [(2 * RHS + TILE, TILE), row, (1, 2 * TILE)],
        src_l, w_l, p_l, q_l, t_l,
    )
    sums = four(first, "grid", 1)
    pack_m, pack_u = run(
        pack_kernel, [(END, TILE), (END + REND, TILE)],
        src_m, w_m, p_m, q_m, piv_m, c_m, t_m,
        src_u, w_u, p_u, q_u, piv_u, c_u, t_u,
        src_r, w_r, p_r, q_r, piv_r,
    )
    m_core, u_core = swap(pack_m, "leaf", 1), swap(pack_u, "leaf", 1)
    *sums, pack_m = together(*sums, pack_m)
    m_prev, m_next = shift(pack_m, 1), shift(pack_m, -1)
    out, z_l, zp_l, k_l = run(
        leaf_up_kernel,
        [(64 * HOLD, LANES), row, row, (TILE, TILE)],
        *sums, y_l, p_l, piv_l, c_l, ranks_l, t_l, slot_l,
    )
    got_m = route_leaf(out)
    m_prev, m_next, pack_u = together(m_prev, m_next, pack_u)
    m_opp = jnp.concatenate([shift(m_prev[:MISC], 1), shift(m_next[MISC:], -1)], axis=0)
    m_prev_core, m_next_core = swap(m_prev, "leaf", 1), swap(m_next, "leaf", 1)
    u_prev, u_next = shift(pack_u, 1), shift(pack_u, -1)
    m_opp_core = swap(m_opp, "leaf", 1)
    held_m = (
        pack_m, m_prev, m_next, m_opp, m_core, m_prev_core, m_next_core, m_opp_core,
    )

    part, y_m, upd_m = run(
        enter_middle_kernel, [(8 * RHS, TILE), flat, high], got_m, held=held_m, rows=VAT - SRC
    )
    part, u_prev, u_next = together(part, u_prev, u_next)
    u_opp = jnp.concatenate([shift(u_prev[:END], 1), shift(u_next[END:], -1)], axis=0)
    u_prev_core, u_next_core = swap(u_prev, "leaf", 1), swap(u_next, "leaf", 1)
    red = between(part, 8)
    part, z_m, zp_m = run(
        middle_kernel, [(8 * 3 * RHS, TILE), flat, row],
        red, y_m, ranks_m, held=held_m, rows=END - VAT,
    )
    part, u_opp = together(part, u_opp)
    u_opp_core = swap(u_opp, "leaf", 1)
    held_u = (
        pack_u, u_prev, u_next, u_opp, u_core, u_prev_core, u_next_core, u_opp_core,
    )
    k_u, k_r = run(
        cross_kernel, [(TILE, TILE)] * 2, held=held_u, rows=END - VAT + REND - RMISC,
        twice=True,
    )
    red = between(part, 8)
    out, k_m = run(
        middle_up_kernel, [(16 * 2 * RHS, LANES), pair],
        red, upd_m, ranks_m, k_u, held=held_m, rows=PAT - MISC,
    )
    got_u = between(out, 16)

    part, y_u, upd_u = run(
        enter_upper_kernel, [(16 * 3 * RHS, TILE), flat, high],
        got_u, held=held_u, rows=MISC - SRC,
    )
    red = between(part, 16)
    out, z_u, zp_u, k_u = run(
        upper_up_kernel, [(32 * 2 * RHS, LANES), flat, row, (TILE, TILE)],
        red, y_u, upd_u, ranks_u, k_r, held=held_u, rows=END - MISC,
    )
    got_r = between(out, 32)

    part, y_r = run(
        enter_root_kernel, [(32 * 3 * RHS, TILE), flat],
        got_r, held=held_u, rows=REND - SRC,
    )
    red = between(part, 32)
    x_r, out = run(
        root_kernel, [row, (256, LANES)],
        red, y_r, ranks_r, got_r, held=held_u, rows=REND - WAT,
    )

    back = between(out, 32)
    part, xu = run(
        functools.partial(fetch_kernel, 15, False), [(16 * 2 * RHS, TILE), high],
        back, zp_u, held=held_u, rows=PAT - MISC,
    )
    red = between(part, 16)
    x_u, out = run(
        functools.partial(down_kernel, 32), [row, (128, LANES)],
        red, z_u, ranks_u, xu, got_u, k_u, held=held_u, rows=MISC - WAT,
    )

    back = between(out, 16)
    part, xu = run(
        functools.partial(fetch_kernel, 14, True), [(8 * 4 * RHS, TILE), high],
        back, zp_m, k_m, held=held_m, rows=PAT - MISC,
    )
    red = between(part, 8)
    x_m, out = run(
        functools.partial(down_kernel, 16), [row, (64, LANES)],
        red, z_m, ranks_m, xu, got_m, held=held_m, rows=MISC - WAT,
    )

    back = between(out, 8)
    part = run(fetch_leaf_kernel, [pair], back, t_l, slot_l, c_l, zp_l)
    x_l = run(
        leaf_kernel, [row], *four(part, "grid", 1), z_l, k_l, w_l, q_l, ranks_l
    )
    return (x_l, x_m, x_u, x_r)


def solution(mesh):
    both = ("leaf", "grid")
    wide = P(None, both)
    deep = P(both, None)
    line = P(both)
    level = (wide, deep, deep, deep, line, deep, P(), line)
    in_specs = level * 3 + (wide, deep, deep, deep, line, P())
    return jax.shard_map(
        shards, mesh=mesh, in_specs=in_specs, out_specs=(wide,) * 4, check_vma=False
    )
```

time: 310 us -> 268 us (0.86)
  waiting for transfers between devices: 59.6 us -> 34.2 us
  blocking collectives: 150 us -> 126 us
  Pallas kernels: 35.3 us -> 54.9 us
  starting transfers between devices: 54 us -> 43 us
    ppermute x32 -> x14, waiting for transfers between devices: 53.1 us -> 6.19 us  [swap(): return lax.ppermute(value, axis, pairs)]
    ppermute x32 -> x14, starting transfers between devices: 46.6 us -> 11.1 us  [swap(): return lax.ppermute(value, axis, pairs)]
    all_to_all x9, blocking collectives: 150 us -> 126 us  [between(): lax.all_to_all(value, 'leaf', split_axis=0, concat_axis=0, tiled=True, ax...]
    pallas_call x14 -> x17, Pallas kernels: 35.3 us -> 54.9 us  [run(): pl.pallas_call(kernel, out_shape=outs[0] if single else outs, name=name,...]
    all_to_all x2 -> x3, starting transfers between devices: 7.38 us -> 21.7 us  [the longest x1 12.3 us: route_leaf(): lax.all_to_all(value, ('leaf', 'grid'), split_axis=0, concat_axis=0, tile...]
    all_to_all x2 -> x3, waiting for transfers between devices: 6.44 us -> 20.1 us  [the longest x2 11.4 us: between(): lax.all_to_all(value, 'leaf', split_axis=0, concat_axis=0, tiled=True, ax...]
    ppermute x0 -> x8, starting transfers between devices: none -> 10.1 us  [shift(): lax.ppermute(value, 'grid', [(s, (s + step) % size) for s in range(size)])]
    ppermute x0 -> x8, waiting for transfers between devices: none -> 7.87 us  [shift(): lax.ppermute(value, 'grid', [(s, (s + step) % size) for s in range(size)])]
  transfers between devices with their start and end apart: 34 -> 25, of which waited for: 23 -> 11; matrix products, arithmetic and copies ran while one was open for 1% -> 2% of each run, Pallas kernels for 2% -> 6%
where the time goes in v1:
time: 268 us; the launch traced here: 266 us
  blocking collectives  126 us (47%)
  Pallas kernels  54.9 us (20%)
  starting transfers between devices  43 us (16%)
  waiting for transfers between devices  34.2 us (13%)
  local copies, waits for them, and re-layouts  6.59 us (2%)
    all_to_all x9, blocking collectives, between(): lax.all_to_all(value, 'leaf', split_axis=0, concat_axis=0, tiled=True, ax...  126 us
    pallas_call x17, Pallas kernels, run(): pl.pallas_call(kernel, out_shape=outs[0] if single else outs, name=name,...  54.9 us
    all_to_all x1, starting transfers between devices, route_leaf(): lax.all_to_all(value, ('leaf', 'grid'), split_axis=0, concat_axis=0, tile...  12.3 us
    all_to_all x2, waiting for transfers between devices, between(): lax.all_to_all(value, 'leaf', split_axis=0, concat_axis=0, tiled=True, ax...  11.4 us
    ppermute x14, starting transfers between devices, swap(): return lax.ppermute(value, axis, pairs)  11.1 us
    ppermute x8, starting transfers between devices, shift(): lax.ppermute(value, 'grid', [(s, (s + step) % size) for s in range(size)])  10.1 us
    all_to_all x2, starting transfers between devices, between(): lax.all_to_all(value, 'leaf', split_axis=0, concat_axis=0, tiled=True, ax...  9.39 us
    all_to_all x1, waiting for transfers between devices, route_leaf(): lax.all_to_all(value, ('leaf', 'grid'), split_axis=0, concat_axis=0, tile...  8.72 us
  transfers between devices with their start and end apart: 25, of which 11 were waited for; matrix products, arithmetic and copies ran while one was open for 2% of the time, Pallas kernels for 6%

profile of v1, /device:TPU:2, one launch (start us, length us, event | category | flops | bytes accessed | tf_op | source)
XLA Modules:
  0.0 266.4 jit_solution(905694783924088187)
XLA Ops:
  0.6 1.9 leaf_start_kernel.1
  2.5 1.5 collective-permute-start.2
  4.0 2.8 %collective-permute-start.1 = (f32[144,128]{1,0:T(8,128)}, f32[144,128]{1,0:T(8,128)S(1)}, u32[]{:S(2)}, u32[]{:S(2)}) collective-permute-start(f32[144,128]{1,0:T(8,128)} %get-tuple-element.62.s0), channel_id=1, source_target_pairs={{0,2},{1,3},{2,0},{3,1},{4,6},{5,7},{6,4},{7,5},{8,10},{9,11},{10,... | collective-permute-start | bytes 221192 | tf_op jit(solution)/shard_map/ppermute | solution.py:573
  6.8 2.2 pack_kernel.1
  9.1 1.3 collective-permute-done.1.s2
  10.4 1.0 collective-permute-done.s1
  11.4 0.8 collective-permute-start.4
  12.2 1.2 collective-permute-start.3
  13.4 5.4 %collective-permute-done.4.refs_2_ = f32[656,128]{1,0:T(8,128)S(1)} collective-permute-done((f32[656,128]{1,0:T(8,128)}, f32[656,128]{1,0:T(8,128)S(1)}, u32[]{:S(2)}, u32[]{:S(2)}) %collective-permute-start.4) | collective-permute-done | bytes 335904 | tf_op jit(solution)/shard_map/ppermute | solution.py:578
  18.8 1.4 collective-permute-done.3.refs_1_
  20.2 0.7 collective-permute-start.5
  20.9 0.7 slice.13
  21.6 2.4 collective-permute-start.6
  24.0 0.7 copy.34.ranks
  24.7 2.5 leaf_up_kernel.1
  27.2 12.3 %all-to-all-start = ((f32[64,8,128]{2,1,0:T(8,128)}), f32[64,8,128]{2,1,0:T(8,128)}, u32[]{:S(2)}, u32[]{:S(2)}) async-start(f32[64,8,128]{2,1,0:T(8,128)} %bitcast.43), calls=%async_computation | async-start | bytes 524288 | tf_op jit(solution)/shard_map/all_to_all | solution.py:608
  39.7 0.5 collective-permute-start.12
  40.2 1.5 collective-permute-start.11
  41.9 0.9 constant_dynamic-update-slice_fusion.refs_3_
  42.9 0.6 collective-permute-start.10
  43.4 8.7 %all-to-all-done = f32[64,8,128]{2,1,0:T(8,128)} async-done(((f32[64,8,128]{2,1,0:T(8,128)}), f32[64,8,128]{2,1,0:T(8,128)}, u32[]{:S(2)}, u32[]{:S(2)}) %all-to-all-start) | async-done | bytes 262176 | tf_op jit(solution)/shard_map/all_to_all | solution.py:608
  52.2 0.7 copy-done.11
  52.9 3.5 %enter_middle_kernel.1 = (f32[64,128]{1,0:T(8,128)}, f32[8,1024]{1,0:T(8,128)}, f32[64,128]{1,0:T(8,128)}) custom-call(f32[656,128]{1,0:T(8,128)} %get-tuple-element.57.refs_0_, f32[656,128]{1,0:T(8,128)} %copy-done.6, f32[656,128]{1,0:T(8,128)} %copy-done.8, f32[656,128]{1,0:T(8,128)} %copy-done.7, f32[656,128]{1,0:T(8,128)} %copy-done.10, ...), custom_call_target="tpu_custom_call" | custom-call | tf_op jit(solution)/shard_map/enter_middle_kernel/pallas_call | solution.py:566
  56.4 0.5 collective-permute-done.12.refs_2_
  56.9 0.7 collective-permute-done.11.refs_1_
  57.6 0.8 collective-permute-start.13
  58.4 2.2 collective-permute-start.14
  60.6 6.0 %all-to-all-start.1 = ((f32[8,8,128]{2,1,0:T(8,128)}), f32[8,8,128]{2,1,0:T(8,128)S(1)}, u32[]{:S(2)}, u32[]{:S(2)}) async-start(f32[8,8,128]{2,1,0:T(8,128)} %bitcast.9), calls=%async_computation.1 | async-start | bytes 65536 | tf_op jit(solution)/shard_map/all_to_all | solution.py:600
  66.6 0.7 copy.35.refs_10_
  67.3 0.5 collective-permute-start.16
  67.9 6.7 %all-to-all-done.1 = f32[8,8,128]{2,1,0:T(8,128)S(1)} async-done(((f32[8,8,128]{2,1,0:T(8,128)}), f32[8,8,128]{2,1,0:T(8,128)S(1)}, u32[]{:S(2)}, u32[]{:S(2)}) %all-to-all-start.1) | async-done | bytes 32800 | tf_op jit(solution)/shard_map/all_to_all | solution.py:600
  74.6 0.6 copy-done.13
  75.3 3.6 %middle_kernel.1 = (f32[192,128]{1,0:T(8,128)}, f32[8,1024]{1,0:T(8,128)}, f32[8,128]{1,0:T(8,128)}) custom-call(f32[656,128]{1,0:T(8,128)} %get-tuple-element.57.refs_0_, f32[656,128]{1,0:T(8,128)} %copy-done.6, f32[656,128]{1,0:T(8,128)} %copy-done.8, f32[656,128]{1,0:T(8,128)} %copy-done.7, f32[656,128]{1,0:T(8,128)} %copy-done.10, ...), custom_call_target="tpu_custom_call" | custom-call | tf_op jit(solution)/shard_map/middle_kernel/pallas_call | solution.py:566
  78.9 1.0 pad_maximum_fusion.refs_3_
  80.0 3.4 %all-to-all-start.2 = ((f32[8,24,128]{2,1,0:T(8,128)}), f32[8,24,128]{2,1,0:T(8,128)S(1)}, u32[]{:S(2)}, u32[]{:S(2)}) async-start(f32[8,24,128]{2,1,0:T(8,128)} %bitcast.11), calls=%async_computation.2 | async-start | bytes 196608 | tf_op jit(solution)/shard_map/all_to_all | solution.py:600
  83.5 0.7 copy-done.4
  84.2 0.2 copy-done.5
  84.4 3.5 %cross_kernel.1 = (f32[128,128]{1,0:T(8,128)}, f32[128,128]{1,0:T(8,128)}) custom-call(f32[1056,128]{1,0:T(8,128)} %get-tuple-element.61.refs_0_, f32[1056,128]{1,0:T(8,128)} %copy-done.1, f32[1056,128]{1,0:T(8,128)} %copy-done.2, f32[1056,128]{1,0:T(8,128)} %copy-done, f32[1056,128]{1,0:T(8,128)} %copy-done.4, f32[1056,128]{1,0:T(8,128)} %copy-done.5, ...), custom_call_target="tpu_custom_call" | custom-call | tf_op jit(solution)/shard_map/cross_kernel/pallas_call | solution.py:566
  88.0 4.7 %all-to-all-done.2 = f32[8,24,128]{2,1,0:T(8,128)S(1)} async-done(((f32[8,24,128]{2,1,0:T(8,128)}), f32[8,24,128]{2,1,0:T(8,128)S(1)}, u32[]{:S(2)}, u32[]{:S(2)}) %all-to-all-start.2) | async-done | bytes 98336 | tf_op jit(solution)/shard_map/all_to_all | solution.py:600
  92.6 0.6 copy-done.12
  93.3 3.3 %middle_up_kernel.1 = (f32[256,128]{1,0:T(8,128)}, f32[16,128]{1,0:T(8,128)}) custom-call(f32[656,128]{1,0:T(8,128)} %get-tuple-element.57.refs_0_, f32[656,128]{1,0:T(8,128)} %copy-done.6, f32[656,128]{1,0:T(8,128)} %copy-done.8, f32[656,128]{1,0:T(8,128)} %copy-done.7, f32[656,128]{1,0:T(8,128)} %copy-done.10, f32[656,128]{1,0:T(8,128)} %collective-permute-done.8.refs_5_, ...), custom_call_target="tpu_custom_call" | custom-call | tf_op jit(solution)/shard_map/middle_up_kernel/pallas_call | solution.py:566
  96.6 12.8 %all_to_all.132 = f32[16,16,128]{2,1,0:T(8,128)} all-to-all(f32[16,16,128]{2,1,0:T(8,128)} %bitcast.47), channel_id=1, replica_groups={{0,8,16,24,32,40,48,56,64,72,80,88,96,104,112,120},{4,12,20,28,36,44,52..., dimensions={0} | all-to-all | bytes 262144 | tf_op jit(solution)/shard_map/all_to_all | solution.py:600
  109.4 3.7 %enter_upper_kernel.1 = (f32[384,128]{1,0:T(8,128)}, f32[8,1024]{1,0:T(8,128)}, f32[64,128]{1,0:T(8,128)}) custom-call(f32[1056,128]{1,0:T(8,128)} %get-tuple-element.61.refs_0_, f32[1056,128]{1,0:T(8,128)} %copy-done.1, f32[1056,128]{1,0:T(8,128)} %copy-done.2, f32[1056,128]{1,0:T(8,128)} %copy-done, f32[1056,128]{1,0:T(8,128)} %copy-done.4, ...), custom_call_target="tpu_custom_call" | custom-call | tf_op jit(solution)/shard_map/enter_upper_kernel/pallas_call | solution.py:566
  113.1 13.0 %all_to_all.133 = f32[16,24,128]{2,1,0:T(8,128)} all-to-all(f32[16,24,128]{2,1,0:T(8,128)} %bitcast.45), channel_id=1, replica_groups={{0,8,16,24,32,40,48,56,64,72,80,88,96,104,112,120},{4,12,20,28,36,44,52..., dimensions={0} | all-to-all | bytes 393216 | tf_op jit(solution)/shard_map/all_to_all | solution.py:600
  126.1 3.8 %upper_up_kernel.1 = (f32[512,128]{1,0:T(8,128)}, f32[8,1024]{1,0:T(8,128)}, f32[8,128]{1,0:T(8,128)}, f32[128,128]{1,0:T(8,128)}) custom-call(f32[1056,128]{1,0:T(8,128)} %get-tuple-element.61.refs_0_, f32[1056,128]{1,0:T(8,128)} %copy-done.1, f32[1056,128]{1,0:T(8,128)} %copy-done.2, f32[1056,128]{1,0:T(8,128)} %copy-done, f32[1056,128]{1,0:T(8,128)} %copy-done.4, ...), custom_call_target="tpu_custom_call" | custom-call | tf_op jit(solution)/shard_map/upper_up_kernel/pallas_call | solution.py:566
  129.9 17.4 %all_to_all.134 = f32[32,16,128]{2,1,0:T(8,128)} all-to-all(f32[32,16,128]{2,1,0:T(8,128)} %bitcast.44), channel_id=1, replica_groups={{0,8,16,24,32,40,48,56,64,72,80,88,96,104,112,120,128,136,144,152,160,1..., dimensions={0} | all-to-all | bytes 524288 | tf_op jit(solution)/shard_map/all_to_all | solution.py:600
  147.3 3.7 %enter_root_kernel.1 = (f32[768,128]{1,0:T(8,128)}, f32[8,1024]{1,0:T(8,128)}) custom-call(f32[1056,128]{1,0:T(8,128)} %get-tuple-element.61.refs_0_, f32[1056,128]{1,0:T(8,128)} %copy-done.1, f32[1056,128]{1,0:T(8,128)} %copy-done.2, f32[1056,128]{1,0:T(8,128)} %copy-done, f32[1056,128]{1,0:T(8,128)} %copy-done.4, f32[1056,128]{1,0:T(8,128)} %copy-done.5, ...), custom_call_target="tpu_custom_call" | custom-call | tf_op jit(solution)/shard_map/enter_root_kernel/pallas_call | solution.py:566
  151.0 16.2 %all_to_all.135 = f32[32,24,128]{2,1,0:T(8,128)} all-to-all(f32[32,24,128]{2,1,0:T(8,128)} %bitcast.41), channel_id=1, replica_groups={{0,8,16,24,32,40,48,56,64,72,80,88,96,104,112,120,128,136,144,152,160,1..., dimensions={0} | all-to-all | bytes 786432 | tf_op jit(solution)/shard_map/all_to_all | solution.py:600
  167.2 4.4 %root_kernel.1 = (f32[8,128]{1,0:T(8,128)}, f32[256,128]{1,0:T(8,128)}) custom-call(f32[1056,128]{1,0:T(8,128)} %get-tuple-element.61.refs_0_, f32[1056,128]{1,0:T(8,128)} %copy-done.1, f32[1056,128]{1,0:T(8,128)} %copy-done.2, f32[1056,128]{1,0:T(8,128)} %copy-done, f32[1056,128]{1,0:T(8,128)} %copy-done.4, f32[1056,128]{1,0:T(8,128)} %copy-done.5, ...), custom_call_target="tpu_custom_call" | custom-call | tf_op jit(solution)/shard_map/root_kernel/pallas_call | solution.py:566
  171.6 15.9 %all_to_all.136 = f32[32,8,128]{2,1,0:T(8,128)} all-to-all(f32[32,8,128]{2,1,0:T(8,128)} %bitcast.48), channel_id=1, replica_groups={{0,8,16,24,32,40,48,56,64,72,80,88,96,104,112,120,128,136,144,152,160,1..., dimensions={0} | all-to-all | bytes 262144 | tf_op jit(solution)/shard_map/all_to_all | solution.py:600
  187.4 3.2 %fetch_kernel.2 = (f32[256,128]{1,0:T(8,128)}, f32[64,128]{1,0:T(8,128)}) custom-call(f32[1056,128]{1,0:T(8,128)} %get-tuple-element.61.refs_0_, f32[1056,128]{1,0:T(8,128)} %copy-done.1, f32[1056,128]{1,0:T(8,128)} %copy-done.2, f32[1056,128]{1,0:T(8,128)} %copy-done, f32[1056,128]{1,0:T(8,128)} %copy-done.4, f32[1056,128]{1,0:T(8,128)} %copy-done.5, ...), custom_call_target="tpu_custom_call" | custom-call | tf_op jit(solution)/shard_map/fetch_kernel/pallas_call | solution.py:566
  190.6 12.7 %all_to_all.137 = f32[16,16,128]{2,1,0:T(8,128)} all-to-all(f32[16,16,128]{2,1,0:T(8,128)} %bitcast.50), channel_id=1, replica_groups={{0,8,16,24,32,40,48,56,64,72,80,88,96,104,112,120},{4,12,20,28,36,44,52..., dimensions={0} | all-to-all | bytes 262144 | tf_op jit(solution)/shard_map/all_to_all | solution.py:600
  203.4 4.4 %down_kernel.2 = (f32[8,128]{1,0:T(8,128)}, f32[128,128]{1,0:T(8,128)}) custom-call(f32[1056,128]{1,0:T(8,128)} %get-tuple-element.61.refs_0_, f32[1056,128]{1,0:T(8,128)} %copy-done.1, f32[1056,128]{1,0:T(8,128)} %copy-done.2, f32[1056,128]{1,0:T(8,128)} %copy-done, f32[1056,128]{1,0:T(8,128)} %copy-done.4, f32[1056,128]{1,0:T(8,128)} %copy-done.5, ...), custom_call_target="tpu_custom_call" | custom-call | tf_op jit(solution)/shard_map/down_kernel/pallas_call | solution.py:566
  207.8 12.7 %all_to_all.138 = f32[16,8,128]{2,1,0:T(8,128)} all-to-all(f32[16,8,128]{2,1,0:T(8,128)} %bitcast.52), channel_id=1, replica_groups={{0,8,16,24,32,40,48,56,64,72,80,88,96,104,112,120},{4,12,20,28,36,44,52..., dimensions={0} | all-to-all | bytes 131072 | tf_op jit(solution)/shard_map/all_to_all | solution.py:600
  220.4 3.1 %fetch_kernel.3 = (f32[256,128]{1,0:T(8,128)}, f32[64,128]{1,0:T(8,128)}) custom-call(f32[656,128]{1,0:T(8,128)} %get-tuple-element.57.refs_0_, f32[656,128]{1,0:T(8,128)} %copy-done.6, f32[656,128]{1,0:T(8,128)} %copy-done.8, f32[656,128]{1,0:T(8,128)} %copy-done.7, f32[656,128]{1,0:T(8,128)} %copy-done.10, f32[656,128]{1,0:T(8,128)} %collective-permute-done.8.refs_5_, ...), custom_call_target="tpu_custom_call" | custom-call | tf_op jit(solution)/shard_map/fetch_kernel/pallas_call | solution.py:566
  223.5 13.1 %all_to_all.139 = f32[8,32,128]{2,1,0:T(8,128)} all-to-all(f32[8,32,128]{2,1,0:T(8,128)} %bitcast.49), channel_id=1, replica_groups={{0,8,16,24,32,40,48,56},{4,12,20,28,36,44,52,60},{64,72,80,88,96,104,11..., dimensions={0} | all-to-all | bytes 262144 | tf_op jit(solution)/shard_map/all_to_all | solution.py:600
  236.6 4.3 %down_kernel.3 = (f32[8,128]{1,0:T(8,128)}, f32[64,128]{1,0:T(8,128)}) custom-call(f32[656,128]{1,0:T(8,128)} %get-tuple-element.57.refs_0_, f32[656,128]{1,0:T(8,128)} %copy-done.6, f32[656,128]{1,0:T(8,128)} %copy-done.8, f32[656,128]{1,0:T(8,128)} %copy-done.7, f32[656,128]{1,0:T(8,128)} %copy-done.10, f32[656,128]{1,0:T(8,128)} %collective-permute-done.8.refs_5_, ...), custom_call_target="tpu_custom_call" | custom-call | tf_op jit(solution)/shard_map/down_kernel/pallas_call | solution.py:566
  240.9 12.0 %all_to_all.140 = f32[8,8,128]{2,1,0:T(8,128)} all-to-all(f32[8,8,128]{2,1,0:T(8,128)} %bitcast.53), channel_id=1, replica_groups={{0,8,16,24,32,40,48,56},{4,12,20,28,36,44,52,60},{64,72,80,88,96,104,11..., dimensions={0} | all-to-all | bytes 65536 | tf_op jit(solution)/shard_map/all_to_all | solution.py:600
  252.8 1.8 fetch_leaf_kernel.1.s0
  254.9 5.1 %collective-permute-start.20 = (f32[16,128]{1,0:T(8,128)}, f32[16,128]{1,0:T(8,128)S(1)}, u32[]{:S(2)}, u32[]{:S(2)}) collective-permute-start(f32[16,128]{1,0:T(8,128)} %fetch_leaf_kernel.1.s0), channel_id=1, source_target_pairs={{0,2},{1,3},{2,0},{3,1},{4,6},{5,7},{6,4},{7,5},{8,10},{9,11},{10,... | collective-permute-start | bytes 24584 | tf_op jit(solution)/shard_map/ppermute | solution.py:573
  260.0 1.9 collective-permute-done.20.s2
  261.8 2.0 collective-permute-done.19.s1
  263.8 0.6 copy-done.19
  264.4 2.0 leaf_kernel.1
  (65 shorter events, 0.9 us)
Async XLA Ops:
  2.5 6.5 %collective-permute-start.2 = (f32[144,128]{1,0:T(8,128)}, f32[144,128]{1,0:T(8,128)S(1)}, u32[]{:S(2)}, u32[]{:S(2)}) collective-permute-start(f32[144,128]{1,0:T(8,128)} %get-tuple-element.62.s0), channel_id=1, source_target_pairs={{0,3},{1,2},{2,1},{3,0},{4,7},{5,6},{6,5},{7,4},{8,11},{9,10},{10,... | collective-permute-start | bytes 221192 | tf_op jit(solution)/shard_map/ppermute | solution.py:573
  4.0 6.4 %collective-permute-start.1 = (f32[144,128]{1,0:T(8,128)}, f32[144,128]{1,0:T(8,128)S(1)}, u32[]{:S(2)}, u32[]{:S(2)}) collective-permute-start(f32[144,128]{1,0:T(8,128)} %get-tuple-element.62.s0), channel_id=1, source_target_pairs={{0,2},{1,3},{2,0},{3,1},{4,6},{5,7},{6,4},{7,5},{8,10},{9,11},{10,... | collective-permute-start | bytes 221192 | tf_op jit(solution)/shard_map/ppermute | solution.py:573
  6.8 4.6 %collective-permute-start = (f32[144,128]{1,0:T(8,128)}, f32[144,128]{1,0:T(8,128)S(1)}, u32[]{:S(2)}, u32[]{:S(2)}) collective-permute-start(f32[144,128]{1,0:T(8,128)} %get-tuple-element.62.s0), channel_id=1, source_target_pairs={{0,1},{1,0},{2,3},{3,2},{4,5},{5,4},{6,7},{7,6},{8,9},{9,8},{10,11... | collective-permute-start | bytes 221192 | tf_op jit(solution)/shard_map/ppermute | solution.py:573
  9.1 11.9 %copy-start.9 = (f32[656,128]{1,0:T(8,128)S(1)}, f32[656,128]{1,0:T(8,128)}, u32[]{:S(2)}) copy-start(f32[656,128]{1,0:T(8,128)} %get-tuple-element.57.refs_0_) | copy-start | bytes 1007620
  9.1 11.1 %copy-start.14 = (f32[144,128]{1,0:T(8,128)}, f32[144,128]{1,0:T(8,128)S(1)}, u32[]{:S(2)}) copy-start(f32[144,128]{1,0:T(8,128)S(1)} %collective-permute-done.2.s3) | copy-start | bytes 221188
  10.4 9.8 %copy-start.15 = (f32[144,128]{1,0:T(8,128)}, f32[144,128]{1,0:T(8,128)S(1)}, u32[]{:S(2)}) copy-start(f32[144,128]{1,0:T(8,128)S(1)} %collective-permute-done.1.s2) | copy-start | bytes 221188
  11.4 8.8 %copy-start.16 = (f32[144,128]{1,0:T(8,128)}, f32[144,128]{1,0:T(8,128)S(1)}, u32[]{:S(2)}) copy-start(f32[144,128]{1,0:T(8,128)S(1)} %collective-permute-done.s1) | copy-start | bytes 221188
  11.4 7.4 %collective-permute-start.4 = (f32[656,128]{1,0:T(8,128)}, f32[656,128]{1,0:T(8,128)S(1)}, u32[]{:S(2)}, u32[]{:S(2)}) collective-permute-start(f32[656,128]{1,0:T(8,128)} %get-tuple-element.57.refs_0_), channel_id=1, source_target_pairs={{0,3},{1,0},{2,1},{3,2},{4,7},{5,4},{6,5},{7,6},{8,11},{9,8},{10,9... | collective-permute-start | bytes 1007624 | tf_op jit(solution)/shard_map/ppermute | solution.py:578
  12.2 8.0 %collective-permute-start.3 = (f32[656,128]{1,0:T(8,128)}, f32[656,128]{1,0:T(8,128)S(1)}, u32[]{:S(2)}, u32[]{:S(2)}) collective-permute-start(f32[656,128]{1,0:T(8,128)} %get-tuple-element.57.refs_0_), channel_id=1, source_target_pairs={{0,1},{1,2},{2,3},{3,0},{4,5},{5,6},{6,7},{7,4},{8,9},{9,10},{10,1... | collective-permute-start | bytes 1007624 | tf_op jit(solution)/shard_map/ppermute | solution.py:578
  18.8 23.0 %copy-start.8 = (f32[656,128]{1,0:T(8,128)}, f32[656,128]{1,0:T(8,128)S(1)}, u32[]{:S(2)}) copy-start(f32[656,128]{1,0:T(8,128)S(1)} %collective-permute-done.4.refs_2_) | copy-start | bytes 1007620
  20.2 19.3 %copy-start.6 = (f32[656,128]{1,0:T(8,128)}, f32[656,128]{1,0:T(8,128)S(1)}, u32[]{:S(2)}) copy-start(f32[656,128]{1,0:T(8,128)S(1)} %collective-permute-done.3.refs_1_) | copy-start | bytes 1007620
  20.2 3.8 %copy-start.20 = (s32[64,2]{0,1:T(2,128)S(1)}, s32[64,2]{0,1:T(2,128)}, u32[]{:S(2)}) copy-start(s32[64,2]{0,1:T(2,128)} %param.36) | copy-start | bytes 1540
  20.2 20.0 %collective-permute-start.5 = (f32[392,128]{1,0:T(8,128)S(1)}, f32[392,128]{1,0:T(8,128)S(1)}, u32[]{:S(2)}, u32[]{:S(2)}) collective-permute-start(f32[392,128]{1,0:T(8,128)S(1)} %slice.12), channel_id=1, source_target_pairs={{0,1},{1,2},{2,3},{3,0},{4,5},{5,6},{6,7},{7,4},{8,9},{9,10},{10,1... | collective-permute-start | bytes 602120 | tf_op jit(solution)/shard_map/ppermute | solution.py:578
  20.9 21.9 %collective-permute-start.7 = (f32[656,128]{1,0:T(8,128)S(1)}, f32[656,128]{1,0:T(8,128)S(1)}, u32[]{:S(2)}, u32[]{:S(2)}) collective-permute-start(f32[656,128]{1,0:T(8,128)S(1)} %copy-done.9), channel_id=1, source_target_pairs={{0,4},{4,0},{8,12},{12,8},{16,20},{20,16},{24,28},{28,24},{32,36},... | collective-permute-start | bytes 1007624 | tf_op jit(solution)/shard_map/ppermute | solution.py:573
  21.6 20.2 %collective-permute-start.6 = (f32[264,128]{1,0:T(8,128)}, f32[264,128]{1,0:T(8,128)}, u32[]{:S(2)}, u32[]{:S(2)}) collective-permute-start(f32[264,128]{1,0:T(8,128)} %slice.13), channel_id=1, source_target_pairs={{0,3},{1,0},{2,1},{3,2},{4,7},{5,4},{6,5},{7,6},{8,11},{9,8},{10,9... | collective-permute-start | bytes 405512 | tf_op jit(solution)/shard_map/ppermute | solution.py:578
  24.7 15.0 %copy-start.3 = (f32[1056,128]{1,0:T(8,128)S(1)}, f32[1056,128]{1,0:T(8,128)}, u32[]{:S(2)}) copy-start(f32[1056,128]{1,0:T(8,128)} %get-tuple-element.61.refs_0_) | copy-start | bytes 1622020
  27.2 25.0 %all-to-all-start = ((f32[64,8,128]{2,1,0:T(8,128)}), f32[64,8,128]{2,1,0:T(8,128)}, u32[]{:S(2)}, u32[]{:S(2)}) async-start(f32[64,8,128]{2,1,0:T(8,128)} %bitcast.43), calls=%async_computation | async-start | bytes 524288 | tf_op jit(solution)/shard_map/all_to_all | solution.py:608
  39.5 12.6 %collective-permute-start.8 = (f32[656,128]{1,0:T(8,128)S(1)}, f32[656,128]{1,0:T(8,128)}, u32[]{:S(2)}, u32[]{:S(2)}) collective-permute-start(f32[656,128]{1,0:T(8,128)S(1)} %collective-permute-done.3.refs_1_), channel_id=1, source_target_pairs={{0,4},{4,0},{8,12},{12,8},{16,20},{20,16},{24,28},{28,24},{32,36},... | collective-permute-start | bytes 1007624 | tf_op jit(solution)/shard_map/ppermute | solution.py:573
  39.7 17.1 %collective-permute-start.12 = (f32[1056,128]{1,0:T(8,128)S(1)}, f32[1056,128]{1,0:T(8,128)S(1)}, u32[]{:S(2)}, u32[]{:S(2)}) collective-permute-start(f32[1056,128]{1,0:T(8,128)S(1)} %copy-done.3), channel_id=1, source_target_pairs={{0,3},{1,0},{2,1},{3,2},{4,7},{5,4},{6,5},{7,6},{8,11},{9,8},{10,9... | collective-permute-start | bytes 1622024 | tf_op jit(solution)/shard_map/ppermute | solution.py:578
  40.2 17.3 %collective-permute-start.11 = (f32[1056,128]{1,0:T(8,128)S(1)}, f32[1056,128]{1,0:T(8,128)S(1)}, u32[]{:S(2)}, u32[]{:S(2)}) collective-permute-start(f32[1056,128]{1,0:T(8,128)S(1)} %copy-done.3), channel_id=1, source_target_pairs={{0,1},{1,2},{2,3},{3,0},{4,5},{5,6},{6,7},{7,4},{8,9},{9,10},{10,1... | collective-permute-start | bytes 1622024 | tf_op jit(solution)/shard_map/ppermute | solution.py:578
  41.8 10.4 %collective-permute-start.9 = (f32[656,128]{1,0:T(8,128)S(1)}, f32[656,128]{1,0:T(8,128)}, u32[]{:S(2)}, u32[]{:S(2)}) collective-permute-start(f32[656,128]{1,0:T(8,128)S(1)} %collective-permute-done.4.refs_2_), channel_id=1, source_target_pairs={{0,4},{4,0},{8,12},{12,8},{16,20},{20,16},{24,28},{28,24},{32,36},... | collective-permute-start | bytes 1007624 | tf_op jit(solution)/shard_map/ppermute | solution.py:573
  42.8 9.4 %copy-start.7 = (f32[656,128]{1,0:T(8,128)}, f32[656,128]{1,0:T(8,128)S(1)}, u32[]{:S(2)}) copy-start(f32[656,128]{1,0:T(8,128)S(1)} %constant_dynamic-update-slice_fusion.refs_3_) | copy-start | bytes 1007620
  42.8 9.3 %copy-start.10 = (f32[656,128]{1,0:T(8,128)}, f32[656,128]{1,0:T(8,128)S(1)}, u32[]{:S(2)}) copy-start(f32[656,128]{1,0:T(8,128)S(1)} %collective-permute-done.7.refs_4_) | copy-start | bytes 1007620
  42.9 9.3 %collective-permute-start.10 = (f32[656,128]{1,0:T(8,128)S(1)}, f32[656,128]{1,0:T(8,128)S(1)}, u32[]{:S(2)}, u32[]{:S(2)}) collective-permute-start(f32[656,128]{1,0:T(8,128)S(1)} %constant_dynamic-update-slice_fusion.refs_3_), channel_id=1, source_target_pairs={{0,4},{4,0},{8,12},{12,8},{16,20},{20,16},{24,28},{28,24},{32,36},... | collective-permute-start | bytes 1007624 | tf_op jit(solution)/shard_map/ppermute | solution.py:573
  52.2 0.7 copy-start.11
  56.9 11.0 %copy-start.2 = (f32[1056,128]{1,0:T(8,128)}, f32[1056,128]{1,0:T(8,128)S(1)}, u32[]{:S(2)}) copy-start(f32[1056,128]{1,0:T(8,128)S(1)} %collective-permute-done.12.refs_2_) | copy-start | bytes 1622020
  57.5 9.8 %copy-start.1 = (f32[1056,128]{1,0:T(8,128)}, f32[1056,128]{1,0:T(8,128)S(1)}, u32[]{:S(2)}) copy-start(f32[1056,128]{1,0:T(8,128)S(1)} %collective-permute-done.11.refs_1_) | copy-start | bytes 1622020
  57.6 21.3 %collective-permute-start.13 = (f32[656,128]{1,0:T(8,128)S(1)}, f32[656,128]{1,0:T(8,128)}, u32[]{:S(2)}, u32[]{:S(2)}) collective-permute-start(f32[656,128]{1,0:T(8,128)S(1)} %slice.14), channel_id=1, source_target_pairs={{0,1},{1,2},{2,3},{3,0},{4,5},{5,6},{6,7},{7,4},{8,9},{9,10},{10,1... | collective-permute-start | bytes 1007624 | tf_op jit(solution)/shard_map/ppermute | solution.py:578
  58.4 20.5 %collective-permute-start.14 = (f32[400,128]{1,0:T(8,128)S(1)}, f32[400,128]{1,0:T(8,128)S(1)}, u32[]{:S(2)}, u32[]{:S(2)}) collective-permute-start(f32[400,128]{1,0:T(8,128)S(1)} %slice.15), channel_id=1, source_target_pairs={{0,3},{1,0},{2,1},{3,2},{4,7},{5,4},{6,5},{7,6},{8,11},{9,8},{10,9... | collective-permute-start | bytes 614408 | tf_op jit(solution)/shard_map/ppermute | solution.py:578
  60.6 6.0 %copy-start.21 = (s32[4,2]{0,1:T(2,128)S(1)}, s32[4,2]{0,1:T(2,128)}, u32[]{:S(2)}) copy-start(s32[4,2]{0,1:T(2,128)} %param.44) | copy-start | bytes 100
  60.6 14.0 %all-to-all-start.1 = ((f32[8,8,128]{2,1,0:T(8,128)}), f32[8,8,128]{2,1,0:T(8,128)S(1)}, u32[]{:S(2)}, u32[]{:S(2)}) async-start(f32[8,8,128]{2,1,0:T(8,128)} %bitcast.9), calls=%async_computation.1 | async-start | bytes 65536 | tf_op jit(solution)/shard_map/all_to_all | solution.py:600
  66.6 16.8 %collective-permute-start.15 = (f32[1056,128]{1,0:T(8,128)S(1)}, f32[1056,128]{1,0:T(8,128)S(1)}, u32[]{:S(2)}, u32[]{:S(2)}) collective-permute-start(f32[1056,128]{1,0:T(8,128)S(1)} %copy-done.3), channel_id=1, source_target_pairs={{0,4},{4,0},{8,12},{12,8},{16,20},{20,16},{24,28},{28,24},{32,36},... | collective-permute-start | bytes 1622024 | tf_op jit(solution)/shard_map/ppermute | solution.py:573
  67.3 16.1 %collective-permute-start.16 = (f32[1056,128]{1,0:T(8,128)S(1)}, f32[1056,128]{1,0:T(8,128)S(1)}, u32[]{:S(2)}, u32[]{:S(2)}) collective-permute-start(f32[1056,128]{1,0:T(8,128)S(1)} %collective-permute-done.11.refs_1_), channel_id=1, source_target_pairs={{0,4},{4,0},{8,12},{12,8},{16,20},{20,16},{24,28},{28,24},{32,36},... | collective-permute-start | bytes 1622024 | tf_op jit(solution)/shard_map/ppermute | solution.py:573
  67.8 15.7 %collective-permute-start.17 = (f32[1056,128]{1,0:T(8,128)S(1)}, f32[1056,128]{1,0:T(8,128)}, u32[]{:S(2)}, u32[]{:S(2)}) collective-permute-start(f32[1056,128]{1,0:T(8,128)S(1)} %collective-permute-done.12.refs_2_), channel_id=1, source_target_pairs={{0,4},{4,0},{8,12},{12,8},{16,20},{20,16},{24,28},{28,24},{32,36},... | collective-permute-start | bytes 1622024 | tf_op jit(solution)/shard_map/ppermute | solution.py:573
  74.6 0.6 copy-start.13
  79.9 3.6 %copy-start = (f32[1056,128]{1,0:T(8,128)}, f32[1056,128]{1,0:T(8,128)S(1)}, u32[]{:S(2)}) copy-start(f32[1056,128]{1,0:T(8,128)S(1)} %pad_maximum_fusion.refs_3_) | copy-start | bytes 1622020
  79.9 3.5 %collective-permute-start.18 = (f32[1056,128]{1,0:T(8,128)S(1)}, f32[1056,128]{1,0:T(8,128)}, u32[]{:S(2)}, u32[]{:S(2)}) collective-permute-start(f32[1056,128]{1,0:T(8,128)S(1)} %pad_maximum_fusion.refs_3_), channel_id=1, source_target_pairs={{0,4},{4,0},{8,12},{12,8},{16,20},{20,16},{24,28},{28,24},{32,36},... | collective-permute-start | bytes 1622024 | tf_op jit(solution)/shard_map/ppermute | solution.py:573
  80.0 12.6 %all-to-all-start.2 = ((f32[8,24,128]{2,1,0:T(8,128)}), f32[8,24,128]{2,1,0:T(8,128)S(1)}, u32[]{:S(2)}, u32[]{:S(2)}) async-start(f32[8,24,128]{2,1,0:T(8,128)} %bitcast.11), calls=%async_computation.2 | async-start | bytes 196608 | tf_op jit(solution)/shard_map/all_to_all | solution.py:600
  83.4 0.8 copy-start.4
  83.4 1.0 copy-start.5
  92.6 0.6 copy-start.12
  254.7 5.3 %collective-permute-start.21 = (f32[16,128]{1,0:T(8,128)}, f32[16,128]{1,0:T(8,128)S(1)}, u32[]{:S(2)}, u32[]{:S(2)}) collective-permute-start(f32[16,128]{1,0:T(8,128)} %fetch_leaf_kernel.1.s0), channel_id=1, source_target_pairs={{0,3},{1,2},{2,1},{3,0},{4,7},{5,6},{6,5},{7,4},{8,11},{9,10},{10,... | collective-permute-start | bytes 24584 | tf_op jit(solution)/shard_map/ppermute | solution.py:573
  254.9 6.9 %collective-permute-start.20 = (f32[16,128]{1,0:T(8,128)}, f32[16,128]{1,0:T(8,128)S(1)}, u32[]{:S(2)}, u32[]{:S(2)}) collective-permute-start(f32[16,128]{1,0:T(8,128)} %fetch_leaf_kernel.1.s0), channel_id=1, source_target_pairs={{0,2},{1,3},{2,0},{3,1},{4,6},{5,7},{6,4},{7,5},{8,10},{9,11},{10,... | collective-permute-start | bytes 24584 | tf_op jit(solution)/shard_map/ppermute | solution.py:573
  260.0 3.9 %collective-permute-start.19 = (f32[16,128]{1,0:T(8,128)}, f32[16,128]{1,0:T(8,128)S(1)}, u32[]{:S(2)}, u32[]{:S(2)}) collective-permute-start(f32[16,128]{1,0:T(8,128)} %fetch_leaf_kernel.1.s0), channel_id=1, source_target_pairs={{0,1},{1,0},{2,3},{3,2},{4,5},{5,4},{6,7},{7,6},{8,9},{9,8},{10,11... | collective-permute-start | bytes 24584 | tf_op jit(solution)/shard_map/ppermute | solution.py:573
  260.0 3.9 %copy-start.17 = (f32[16,128]{1,0:T(8,128)}, f32[16,128]{1,0:T(8,128)S(1)}, u32[]{:S(2)}) copy-start(f32[16,128]{1,0:T(8,128)S(1)} %collective-permute-done.21.s3) | copy-start | bytes 24580
  261.8 2.0 copy-start.18
  263.8 0.6 copy-start.19

commit v2 on v1

v2 whole, which is shorter than its diff:
```python
import functools

import jax
import jax.numpy as jnp
from jax import lax
from jax.experimental import pallas as pl
from jax.experimental.pallas import tpu as pltpu
from jax.sharding import PartitionSpec as P

RHS = 8
LANES = 128
TILE = 128
HOLD = 8
SLOT = 16
SLOTS_LEAF = 4

SRC, WAT, QAT, VAT, MISC, CAT, PAT, END = 0, 8, 136, 264, 392, 400, 528, 656
RMISC, RPAT, REND = 264, 272, 400

F32 = jnp.float32
BF16 = jnp.bfloat16


def iota(shape, dim):
    return lax.broadcasted_iota(jnp.int32, shape, dim)


def raw(a, b, ca, cb):
    return lax.dot_general(a, b, (((ca,), (cb,)), ((), ())), preferred_element_type=F32)


def halves(a):
    high = a.astype(BF16)
    low = (a - high.astype(F32)).astype(BF16)
    return high, low


def stacked(a):
    high = a.astype(BF16).astype(F32)
    return jnp.concatenate([high, a - high], axis=0).astype(BF16)


def fold(total):
    rows = total.shape[0] // 2
    return total[0:rows] + total[rows:]


def dot(a, b, ca, cb):
    high, low = halves(b)
    both = stacked(a)
    return fold(raw(both, high, ca, cb) + raw(both, low, ca, cb))


def mm(a, b):
    return dot(a, b, 1, 0)


def mmt(a, b):
    return dot(a, b, 1, 1)


def cross(a, b):
    a_high, a_low = halves(a)
    b_high, b_low = halves(b)
    return (raw(a_low, b_high, 0, 0) + raw(a_high, b_low, 0, 0)) + raw(a_high, b_high, 0, 0)


def mask_rows(ranks_ref, groups):
    front = lax.axis_index("leaf") // groups
    both = ranks_ref[...].astype(F32)
    own = iota(both.shape, 1) == front
    pair = jnp.sum(jnp.where(own, both, 0.0), axis=1, keepdims=True)
    lane = iota((1, TILE), 1).astype(F32)
    return [(lane < pair[i : i + 1, :]).astype(F32) for i in range(2)]


def masks(rows_ref, level):
    return rows_ref[2 * level : 2 * level + 1, :], rows_ref[2 * level + 1 : 2 * level + 2, :]


def split_target(targets, shift):
    piece = lax.shift_right_logical(targets, shift)
    within = jnp.bitwise_and(targets, (1 << shift) - 1)
    dest = lax.shift_right_logical(within, 7)
    label = piece * TILE + jnp.bitwise_and(within, TILE - 1)
    return dest, label.astype(F32)


def row_onehot(at, count):
    n = at.shape[1]
    if at.dtype == jnp.int32:
        rows = iota((count, n), 0)
    else:
        rows = iota((count, n), 0).astype(F32)
    return (rows == jnp.broadcast_to(at, (count, n))).astype(F32)


def leaf_slots(onehot):
    n = onehot.shape[1]
    upper = (iota((n, n), 0) <= iota((n, n), 1)).astype(BF16)
    order = raw(onehot.astype(BF16), upper, 1, 0)
    return jnp.sum(order * onehot, axis=0, keepdims=True) - 1.0


def label_rows(label):
    n = label.shape[1]
    return jnp.where(iota((SLOT - RHS, n), 0) == 0, jnp.broadcast_to(label, (SLOT - RHS, n)), 0.0)


def fill(rows, n):
    used = sum(r.shape[0] for r in rows)
    if used < LANES:
        rows = rows + [jnp.zeros((LANES - used, n), F32)]
    return jnp.concatenate(rows, axis=0)


def block_mask(n):
    lane = jnp.bitwise_and(iota((RHS, n), 1), HOLD - 1)
    return jnp.concatenate([(lane == at).astype(F32) for at in numbers()], axis=0)


def received(turned, slots, cols):
    n = turned.shape[1]
    mask = block_mask(n)
    total = None
    for k in range(slots):
        values = turned[SLOT * k : SLOT * k + RHS, :]
        label = turned[SLOT * k + RHS : SLOT * k + RHS + 1, :]
        spread = jnp.concatenate([values] * HOLD, axis=0) * mask
        part = raw(stacked(spread), row_onehot(label, cols).astype(BF16), 1, 1)
        total = part if total is None else total + part
    return fold(total)


def replies(turned, slots, rows):
    n = turned.shape[1]
    mask = block_mask(n)
    both = stacked(rows)
    out = []
    for k in range(slots):
        label = turned[SLOT * k + RHS : SLOT * k + RHS + 1, :]
        found = fold(raw(both, row_onehot(label, rows.shape[1]).astype(BF16), 1, 0)) * mask
        one = found[0:RHS]
        for j in range(1, HOLD):
            one = one + found[RHS * j : RHS * (j + 1)]
        out += [one, jnp.zeros((SLOT - RHS, n), F32)]
    return fill(out, n).T


def slot_rows(at):
    return pl.ds(pl.multiple_of(SLOT * at, SLOT), SLOT)


def messages(blocks, targets, shift, count, scratch):
    for r, at in enumerate(numbers()):
        dest, label = split_target(targets[r : r + 1], shift)
        one = jnp.concatenate([blocks[r], label_rows(label)], axis=0)
        found = fold(raw(stacked(one), row_onehot(dest, count).astype(BF16), 1, 1))
        scratch[slot_rows(at), :] = found
    return scratch[...].T


def fetched(back, targets, shift, scratch):
    scratch[...] = back.T
    count = scratch.shape[1]
    out = []
    for r, at in enumerate(numbers()):
        dest, _ = split_target(targets[r : r + 1], shift)
        values = scratch[slot_rows(at), :][0:RHS]
        out.append(fold(raw(stacked(values), row_onehot(dest, count).astype(BF16), 1, 0)))
    return out


def lanes(blocks):
    return jnp.concatenate(blocks, axis=1)


def tall(blocks):
    return jnp.concatenate(blocks, axis=0)


def cut_lanes(value):
    return [value[:, TILE * b : TILE * (b + 1)] for b in range(HOLD)]


def cut_tall(value):
    return [value[RHS * b : RHS * (b + 1)] for b in range(HOLD)]


def own_number():
    core = jnp.bitwise_and(lax.axis_index("leaf"), 1)
    return core * 4 + lax.axis_index("grid")


def numbers():
    core = jnp.bitwise_and(lax.axis_index("leaf"), 1)
    at = lax.axis_index("grid")
    out = []
    for c in (core, 1 - core):
        for step in (0, 3, 1, 2):
            out.append(c * 4 + jnp.bitwise_and(at + step, 3))
    return out


class Held:
    def __init__(self, refs, cut, base=0):
        own, prev, after, low, high = refs[0:5]
        self.own = (own, prev, after)
        self.opposite = (low, high)
        self.core = refs[5:8]
        self.core_opposite = refs[8:10]
        self.cut = cut
        self.base = base

    def one(self, b, at, rows=TILE):
        at = at + self.base
        singles, split = (
            (self.own, self.opposite) if b < 4 else (self.core, self.core_opposite)
        )
        if b % 4 < 3:
            ref = singles[b % 4]
        elif at < self.cut:
            ref = split[0]
        else:
            ref = split[1]
            at = at - self.cut
        return ref[at : at + rows, :]

    def all(self, at):
        return jnp.concatenate([self.one(b, at) for b in range(HOLD)], axis=0)

    def misc(self, at, row):
        return jnp.concatenate([self.one(b, at + row, 1) for b in range(HOLD)], axis=0)


class Fetched(Held):
    def __init__(self, refs, cut, low, high, scratch, sems):
        self.low = low
        self.scratch = scratch
        self.copies = []
        own, core = refs[0:5], refs[5:10]
        for half, bufs in enumerate((own, core)):
            for b in range(3):
                self.start(bufs[b], low, low, high, 4 * half + b, sems)
            if low < cut:
                self.start(bufs[3], low, low, min(high, cut), 4 * half + 3, sems)
            if high > cut:
                at = max(low, cut)
                self.start(bufs[4], at - cut, at, high, 4 * half + 3, sems)

    def start(self, buf, source, low, high, b, sems):
        copy = pltpu.make_async_copy(
            buf.at[pl.ds(source, high - low)],
            self.scratch.at[b, pl.ds(low - self.low, high - low)],
            sems.at[len(self.copies)],
        )
        copy.start()
        self.copies.append(copy)

    def wait(self):
        for copy in self.copies:
            copy.wait()

    def one(self, b, at, rows=TILE):
        return self.scratch[b, at - self.low : at - self.low + rows, :]


def by_tiles(blocks, held, at, turned=False):
    return [
        dot(blocks[b], held.one(b, at), 1, 1 if turned else 0) for b in range(HOLD)
    ]


HELD_REFS = 10


LW, LQ, LV, LP, LC, LEND = 0, 128, 256, 384, 512, 768


def leaf_start_kernel(
    src, w, p, q, c, piv, tl, ranks_l, ranks_m, ranks_u, ranks_r,
    first, y0, plan, rows, hold,
):
    b = src[...]
    y = mm(b, w[...])
    v = q[:, TILE:]
    first[0:RHS, :] = mm(b, q[:, 0:TILE])
    first[RHS : 2 * RHS, :] = mm(y, v)
    first[2 * RHS :, :] = cross(p[...], v)
    y0[...] = y
    dest, label = split_target(tl[...], 13)
    plan[0:1, :] = dest.astype(F32)
    plan[1:2, :] = label
    plan[2:3, :] = leaf_slots(row_onehot(dest, 64))
    plan[3:8, :] = jnp.zeros((5, 2 * TILE), F32)
    found = []
    for ranks, groups in ((ranks_l, 1), (ranks_m, 16), (ranks_u, 32), (ranks_r, 64)):
        found += mask_rows(ranks, groups)
    rows[...] = jnp.concatenate(found[0:7] + [piv[...]], axis=0)
    hold[LW:LQ, :] = w[...]
    hold[LQ:LV, :] = q[:, 0:TILE]
    hold[LV:LP, :] = v
    hold[LP:LC, :] = p[...]
    hold[LC:LEND, :] = c[...]


def pack_kernel(*refs):
    (sm, wm, pm, qm, vm, cm, tm), rest = refs[0:7], refs[7:]
    (su, wu, pu, qu, vu, cu, tu), rest = rest[0:7], rest[7:]
    (sr, wr, pr, qr, vr), rest = rest[0:5], rest[5:]
    pack_m, pack_u = rest
    for pack, s, wt, pt, qt, vt, ct, t in (
        (pack_m, sm, wm, pm, qm, vm, cm, tm),
        (pack_u, su, wu, pu, qu, vu, cu, tu),
    ):
        pack[SRC:WAT, :] = s[...]
        pack[WAT:QAT, :] = wt[...]
        pack[QAT:VAT, :] = qt[:, 0:TILE]
        pack[VAT:MISC, :] = qt[:, TILE:]
        at = iota((8, TILE), 0)
        pack[MISC:CAT, :] = jnp.where(
            at == 0,
            jnp.broadcast_to(vt[...], (8, TILE)),
            jnp.broadcast_to(t[...].astype(F32), (8, TILE)),
        )
        pack[CAT:PAT, :] = ct[...]
        pack[PAT:END, :] = pt[...]
    pack_u[END + SRC : END + WAT, :] = sr[...]
    pack_u[END + WAT : END + QAT, :] = wr[...]
    pack_u[END + QAT : END + RMISC, :] = qr[:, 0:TILE]
    pack_u[END + RMISC : END + RPAT, :] = jnp.broadcast_to(vr[...], (8, TILE))
    pack_u[END + RPAT : END + REND, :] = pr[...]


def cross_kernel(*refs):
    _, k1, k2 = refs[HELD_REFS:]
    upper = Held(refs, END)
    root = Held(refs, END, END)
    k1[...] = cross(upper.all(PAT), upper.all(VAT))
    total = None
    for b in range(HOLD):
        p = root.one(b, RPAT)
        part = mm(p.T * root.one(b, RMISC, 1), p)
        total = part if total is None else total + part
    k2[...] = total


def leaf_up_kernel(s0, s1, s2, s3, y0, plan, rows, hold, out, z_out, zp_out, k_out):
    total = (s0[...] + s1[...]) + (s2[...] + s3[...])
    mh, mc = masks(rows, 0)
    k1 = total[2 * RHS :, :]
    hq = total[0:RHS, :] * mh
    wv = (total[RHS : 2 * RHS, :] + mm(hq, k1)) * mc
    e = -mmt(wv, hold[LC:LEND, :])
    both = jnp.concatenate([e, label_rows(plan[1:2, :])], axis=0)
    at = plan[2:3, :]
    parts = jnp.concatenate(
        [both * (at == float(k)).astype(F32) for k in range(SLOTS_LEAF)], axis=0
    )
    sent = fold(raw(stacked(parts), row_onehot(plan[0:1, :], 64).astype(BF16), 1, 1))
    sent = fill([sent], 64).T
    for place in range(HOLD):
        part = sent[HOLD * place : HOLD * (place + 1), :]
        for copy in range(HOLD):
            low = (place * HOLD + copy) * HOLD
            out[low : low + HOLD, :] = part
    p = hold[LP:LC, :]
    z = (y0[...] + mmt(hq, p)) * rows[7:8, :]
    z_out[...] = z
    zp_out[...] = mm(z, p)
    k_out[...] = k1


def write_copies(ref, value):
    rows = value.shape[0]
    for i in range(ref.shape[0] // rows):
        ref[rows * i : rows * (i + 1), :] = value


def write_shares(ref, members, value, parts):
    step = ref.shape[0] // members
    rows = step - parts.shape[0] // min(members, 16)
    each = step - rows
    common = value.shape[0] == rows
    for i in range(members):
        low = step * i
        ref[low : low + rows, :] = value if common else value[rows * i : rows * (i + 1)]
        at = each * (i % 16)
        ref[low + rows : low + step, :] = parts[at : at + each]


def sum_rows(ref, step, low, high):
    total = ref[low:high, :]
    for i in range(1, ref.shape[0] // step):
        total = total + ref[step * i + low : step * i + high, :]
    return total


def stack_rows(ref, step, low, high, count):
    return jnp.concatenate(
        [ref[step * i + low : step * i + high, :] for i in range(count)], axis=0
    )


def enter_middle_kernel(*refs):
    got, part, y_out, upd_out, scratch, sems = refs[HELD_REFS:]
    held = Fetched(refs, MISC, SRC, VAT, scratch, sems)
    inc = received(got[...].T, SLOTS_LEAF, 2 * TILE)
    held.wait()
    b = [held.one(j, SRC, RHS) + inc[RHS * j : RHS * (j + 1), 0:TILE] for j in range(HOLD)]
    write_copies(part, mm(lanes(b), held.all(QAT)))
    y_out[...] = lanes(by_tiles(b, held, WAT))
    upd_out[...] = inc[:, TILE:]


def middle_kernel(*refs):
    red, y0, rows, part, z_out, zp_out, scratch, sems = refs[HELD_REFS:]
    held = Fetched(refs, MISC, VAT, END, scratch, sems)
    mh, _ = masks(rows, 1)
    hq = sum_rows(red, RHS, 0, RHS) * mh
    held.wait()
    p, v = held.all(PAT), held.all(VAT)
    y = y0[...] + mmt(hq, p)
    write_shares(part, 8, mm(y, v), cross(p, v))
    z = y * lanes([held.one(b, MISC, 1) for b in range(HOLD)])
    z_out[...] = z
    zp_out[...] = mm(z, p)


def middle_up_kernel(*refs):
    red, upd, rows, k1, out, k_out, scratch, copied, sems = refs[HELD_REFS:]
    held = Fetched(refs, MISC, MISC, PAT, copied, sems)
    _, mc = masks(rows, 1)
    total = sum_rows(red, 3 * RHS, 0, 3 * RHS)
    k_out[...] = total[RHS:, :]
    wv = total[0:RHS, :] * mc
    held.wait()
    e = cut_lanes(mmt(wv, held.all(CAT)))
    upds = cut_tall(upd[...])
    targets = held.misc(MISC, 1).astype(jnp.int32)
    sent = messages([u - v for u, v in zip(upds, e)], targets, 14, 128, scratch)
    write_shares(out, 16, sent, k1[...])


def enter_upper_kernel(*refs):
    got, part, y_out, upd_out = refs[HELD_REFS:]
    held = Held(refs, END)
    k1 = sum_rows(got, 2 * RHS, RHS, 2 * RHS)
    inc = received(stack_rows(got, 2 * RHS, 0, RHS, 16).T, HOLD, 2 * TILE)
    b = [held.one(j, SRC, RHS) + inc[RHS * j : RHS * (j + 1), 0:TILE] for j in range(HOLD)]
    y = lanes(by_tiles(b, held, WAT))
    write_copies(part, tall([mm(lanes(b), held.all(QAT)), mm(y, held.all(VAT)), k1]))
    y_out[...] = y
    upd_out[...] = inc[:, TILE:]


def upper_up_kernel(*refs):
    red, y0, upd, rows, k2, out, z_out, zp_out, k_out, scratch = refs[HELD_REFS:]
    held = Held(refs, END)
    total = sum_rows(red, 3 * RHS, 0, 2 * RHS)
    k1 = stack_rows(red, 3 * RHS, 2 * RHS, 3 * RHS, 16)
    k_out[...] = k1
    mh, mc = masks(rows, 2)
    hq = total[0:RHS, :] * mh
    wv = (total[RHS:, :] + mm(hq, k1)) * mc
    e = cut_lanes(mmt(wv, held.all(CAT)))
    upds = cut_tall(upd[...])
    targets = held.misc(MISC, 1).astype(jnp.int32)
    sent = messages([u - v for u, v in zip(upds, e)], targets, 15, 256, scratch)
    write_shares(out, 32, sent, k2[...])
    p = held.all(PAT)
    y = y0[...] + mmt(hq, p)
    z = y * lanes([held.one(b, MISC, 1) for b in range(HOLD)])
    z_out[...] = z
    zp_out[...] = mm(z, p)


def enter_root_kernel(*refs):
    got, part, y_out = refs[HELD_REFS:]
    held = Held(refs, END, END)
    k2 = sum_rows(got, 2 * RHS, RHS, 2 * RHS)
    inc = received(stack_rows(got, 2 * RHS, 0, RHS, 32).T, HOLD, TILE)
    b = [held.one(j, SRC, RHS) + inc[RHS * j : RHS * (j + 1)] for j in range(HOLD)]
    y = lanes(by_tiles(b, held, WAT))
    z = y * lanes([held.one(j, RMISC, 1) for j in range(HOLD)])
    write_copies(part, tall([mm(lanes(b), held.all(QAT)), mm(z, held.all(RPAT)), k2]))
    y_out[...] = y


def root_kernel(*refs):
    red, y0, rows, got, answer, reply = refs[HELD_REFS:]
    held = Held(refs, END, END)
    total = sum_rows(red, 3 * RHS, 0, 2 * RHS)
    k2 = stack_rows(red, 3 * RHS, 2 * RHS, 3 * RHS, 16)
    mh = rows[6:7, :]
    hq = total[0:RHS, :] * mh
    pr = (total[RHS:, :] + mm(hq, k2)) * mh
    turned = stack_rows(got, 2 * RHS, 0, RHS, 32).T
    r = y0[...] + mmt(hq, held.all(RPAT))
    r = r * lanes([held.one(j, RMISC, 1) for j in range(HOLD)])
    x = by_tiles(cut_lanes(r), held, WAT, True)
    low = cut_lanes(mmt(pr, held.all(QAT)))
    x = [u + v for u, v in zip(x, low)]
    answer[...] = x[0]
    reply[...] = replies(turned, HOLD, tall(x))


def fetch_kernel(shift, cut, *refs):
    back, *tails, part, xu_out, scratch = refs[HELD_REFS:]
    held = Held(refs, cut)
    targets = held.misc(MISC, 1).astype(jnp.int32)
    xu = fetched(back[...], targets, shift, scratch)
    write_copies(part, tall([mm(lanes(xu), held.all(CAT))] + [ref[...] for ref in tails]))
    xu_out[...] = tall(xu)


def solve_held(total, z, k1, held, mh, mc):
    s = total[0:RHS, :] * mc
    r = z - mmt(s, held.all(VAT))
    pr = (total[RHS:, :] - mmt(s, k1)) * mh
    x = by_tiles(cut_lanes(r), held, WAT, True)
    low = cut_lanes(mmt(pr, held.all(QAT)))
    return [u + v for u, v in zip(x, low)]


def down_upper_kernel(*refs):
    red, z, rows, xu, got, k1, answer, reply = refs[HELD_REFS:]
    held = Held(refs, END)
    mh, mc = masks(rows, 2)
    total = sum_rows(red, 2 * RHS, 0, 2 * RHS)
    turned = stack_rows(got, 2 * RHS, 0, RHS, 16).T
    x = solve_held(total, z[...], k1[...], held, mh, mc)
    answer[...] = x[0]
    reply[...] = replies(turned, HOLD, jnp.concatenate([tall(x), xu[...]], axis=1))


def down_middle_kernel(*refs):
    red, z, rows, xu, got, answer, reply = refs[HELD_REFS:]
    held = Held(refs, MISC)
    mh, mc = masks(rows, 1)
    total = sum_rows(red, 4 * RHS, 0, 2 * RHS)
    k1 = stack_rows(red, 4 * RHS, 2 * RHS, 4 * RHS, 8)
    me = own_number()
    asked = [
        got[pl.ds(pl.multiple_of((HOLD * i + me) * HOLD, HOLD), HOLD), :]
        for i in range(HOLD)
    ]
    x = solve_held(total, z[...], k1, held, mh, mc)
    answer[...] = x[0]
    both = jnp.concatenate([tall(x), xu[...]], axis=1)
    reply[...] = replies(tall(asked).T, SLOTS_LEAF, both)


def fetch_leaf_kernel(back, plan, hold, zp, part):
    turned = back[...].T
    slots = tall([turned[SLOT * k : SLOT * k + RHS, :] for k in range(SLOTS_LEAF)])
    both = fold(raw(stacked(slots), row_onehot(plan[0:1, :], 64).astype(BF16), 1, 0))
    at = plan[2:3, :]
    xu = None
    for k in range(SLOTS_LEAF):
        one = both[RHS * k : RHS * (k + 1), :] * (at == float(k)).astype(F32)
        xu = one if xu is None else xu + one
    part[0:RHS, :] = mm(xu, hold[LC:LEND, :])
    part[RHS:, :] = zp[...]


def leaf_kernel(s0, s1, s2, s3, z, k1, hold, rows, answer):
    total = (s0[...] + s1[...]) + (s2[...] + s3[...])
    mh, mc = masks(rows, 0)
    s = total[0:RHS, :] * mc
    r = z[...] - mmt(s, hold[LV:LP, :])
    pr = (total[RHS:, :] - mmt(s, k1[...])) * mh
    answer[...] = mmt(r, hold[LW:LQ, :]) + mmt(pr, hold[LQ:LV, :])


def run(kernel, shapes, *args, answer=False, inputs=False, scratch=(), copied=0):
    outs = [pltpu.VMEM(s, F32) for s in shapes]
    if answer:
        outs[0] = jax.ShapeDtypeStruct(shapes[0], F32)
    options = {}
    scratch = [pltpu.VMEM(s, F32) for s in scratch]
    if copied:
        scratch += [pltpu.VMEM((HOLD, copied, TILE), F32), pltpu.SemaphoreType.DMA((12,))]
        rest = [pltpu.with_memory_space_constraint(a, pltpu.VMEM) for a in args[HELD_REFS:]]
        far = [pltpu.with_memory_space_constraint(a, pltpu.HBM) for a in args[:HELD_REFS]]
        args = far + rest
        options["in_specs"] = [pl.BlockSpec(memory_space=pltpu.HBM)] * HELD_REFS + [
            pl.BlockSpec(memory_space=pltpu.VMEM) for _ in rest
        ]
    elif not inputs:
        args = [pltpu.with_memory_space_constraint(a, pltpu.VMEM) for a in args]
    return pl.pallas_call(
        kernel,
        out_shape=outs[0] if len(outs) == 1 else outs,
        scratch_shapes=scratch,
        compiler_params=None if inputs else pltpu.CompilerParams(vmem_limit_bytes=16 << 20),
        name=getattr(kernel, "func", kernel).__name__,
        **options,
    )(*args)


def after(done, *values):
    return lax.optimization_barrier((*values, done))[:-1]


def swap(value, axis, mask):
    pairs = [(s, s ^ mask) for s in range(lax.axis_size(axis))]
    return lax.ppermute(value, axis, pairs)


def shift(value, step):
    size = lax.axis_size("grid")
    return lax.ppermute(value, "grid", [(s, (s + step) % size) for s in range(size)])


def four(value, axis, unit):
    return [value] + [swap(value, axis, unit * m) for m in (1, 2, 3)]


def add_four(values):
    return (values[0] + values[1]) + (values[2] + values[3])


def together(*values):
    return lax.optimization_barrier(values)


def between(value, members):
    size = lax.axis_size("leaf")
    groups = [
        [start + core + 2 * i for i in range(members)]
        for start in range(0, size, 2 * members)
        for core in range(2)
    ]
    return lax.all_to_all(
        value, "leaf", split_axis=0, concat_axis=0, tiled=True, axis_index_groups=groups
    )


def route_leaf(value):
    size = lax.axis_size("leaf") * lax.axis_size("grid")
    groups = [list(range(g, g + 64)) for g in range(0, size, 64)]
    return lax.all_to_all(
        value,
        ("leaf", "grid"),
        split_axis=0,
        concat_axis=0,
        tiled=True,
        axis_index_groups=groups,
    )


def shards(
    src_l, w_l, p_l, q_l, piv_l, c_l, ranks_l, t_l,
    src_m, w_m, p_m, q_m, piv_m, c_m, ranks_m, t_m,
    src_u, w_u, p_u, q_u, piv_u, c_u, ranks_u, t_u,
    src_r, w_r, p_r, q_r, piv_r, ranks_r,
):
    ranks_l, ranks_m, ranks_u, ranks_r = (r.T for r in (ranks_l, ranks_m, ranks_u, ranks_r))
    t_l, t_m, t_u = (t.reshape(1, -1) for t in (t_l, t_m, t_u))
    piv_l, piv_m, piv_u, piv_r = (v.reshape(1, -1) for v in (piv_l, piv_m, piv_u, piv_r))
    row = (RHS, TILE)
    pair = (2 * RHS, TILE)
    flat = (RHS, HOLD * TILE)
    high = (HOLD * RHS, TILE)

    first, y_l, plan, rows, hold = run(
        leaf_start_kernel,
        [(2 * RHS + TILE, TILE), row, (RHS, 2 * TILE), row, (LEND, TILE)],
        src_l, w_l, p_l, q_l, c_l, piv_l, t_l, ranks_l, ranks_m, ranks_u, ranks_r,
        inputs=True,
    )
    sums = four(first, "grid", 1)
    pack_m, pack_u = run(
        pack_kernel, [(END, TILE), (END + REND, TILE)],
        src_m, w_m, p_m, q_m, piv_m, c_m, t_m,
        src_u, w_u, p_u, q_u, piv_u, c_u, t_u,
        src_r, w_r, p_r, q_r, piv_r,
        inputs=True,
    )
    m_core, u_core = swap(pack_m, "leaf", 1), swap(pack_u, "leaf", 1)
    *sums, pack_m = together(*sums, pack_m)
    m_prev, m_next = shift(pack_m, 1), shift(pack_m, -1)
    out, z_l, zp_l, k_l = run(
        leaf_up_kernel,
        [(64 * HOLD, LANES), row, row, (TILE, TILE)],
        *sums, y_l, plan, rows, hold,
    )
    m_prev, m_next = after(out, m_prev, m_next)
    m_low, m_high, out = together(m_prev[:MISC], m_next[MISC:], out)
    m_low, m_high = shift(m_low, 1), shift(m_high, -1)
    got_m = route_leaf(out)
    m_prev_core, m_next_core = swap(m_prev, "leaf", 1), swap(m_next, "leaf", 1)
    m_low, m_high, pack_u = after(got_m, m_low, m_high, pack_u)
    u_prev, u_next = shift(pack_u, 1), shift(pack_u, -1)
    held_m = (
        pack_m, m_prev, m_next, m_low, m_high,
        m_core, m_prev_core, m_next_core, swap(m_low, "leaf", 1), swap(m_high, "leaf", 1),
    )

    part, y_m, upd_m = run(
        enter_middle_kernel, [(8 * RHS, TILE), flat, high], *held_m, got_m,
        copied=VAT - SRC,
    )
    red = between(part, 8)
    u_prev, u_next = after(red, u_prev, u_next)
    u_low, u_high = shift(u_prev[:END], 1), shift(u_next[END:], -1)
    u_prev_core, u_next_core = swap(u_prev, "leaf", 1), swap(u_next, "leaf", 1)
    part, z_m, zp_m = run(
        middle_kernel, [(8 * 3 * RHS, TILE), flat, row], *held_m, red, y_m, rows,
        copied=END - VAT,
    )
    u_low, u_high = after(part, u_low, u_high)
    held_u = (
        pack_u, u_prev, u_next, u_low, u_high,
        u_core, u_prev_core, u_next_core, swap(u_low, "leaf", 1), swap(u_high, "leaf", 1),
    )
    red = between(part, 8)
    k_u, k_r = run(cross_kernel, [(TILE, TILE)] * 2, *held_u, red)
    out, k_m = run(
        middle_up_kernel, [(16 * 2 * RHS, LANES), pair],
        *held_m, red, upd_m, rows, k_u, scratch=[(LANES, 128)], copied=PAT - MISC,
    )
    got_u = between(out, 16)

    part, y_u, upd_u = run(
        enter_upper_kernel, [(16 * 3 * RHS, TILE), flat, high], *held_u, got_u
    )
    red = between(part, 16)
    out, z_u, zp_u, k_u = run(
        upper_up_kernel, [(32 * 2 * RHS, LANES), flat, row, (TILE, TILE)],
        *held_u, red, y_u, upd_u, rows, k_r, scratch=[(LANES, 256)],
    )
    got_r = between(out, 32)

    part, y_r = run(enter_root_kernel, [(32 * 3 * RHS, TILE), flat], *held_u, got_r)
    red = between(part, 32)
    x_r, out = run(
        root_kernel, [row, (256, LANES)], *held_u, red, y_r, rows, got_r, answer=True
    )

    back = between(out, 32)
    part, xu = run(
        functools.partial(fetch_kernel, 15, END), [(16 * 2 * RHS, TILE), high],
        *held_u, back, zp_u, scratch=[(LANES, 256)],
    )
    red = between(part, 16)
    x_u, out = run(
        down_upper_kernel, [row, (128, LANES)],
        *held_u, red, z_u, rows, xu, got_u, k_u, answer=True,
    )

    back = between(out, 16)
    part, xu = run(
        functools.partial(fetch_kernel, 14, MISC), [(8 * 4 * RHS, TILE), high],
        *held_m, back, zp_m, k_m, scratch=[(LANES, 128)],
    )
    red = between(part, 8)
    x_m, out = run(
        down_middle_kernel, [row, (64, LANES)],
        *held_m, red, z_m, rows, xu, got_m, answer=True,
    )

    back = between(out, 8)
    part = run(fetch_leaf_kernel, [pair], back, plan, hold, zp_l)
    x_l = run(leaf_kernel, [row], *four(part, "grid", 1), z_l, k_l, hold, rows, answer=True)
    return (x_l, x_m, x_u, x_r)


def solution(mesh):
    both = ("leaf", "grid")
    wide = P(None, both)
    deep = P(both, None)
    line = P(both)
    level = (wide, deep, deep, deep, line, deep, P(), line)
    in_specs = level * 3 + (wide, deep, deep, deep, line, P())
    return jax.shard_map(
        shards, mesh=mesh, in_specs=in_specs, out_specs=(wide,) * 4, check_vma=False
    )
```

time: 268 us -> 237 us (0.88)
  Pallas kernels: 54.9 us -> 27.7 us
  starting transfers between devices: 43 us -> 35.1 us
    pallas_call x17, Pallas kernels: 54.9 us -> 27.7 us  [run(): pl.pallas_call(kernel, out_shape=outs[0] if len(outs) == 1 else outs, scr...]
    ppermute x8, waiting for transfers between devices: 7.87 us -> 14.6 us  [shift(): lax.ppermute(value, 'grid', [(s, (s + step) % size) for s in range(size)])]
    all_to_all x2 -> x1, starting transfers between devices: 9.39 us -> 3.36 us  [between(): lax.all_to_all(value, 'leaf', split_axis=0, concat_axis=0, tiled=True, ax...]
    all_to_all x1, waiting for transfers between devices: 8.72 us -> 3.39 us  [route_leaf(): lax.all_to_all(value, ('leaf', 'grid'), split_axis=0, concat_axis=0, tile...]
    ppermute x14 -> x16, waiting for transfers between devices: 6.19 us -> 8.89 us  [swap(): return lax.ppermute(value, axis, pairs)]
    all_to_all x2 -> x1, waiting for transfers between devices: 11.4 us -> 8.77 us  [between(): lax.all_to_all(value, 'leaf', split_axis=0, concat_axis=0, tiled=True, ax...]
    all_to_all x9 -> x10, blocking collectives: 126 us -> 128 us  [between(): lax.all_to_all(value, 'leaf', split_axis=0, concat_axis=0, tiled=True, ax...]
    unnamed x47 -> x79, local copies, waits for them, and re-layouts: 4.96 us -> 7.49 us
  transfers between devices with their start and end apart: 25 -> 26, of which waited for: 11 -> 15; matrix products, arithmetic and copies ran while one was open for 2% -> 0% of each run, Pallas kernels for 6% -> 3%
where the time goes in v2:
time: 237 us; the launch traced here: 236 us
  blocking collectives  128 us (54%)
  waiting for transfers between devices  35.6 us (15%)
  starting transfers between devices  35.1 us (15%)
  Pallas kernels  27.7 us (12%)
  local copies, waits for them, and re-layouts  8.2 us (3%)
    all_to_all x10, blocking collectives, between(): lax.all_to_all(value, 'leaf', split_axis=0, concat_axis=0, tiled=True, ax...  128 us
    pallas_call x17, Pallas kernels, run(): pl.pallas_call(kernel, out_shape=outs[0] if len(outs) == 1 else outs, scr...  27.7 us
    ppermute x8, waiting for transfers between devices, shift(): lax.ppermute(value, 'grid', [(s, (s + step) % size) for s in range(size)])  14.6 us
    all_to_all x1, starting transfers between devices, route_leaf(): lax.all_to_all(value, ('leaf', 'grid'), split_axis=0, concat_axis=0, tile...  12 us
    ppermute x16, starting transfers between devices, swap(): return lax.ppermute(value, axis, pairs)  11.2 us
    ppermute x16, waiting for transfers between devices, swap(): return lax.ppermute(value, axis, pairs)  8.89 us
    all_to_all x1, waiting for transfers between devices, between(): lax.all_to_all(value, 'leaf', split_axis=0, concat_axis=0, tiled=True, ax...  8.77 us
    ppermute x8, starting transfers between devices, shift(): lax.ppermute(value, 'grid', [(s, (s + step) % size) for s in range(size)])  8.53 us
  transfers between devices with their start and end apart: 26, of which 15 were waited for; matrix products, arithmetic and copies ran while one was open for 0% of the time, Pallas kernels for 3%

profile of v2, /device:TPU:2, one launch (start us, length us, event | category | flops | bytes accessed | tf_op | source)
XLA Modules:
  0.0 236.0 jit_solution(1796145529438377274)
XLA Ops:
  0.6 1.3 copy.34
  2.0 0.7 copy-done.38
  2.6 0.6 copy.35.ranks_r
  3.3 1.5 leaf_start_kernel.1
  4.7 1.6 collective-permute-start.2
  6.3 2.8 %collective-permute-start.1 = (f32[144,128]{1,0:T(8,128)S(1)}, f32[144,128]{1,0:T(8,128)S(1)}, u32[]{:S(2)}, u32[]{:S(2)}) collective-permute-start(f32[144,128]{1,0:T(8,128)S(1)} %get-tuple-element.64.s0), channel_id=1, source_target_pairs={{0,2},{1,3},{2,0},{3,1},{4,6},{5,7},{6,4},{7,5},{8,10},{9,11},{10,... | collective-permute-start | bytes 221192 | tf_op jit(solution)/shard_map/ppermute | solution.py:608
  9.1 1.3 pack_kernel.1
  10.5 2.0 collective-permute-done.1.s2
  12.5 1.0 collective-permute-done.s1
  13.5 0.8 collective-permute-start.4
  14.3 1.2 collective-permute-start.3
  15.5 1.2 leaf_up_kernel.1
  16.8 3.9 %collective-permute-done.4.refs_2_ = f32[656,128]{1,0:T(8,128)S(1)} collective-permute-done((f32[656,128]{1,0:T(8,128)S(1)}, f32[656,128]{1,0:T(8,128)S(1)}, u32[]{:S(2)}, u32[]{:S(2)}) %collective-permute-start.4) | collective-permute-done | bytes 335904 | tf_op jit(solution)/shard_map/ppermute | solution.py:613
  20.7 1.3 collective-permute-done.3.refs_1_
  22.0 12.0 %all-to-all-start = ((f32[64,8,128]{2,1,0:T(8,128)}), f32[64,8,128]{2,1,0:T(8,128)S(1)}, u32[]{:S(2)}, u32[]{:S(2)}) async-start(f32[64,8,128]{2,1,0:T(8,128)} %bitcast.11), calls=%async_computation | async-start | bytes 524288 | tf_op jit(solution)/shard_map/all_to_all | solution.py:643
  34.0 1.5 collective-permute-start.5
  35.6 0.6 collective-permute-start.6
  36.1 6.3 %collective-permute-done.6.refs_4_ = f32[264,128]{1,0:T(8,128)S(1)} collective-permute-done((f32[264,128]{1,0:T(8,128)S(1)}, f32[264,128]{1,0:T(8,128)S(1)}, u32[]{:S(2)}, u32[]{:S(2)}) %collective-permute-start.6) | collective-permute-done | bytes 135200 | tf_op jit(solution)/shard_map/ppermute | solution.py:613
  42.5 0.9 collective-permute-done.5.refs_3_
  43.3 3.4 %all-to-all-done = f32[64,8,128]{2,1,0:T(8,128)S(1)} async-done(((f32[64,8,128]{2,1,0:T(8,128)}), f32[64,8,128]{2,1,0:T(8,128)S(1)}, u32[]{:S(2)}, u32[]{:S(2)}) %all-to-all-start) | async-done | bytes 262176 | tf_op jit(solution)/shard_map/all_to_all | solution.py:643
  46.7 0.7 copy-done.22
  47.4 1.6 collective-permute-start.13
  50.1 1.0 collective-permute-done.8.refs_6_
  51.6 0.9 collective-permute-done.11.refs_9_
  52.5 0.6 copy-done.20
  53.1 0.7 copy-done.14
  53.8 0.9 copy-done.23
  54.8 2.0 enter_middle_kernel.1
  56.8 11.2 %all_to_all.132 = f32[8,8,128]{2,1,0:T(8,128)S(1)} all-to-all(f32[8,8,128]{2,1,0:T(8,128)S(1)} %bitcast.61), channel_id=1, replica_groups={{0,8,16,24,32,40,48,56},{4,12,20,28,36,44,52,60},{64,72,80,88,96,104,11..., dimensions={0} | all-to-all | bytes 65536 | tf_op jit(solution)/shard_map/all_to_all | solution.py:635
  68.1 1.2 collective-permute-start.14
  69.3 1.2 collective-permute-start.15
  70.5 0.5 collective-permute-start.17
  71.0 2.3 middle_kernel.1
  73.3 0.6 copy-done.25
  73.9 0.6 copy-done.28
  74.5 0.6 copy-done.36
  75.1 0.5 collective-permute-done.15.refs_4_
  75.7 1.6 collective-permute-done.14.refs_3_
  77.8 3.4 %all-to-all-start.2 = ((f32[8,24,128]{2,1,0:T(8,128)}), f32[8,24,128]{2,1,0:T(8,128)S(1)}, u32[]{:S(2)}, u32[]{:S(2)}) async-start(f32[8,24,128]{2,1,0:T(8,128)} %bitcast.58), calls=%async_computation.2 | async-start | bytes 196608 | tf_op jit(solution)/shard_map/all_to_all | solution.py:635
  81.2 8.8 %all-to-all-done.2 = f32[8,24,128]{2,1,0:T(8,128)S(1)} async-done(((f32[8,24,128]{2,1,0:T(8,128)}), f32[8,24,128]{2,1,0:T(8,128)S(1)}, u32[]{:S(2)}, u32[]{:S(2)}) %all-to-all-start.2) | async-done | bytes 98336 | tf_op jit(solution)/shard_map/all_to_all | solution.py:635
  90.0 1.9 cross_kernel.1
  91.9 1.8 middle_up_kernel.1
  93.7 11.3 %all_to_all.133 = f32[16,16,128]{2,1,0:T(8,128)S(1)} all-to-all(f32[16,16,128]{2,1,0:T(8,128)S(1)} %bitcast.54), channel_id=1, replica_groups={{0,8,16,24,32,40,48,56,64,72,80,88,96,104,112,120},{4,12,20,28,36,44,52..., dimensions={0} | all-to-all | bytes 262144 | tf_op jit(solution)/shard_map/all_to_all | solution.py:635
  105.0 2.1 enter_upper_kernel.1
  107.1 11.8 %all_to_all.134 = f32[16,24,128]{2,1,0:T(8,128)S(1)} all-to-all(f32[16,24,128]{2,1,0:T(8,128)S(1)} %bitcast.51), channel_id=1, replica_groups={{0,8,16,24,32,40,48,56,64,72,80,88,96,104,112,120},{4,12,20,28,36,44,52..., dimensions={0} | all-to-all | bytes 393216 | tf_op jit(solution)/shard_map/all_to_all | solution.py:635
  119.0 2.0 upper_up_kernel.1
  121.0 17.1 %all_to_all.135 = f32[32,16,128]{2,1,0:T(8,128)S(1)} all-to-all(f32[32,16,128]{2,1,0:T(8,128)S(1)} %bitcast.50), channel_id=1, replica_groups={{0,8,16,24,32,40,48,56,64,72,80,88,96,104,112,120,128,136,144,152,160,1..., dimensions={0} | all-to-all | bytes 524288 | tf_op jit(solution)/shard_map/all_to_all | solution.py:635
  138.0 1.9 enter_root_kernel.1
  140.0 15.9 %all_to_all.136 = f32[32,24,128]{2,1,0:T(8,128)S(1)} all-to-all(f32[32,24,128]{2,1,0:T(8,128)S(1)} %bitcast.48), channel_id=1, replica_groups={{0,8,16,24,32,40,48,56,64,72,80,88,96,104,112,120,128,136,144,152,160,1..., dimensions={0} | all-to-all | bytes 786432 | tf_op jit(solution)/shard_map/all_to_all | solution.py:635
  155.9 2.5 %root_kernel.1 = (f32[8,128]{1,0:T(8,128)}, f32[256,128]{1,0:T(8,128)S(1)}) custom-call(f32[1056,128]{1,0:T(8,128)S(1)} %get-tuple-element.81.refs_0_, f32[1056,128]{1,0:T(8,128)S(1)} %collective-permute-done.12.refs_1_, f32[1056,128]{1,0:T(8,128)S(1)} %collective-permute-done.13.refs_2_, f32[656,128]{1,0:T(8,128)} %collective-permute-done.14.refs_3_, ...), custom_call_target="tpu_custom_call" | custom-call | tf_op jit(solution)/shard_map/root_kernel/pallas_call | solution.py:592
  158.3 15.5 %all_to_all.137 = f32[32,8,128]{2,1,0:T(8,128)S(1)} all-to-all(f32[32,8,128]{2,1,0:T(8,128)S(1)} %bitcast.55), channel_id=1, replica_groups={{0,8,16,24,32,40,48,56,64,72,80,88,96,104,112,120,128,136,144,152,160,1..., dimensions={0} | all-to-all | bytes 262144 | tf_op jit(solution)/shard_map/all_to_all | solution.py:635
  173.9 1.6 fetch_kernel.2
  175.4 11.2 %all_to_all.138 = f32[16,16,128]{2,1,0:T(8,128)S(1)} all-to-all(f32[16,16,128]{2,1,0:T(8,128)S(1)} %bitcast.57), channel_id=1, replica_groups={{0,8,16,24,32,40,48,56,64,72,80,88,96,104,112,120},{4,12,20,28,36,44,52..., dimensions={0} | all-to-all | bytes 262144 | tf_op jit(solution)/shard_map/all_to_all | solution.py:635
  186.7 2.6 %down_upper_kernel.1 = (f32[8,128]{1,0:T(8,128)}, f32[128,128]{1,0:T(8,128)S(1)}) custom-call(f32[1056,128]{1,0:T(8,128)S(1)} %get-tuple-element.81.refs_0_, f32[1056,128]{1,0:T(8,128)S(1)} %collective-permute-done.12.refs_1_, f32[1056,128]{1,0:T(8,128)S(1)} %collective-permute-done.13.refs_2_, f32[656,128]{1,0:T(8,128)} %collective-permute-done.14.refs_3_, ...), custom_call_target="tpu_custom_call" | custom-call | tf_op jit(solution)/shard_map/down_upper_kernel/pallas_call | solution.py:592
  189.3 11.8 %all_to_all.139 = f32[16,8,128]{2,1,0:T(8,128)S(1)} all-to-all(f32[16,8,128]{2,1,0:T(8,128)S(1)} %bitcast.59), channel_id=1, replica_groups={{0,8,16,24,32,40,48,56,64,72,80,88,96,104,112,120},{4,12,20,28,36,44,52..., dimensions={0} | all-to-all | bytes 131072 | tf_op jit(solution)/shard_map/all_to_all | solution.py:635
  201.2 0.6 copy-done.37
  202.2 11.9 %all_to_all.140 = f32[8,32,128]{2,1,0:T(8,128)S(1)} all-to-all(f32[8,32,128]{2,1,0:T(8,128)S(1)} %bitcast.56), channel_id=1, replica_groups={{0,8,16,24,32,40,48,56},{4,12,20,28,36,44,52,60},{64,72,80,88,96,104,11..., dimensions={0} | all-to-all | bytes 262144 | tf_op jit(solution)/shard_map/all_to_all | solution.py:635
  214.2 1.3 down_middle_kernel.1
  215.5 10.5 %all_to_all.141 = f32[8,8,128]{2,1,0:T(8,128)S(1)} all-to-all(f32[8,8,128]{2,1,0:T(8,128)S(1)} %bitcast.60), channel_id=1, replica_groups={{0,8,16,24,32,40,48,56},{4,12,20,28,36,44,52,60},{64,72,80,88,96,104,11..., dimensions={0} | all-to-all | bytes 65536 | tf_op jit(solution)/shard_map/all_to_all | solution.py:635
  226.3 0.7 collective-permute-start.23
  227.1 4.3 %collective-permute-start.22 = (f32[16,128]{1,0:T(8,128)S(1)}, f32[16,128]{1,0:T(8,128)S(1)}, u32[]{:S(2)}, u32[]{:S(2)}) collective-permute-start(f32[16,128]{1,0:T(8,128)S(1)} %fetch_leaf_kernel.1.s0), channel_id=1, source_target_pairs={{0,2},{1,3},{2,0},{3,1},{4,6},{5,7},{6,4},{7,5},{8,10},{9,11},{10,... | collective-permute-start | bytes 24584 | tf_op jit(solution)/shard_map/ppermute | solution.py:608
  231.4 1.6 collective-permute-done.22.s2
  233.0 2.0 collective-permute-done.21.s1
  235.0 0.9 leaf_kernel.1
  (99 shorter events, 3.0 us)
Async XLA Ops:
  2.0 0.7 copy-start.38
  4.7 10.8 %copy-start.16 = (f32[768,128]{1,0:T(8,128)}, f32[768,128]{1,0:T(8,128)S(1)}, u32[]{:S(2)}) copy-start(f32[768,128]{1,0:T(8,128)S(1)} %get-tuple-element.71.hold) | copy-start | bytes 1179652
  4.7 10.8 %copy-start.32 = (f32[8,256]{1,0:T(8,128)}, f32[8,256]{1,0:T(8,128)S(1)}, u32[]{:S(2)}) copy-start(f32[8,256]{1,0:T(8,128)S(1)} %get-tuple-element.69.plan) | copy-start | bytes 24580
  4.7 5.8 %collective-permute-start.2 = (f32[144,128]{1,0:T(8,128)S(1)}, f32[144,128]{1,0:T(8,128)S(1)}, u32[]{:S(2)}, u32[]{:S(2)}) collective-permute-start(f32[144,128]{1,0:T(8,128)S(1)} %get-tuple-element.64.s0), channel_id=1, source_target_pairs={{0,3},{1,2},{2,1},{3,0},{4,7},{5,6},{6,5},{7,4},{8,11},{9,10},{10,... | collective-permute-start | bytes 221192 | tf_op jit(solution)/shard_map/ppermute | solution.py:608
  6.3 6.1 %collective-permute-start.1 = (f32[144,128]{1,0:T(8,128)S(1)}, f32[144,128]{1,0:T(8,128)S(1)}, u32[]{:S(2)}, u32[]{:S(2)}) collective-permute-start(f32[144,128]{1,0:T(8,128)S(1)} %get-tuple-element.64.s0), channel_id=1, source_target_pairs={{0,2},{1,3},{2,0},{3,1},{4,6},{5,7},{6,4},{7,5},{8,10},{9,11},{10,... | collective-permute-start | bytes 221192 | tf_op jit(solution)/shard_map/ppermute | solution.py:608
  9.1 4.4 %collective-permute-start = (f32[144,128]{1,0:T(8,128)S(1)}, f32[144,128]{1,0:T(8,128)S(1)}, u32[]{:S(2)}, u32[]{:S(2)}) collective-permute-start(f32[144,128]{1,0:T(8,128)S(1)} %get-tuple-element.64.s0), channel_id=1, source_target_pairs={{0,1},{1,0},{2,3},{3,2},{4,5},{5,4},{6,7},{7,6},{8,9},{9,8},{10,11... | collective-permute-start | bytes 221192 | tf_op jit(solution)/shard_map/ppermute | solution.py:608
  10.5 25.6 %copy-start.4 = (f32[656,128]{1,0:T(8,128)}, f32[656,128]{1,0:T(8,128)S(1)}, u32[]{:S(2)}) copy-start(f32[656,128]{1,0:T(8,128)S(1)} %get-tuple-element.63.refs_0_) | copy-start | bytes 1007620
  13.5 7.2 %collective-permute-start.4 = (f32[656,128]{1,0:T(8,128)S(1)}, f32[656,128]{1,0:T(8,128)S(1)}, u32[]{:S(2)}, u32[]{:S(2)}) collective-permute-start(f32[656,128]{1,0:T(8,128)S(1)} %get-tuple-element.63.refs_0_), channel_id=1, source_target_pairs={{0,3},{1,0},{2,1},{3,2},{4,7},{5,4},{6,5},{7,6},{8,11},{9,8},{10,9... | collective-permute-start | bytes 1007624 | tf_op jit(solution)/shard_map/ppermute | solution.py:613
  14.3 7.7 %collective-permute-start.3 = (f32[656,128]{1,0:T(8,128)S(1)}, f32[656,128]{1,0:T(8,128)S(1)}, u32[]{:S(2)}, u32[]{:S(2)}) collective-permute-start(f32[656,128]{1,0:T(8,128)S(1)} %get-tuple-element.63.refs_0_), channel_id=1, source_target_pairs={{0,1},{1,2},{2,3},{3,0},{4,5},{5,6},{6,7},{7,4},{8,9},{9,10},{10,1... | collective-permute-start | bytes 1007624 | tf_op jit(solution)/shard_map/ppermute | solution.py:613
  16.8 5.2 %copy-start.26 = (f32[128,128]{1,0:T(8,128)}, f32[128,128]{1,0:T(8,128)S(1)}, u32[]{:S(2)}) copy-start(f32[128,128]{1,0:T(8,128)S(1)} %get-tuple-element.114.k1) | copy-start | bytes 196612
  16.8 5.2 %copy-start.34 = (f32[8,128]{1,0:T(8,128)}, f32[8,128]{1,0:T(8,128)S(1)}, u32[]{:S(2)}) copy-start(f32[8,128]{1,0:T(8,128)S(1)} %get-tuple-element.112.zp) | copy-start | bytes 12292
  20.7 28.8 %copy-start.2 = (f32[656,128]{1,0:T(8,128)}, f32[656,128]{1,0:T(8,128)S(1)}, u32[]{:S(2)}) copy-start(f32[656,128]{1,0:T(8,128)S(1)} %collective-permute-done.4.refs_2_) | copy-start | bytes 1007620
  22.0 27.5 %copy-start = (f32[656,128]{1,0:T(8,128)}, f32[656,128]{1,0:T(8,128)S(1)}, u32[]{:S(2)}) copy-start(f32[656,128]{1,0:T(8,128)S(1)} %collective-permute-done.3.refs_1_) | copy-start | bytes 1007620
  22.0 24.7 %all-to-all-start = ((f32[64,8,128]{2,1,0:T(8,128)}), f32[64,8,128]{2,1,0:T(8,128)S(1)}, u32[]{:S(2)}, u32[]{:S(2)}) async-start(f32[64,8,128]{2,1,0:T(8,128)} %bitcast.11), calls=%async_computation | async-start | bytes 524288 | tf_op jit(solution)/shard_map/all_to_all | solution.py:643
  34.0 9.3 %collective-permute-start.5 = (f32[392,128]{1,0:T(8,128)S(1)}, f32[392,128]{1,0:T(8,128)S(1)}, u32[]{:S(2)}, u32[]{:S(2)}) collective-permute-start(f32[392,128]{1,0:T(8,128)S(1)} %slice.12), channel_id=1, source_target_pairs={{0,1},{1,2},{2,3},{3,0},{4,5},{5,6},{6,7},{7,4},{8,9},{9,10},{10,1... | collective-permute-start | bytes 602120 | tf_op jit(solution)/shard_map/ppermute | solution.py:613
  35.6 6.9 %collective-permute-start.6 = (f32[264,128]{1,0:T(8,128)S(1)}, f32[264,128]{1,0:T(8,128)S(1)}, u32[]{:S(2)}, u32[]{:S(2)}) collective-permute-start(f32[264,128]{1,0:T(8,128)S(1)} %slice.13), channel_id=1, source_target_pairs={{0,3},{1,0},{2,1},{3,2},{4,7},{5,4},{6,5},{7,6},{8,11},{9,8},{10,9... | collective-permute-start | bytes 405512 | tf_op jit(solution)/shard_map/ppermute | solution.py:613
  36.1 13.9 %collective-permute-start.7 = (f32[656,128]{1,0:T(8,128)S(1)}, f32[656,128]{1,0:T(8,128)S(1)}, u32[]{:S(2)}, u32[]{:S(2)}) collective-permute-start(f32[656,128]{1,0:T(8,128)S(1)} %get-tuple-element.63.refs_0_), channel_id=1, source_target_pairs={{0,4},{4,0},{8,12},{12,8},{16,20},{20,16},{24,28},{28,24},{32,36},... | collective-permute-start | bytes 1007624 | tf_op jit(solution)/shard_map/ppermute | solution.py:608
  42.5 10.0 %copy-start.18 = (f32[264,128]{1,0:T(8,128)}, f32[264,128]{1,0:T(8,128)S(1)}, u32[]{:S(2)}) copy-start(f32[264,128]{1,0:T(8,128)S(1)} %collective-permute-done.6.refs_4_) | copy-start | bytes 405508
  43.3 9.1 %copy-start.12 = (f32[392,128]{1,0:T(8,128)}, f32[392,128]{1,0:T(8,128)S(1)}, u32[]{:S(2)}) copy-start(f32[392,128]{1,0:T(8,128)S(1)} %collective-permute-done.5.refs_3_) | copy-start | bytes 602116
  46.7 0.7 copy-start.22
  47.4 20.6 %collective-permute-start.13 = (f32[1056,128]{1,0:T(8,128)S(1)}, f32[1056,128]{1,0:T(8,128)S(1)}, u32[]{:S(2)}, u32[]{:S(2)}) collective-permute-start(f32[1056,128]{1,0:T(8,128)S(1)} %get-tuple-element.81.refs_0_), channel_id=1, source_target_pairs={{0,3},{1,0},{2,1},{3,2},{4,7},{5,4},{6,5},{7,6},{8,11},{9,8},{10,9... | collective-permute-start | bytes 1622024 | tf_op jit(solution)/shard_map/ppermute | solution.py:613
  49.0 19.1 %collective-permute-start.12 = (f32[1056,128]{1,0:T(8,128)S(1)}, f32[1056,128]{1,0:T(8,128)S(1)}, u32[]{:S(2)}, u32[]{:S(2)}) collective-permute-start(f32[1056,128]{1,0:T(8,128)S(1)} %get-tuple-element.81.refs_0_), channel_id=1, source_target_pairs={{0,1},{1,2},{2,3},{3,0},{4,5},{5,6},{6,7},{7,4},{8,9},{9,10},{10,1... | collective-permute-start | bytes 1622024 | tf_op jit(solution)/shard_map/ppermute | solution.py:613
  49.5 1.6 collective-permute-start.8
  49.5 2.1 collective-permute-start.9
  50.0 2.5 %copy-start.6 = (f32[656,128]{1,0:T(8,128)}, f32[656,128]{1,0:T(8,128)S(1)}, u32[]{:S(2)}) copy-start(f32[656,128]{1,0:T(8,128)S(1)} %collective-permute-done.7.refs_5_) | copy-start | bytes 1007620
  50.0 2.5 %collective-permute-start.10 = (f32[392,128]{1,0:T(8,128)S(1)}, f32[392,128]{1,0:T(8,128)S(1)}, u32[]{:S(2)}, u32[]{:S(2)}) collective-permute-start(f32[392,128]{1,0:T(8,128)S(1)} %collective-permute-done.5.refs_3_), channel_id=1, source_target_pairs={{0,4},{4,0},{8,12},{12,8},{16,20},{20,16},{24,28},{28,24},{32,36},... | collective-permute-start | bytes 602120 | tf_op jit(solution)/shard_map/ppermute | solution.py:608
  51.1 1.4 copy-start.8
  51.1 1.4 collective-permute-start.11
  51.6 0.9 copy-start.10
  52.5 0.7 copy-start.20
  53.1 0.7 copy-start.14
  53.8 0.9 copy-start.23
  56.8 11.3 %copy-start.30 = (f32[64,128]{1,0:T(8,128)}, f32[64,128]{1,0:T(8,128)S(1)}, u32[]{:S(2)}) copy-start(f32[64,128]{1,0:T(8,128)S(1)} %get-tuple-element.89.refs_11_) | copy-start | bytes 98308
  68.1 9.2 %collective-permute-start.14 = (f32[656,128]{1,0:T(8,128)S(1)}, f32[656,128]{1,0:T(8,128)}, u32[]{:S(2)}, u32[]{:S(2)}) collective-permute-start(f32[656,128]{1,0:T(8,128)S(1)} %slice.14), channel_id=1, source_target_pairs={{0,1},{1,2},{2,3},{3,0},{4,5},{5,6},{6,7},{7,4},{8,9},{9,10},{10,1... | collective-permute-start | bytes 1007624 | tf_op jit(solution)/shard_map/ppermute | solution.py:613
  69.3 6.3 %collective-permute-start.15 = (f32[400,128]{1,0:T(8,128)S(1)}, f32[400,128]{1,0:T(8,128)S(1)}, u32[]{:S(2)}, u32[]{:S(2)}) collective-permute-start(f32[400,128]{1,0:T(8,128)S(1)} %slice.15), channel_id=1, source_target_pairs={{0,3},{1,0},{2,1},{3,2},{4,7},{5,4},{6,5},{7,6},{8,11},{9,8},{10,9... | collective-permute-start | bytes 614408 | tf_op jit(solution)/shard_map/ppermute | solution.py:613
  70.5 10.7 %collective-permute-start.16 = (f32[1056,128]{1,0:T(8,128)S(1)}, f32[1056,128]{1,0:T(8,128)S(1)}, u32[]{:S(2)}, u32[]{:S(2)}) collective-permute-start(f32[1056,128]{1,0:T(8,128)S(1)} %get-tuple-element.81.refs_0_), channel_id=1, source_target_pairs={{0,4},{4,0},{8,12},{12,8},{16,20},{20,16},{24,28},{28,24},{32,36},... | collective-permute-start | bytes 1622024 | tf_op jit(solution)/shard_map/ppermute | solution.py:608
  70.5 19.5 %collective-permute-start.17 = (f32[1056,128]{1,0:T(8,128)S(1)}, f32[1056,128]{1,0:T(8,128)S(1)}, u32[]{:S(2)}, u32[]{:S(2)}) collective-permute-start(f32[1056,128]{1,0:T(8,128)S(1)} %collective-permute-done.12.refs_1_), channel_id=1, source_target_pairs={{0,4},{4,0},{8,12},{12,8},{16,20},{20,16},{24,28},{28,24},{32,36},... | collective-permute-start | bytes 1622024 | tf_op jit(solution)/shard_map/ppermute | solution.py:608
  71.0 19.0 %collective-permute-start.18 = (f32[1056,128]{1,0:T(8,128)S(1)}, f32[1056,128]{1,0:T(8,128)S(1)}, u32[]{:S(2)}, u32[]{:S(2)}) collective-permute-start(f32[1056,128]{1,0:T(8,128)S(1)} %collective-permute-done.13.refs_2_), channel_id=1, source_target_pairs={{0,4},{4,0},{8,12},{12,8},{16,20},{20,16},{24,28},{28,24},{32,36},... | collective-permute-start | bytes 1622024 | tf_op jit(solution)/shard_map/ppermute | solution.py:608
  73.3 0.6 copy-start.25
  73.9 0.6 copy-start.28
  77.3 12.7 %collective-permute-start.19 = (f32[656,128]{1,0:T(8,128)}, f32[656,128]{1,0:T(8,128)}, u32[]{:S(2)}, u32[]{:S(2)}) collective-permute-start(f32[656,128]{1,0:T(8,128)} %collective-permute-done.14.refs_3_), channel_id=1, source_target_pairs={{0,4},{4,0},{8,12},{12,8},{16,20},{20,16},{24,28},{28,24},{32,36},... | collective-permute-start | bytes 1007624 | tf_op jit(solution)/shard_map/ppermute | solution.py:608
  77.3 12.7 %collective-permute-start.20 = (f32[400,128]{1,0:T(8,128)S(1)}, f32[400,128]{1,0:T(8,128)}, u32[]{:S(2)}, u32[]{:S(2)}) collective-permute-start(f32[400,128]{1,0:T(8,128)S(1)} %collective-permute-done.15.refs_4_), channel_id=1, source_target_pairs={{0,4},{4,0},{8,12},{12,8},{16,20},{20,16},{24,28},{28,24},{32,36},... | collective-permute-start | bytes 614408 | tf_op jit(solution)/shard_map/ppermute | solution.py:608
  77.8 12.1 %all-to-all-start.2 = ((f32[8,24,128]{2,1,0:T(8,128)}), f32[8,24,128]{2,1,0:T(8,128)S(1)}, u32[]{:S(2)}, u32[]{:S(2)}) async-start(f32[8,24,128]{2,1,0:T(8,128)} %bitcast.58), calls=%async_computation.2 | async-start | bytes 196608 | tf_op jit(solution)/shard_map/all_to_all | solution.py:635
  90.0 1.9 copy-start.31
  186.6 14.5 %copy-start.1 = (f32[656,128]{1,0:T(8,128)S(1)}, f32[656,128]{1,0:T(8,128)}, u32[]{:S(2)}) copy-start(f32[656,128]{1,0:T(8,128)} %copy-done) | copy-start | bytes 1007620
  186.6 14.5 %copy-start.3 = (f32[656,128]{1,0:T(8,128)S(1)}, f32[656,128]{1,0:T(8,128)}, u32[]{:S(2)}) copy-start(f32[656,128]{1,0:T(8,128)} %copy-done.2) | copy-start | bytes 1007620
  186.6 14.5 %copy-start.5 = (f32[656,128]{1,0:T(8,128)S(1)}, f32[656,128]{1,0:T(8,128)}, u32[]{:S(2)}) copy-start(f32[656,128]{1,0:T(8,128)} %copy-done.4) | copy-start | bytes 1007620
  186.6 14.5 %copy-start.7 = (f32[656,128]{1,0:T(8,128)S(1)}, f32[656,128]{1,0:T(8,128)}, u32[]{:S(2)}) copy-start(f32[656,128]{1,0:T(8,128)} %copy-done.6) | copy-start | bytes 1007620
  186.6 14.5 %copy-start.9 = (f32[656,128]{1,0:T(8,128)S(1)}, f32[656,128]{1,0:T(8,128)}, u32[]{:S(2)}) copy-start(f32[656,128]{1,0:T(8,128)} %copy-done.8) | copy-start | bytes 1007620
  186.7 14.5 %copy-start.11 = (f32[656,128]{1,0:T(8,128)S(1)}, f32[656,128]{1,0:T(8,128)}, u32[]{:S(2)}) copy-start(f32[656,128]{1,0:T(8,128)} %copy-done.10) | copy-start | bytes 1007620
  186.7 14.5 %copy-start.13 = (f32[392,128]{1,0:T(8,128)S(1)}, f32[392,128]{1,0:T(8,128)}, u32[]{:S(2)}) copy-start(f32[392,128]{1,0:T(8,128)} %copy-done.12) | copy-start | bytes 602116
  186.7 14.5 %copy-start.15 = (f32[392,128]{1,0:T(8,128)S(1)}, f32[392,128]{1,0:T(8,128)}, u32[]{:S(2)}) copy-start(f32[392,128]{1,0:T(8,128)} %copy-done.14) | copy-start | bytes 602116
  186.7 14.5 %copy-start.21 = (f32[264,128]{1,0:T(8,128)S(1)}, f32[264,128]{1,0:T(8,128)}, u32[]{:S(2)}) copy-start(f32[264,128]{1,0:T(8,128)} %copy-done.20) | copy-start | bytes 405508
  189.3 11.9 %copy-start.19 = (f32[264,128]{1,0:T(8,128)S(1)}, f32[264,128]{1,0:T(8,128)}, u32[]{:S(2)}) copy-start(f32[264,128]{1,0:T(8,128)} %copy-done.18) | copy-start | bytes 405508
  201.1 0.7 copy-start.37
  201.8 12.3 %copy-start.29 = (f32[8,1024]{1,0:T(8,128)S(1)}, f32[8,1024]{1,0:T(8,128)}, u32[]{:S(2)}) copy-start(f32[8,1024]{1,0:T(8,128)} %copy-done.28) | copy-start | bytes 98308
  202.2 11.9 %copy-start.24 = (f32[64,8,128]{2,1,0:T(8,128)S(1)}, f32[64,8,128]{2,1,0:T(8,128)}, u32[]{:S(2)}) copy-start(f32[64,8,128]{2,1,0:T(8,128)} %copy-done.22) | copy-start | bytes 786436
  214.2 11.9 %copy-start.17 = (f32[768,128]{1,0:T(8,128)S(1)}, f32[768,128]{1,0:T(8,128)}, u32[]{:S(2)}) copy-start(f32[768,128]{1,0:T(8,128)} %copy-done.16) | copy-start | bytes 1179652
  214.2 11.9 %copy-start.33 = (f32[8,256]{1,0:T(8,128)S(1)}, f32[8,256]{1,0:T(8,128)}, u32[]{:S(2)}) copy-start(f32[8,256]{1,0:T(8,128)} %copy-done.32) | copy-start | bytes 24580
  215.5 10.5 %copy-start.35 = (f32[8,128]{1,0:T(8,128)S(1)}, f32[8,128]{1,0:T(8,128)}, u32[]{:S(2)}) copy-start(f32[8,128]{1,0:T(8,128)} %copy-done.34) | copy-start | bytes 12292
  226.0 9.0 %copy-start.27 = (f32[128,128]{1,0:T(8,128)S(1)}, f32[128,128]{1,0:T(8,128)}, u32[]{:S(2)}) copy-start(f32[128,128]{1,0:T(8,128)} %copy-done.26) | copy-start | bytes 196612
  226.3 5.0 %collective-permute-start.23 = (f32[16,128]{1,0:T(8,128)S(1)}, f32[16,128]{1,0:T(8,128)S(1)}, u32[]{:S(2)}, u32[]{:S(2)}) collective-permute-start(f32[16,128]{1,0:T(8,128)S(1)} %fetch_leaf_kernel.1.s0), channel_id=1, source_target_pairs={{0,3},{1,2},{2,1},{3,0},{4,7},{5,6},{6,5},{7,4},{8,11},{9,10},{10,... | collective-permute-start | bytes 24584 | tf_op jit(solution)/shard_map/ppermute | solution.py:608
  227.1 6.0 %collective-permute-start.22 = (f32[16,128]{1,0:T(8,128)S(1)}, f32[16,128]{1,0:T(8,128)S(1)}, u32[]{:S(2)}, u32[]{:S(2)}) collective-permute-start(f32[16,128]{1,0:T(8,128)S(1)} %fetch_leaf_kernel.1.s0), channel_id=1, source_target_pairs={{0,2},{1,3},{2,0},{3,1},{4,6},{5,7},{6,4},{7,5},{8,10},{9,11},{10,... | collective-permute-start | bytes 24584 | tf_op jit(solution)/shard_map/ppermute | solution.py:608
  231.4 3.7 %collective-permute-start.21 = (f32[16,128]{1,0:T(8,128)S(1)}, f32[16,128]{1,0:T(8,128)S(1)}, u32[]{:S(2)}, u32[]{:S(2)}) collective-permute-start(f32[16,128]{1,0:T(8,128)S(1)} %fetch_leaf_kernel.1.s0), channel_id=1, source_target_pairs={{0,1},{1,0},{2,3},{3,2},{4,5},{5,4},{6,7},{7,6},{8,9},{9,8},{10,11... | collective-permute-start | bytes 24584 | tf_op jit(solution)/shard_map/ppermute | solution.py:608
  (1 other events, 0.6 us)

commit v3 on v2

--- a/solution.py
+++ b/solution.py
@@ -7,6 +7,7 @@
 from jax.experimental.pallas import tpu as pltpu
 from jax.sharding import PartitionSpec as P
 
+
 RHS = 8
 LANES = 128
 TILE = 128
@@ -65,12 +66,14 @@
     return (raw(a_low, b_high, 0, 0) + raw(a_high, b_low, 0, 0)) + raw(a_high, b_high, 0, 0)
 
 
-def mask_rows(ranks_ref, groups):
+def mask_rows(ranks_ref, groups, fronts_dim):
     front = lax.axis_index("leaf") // groups
     both = ranks_ref[...].astype(F32)
-    own = iota(both.shape, 1) == front
-    pair = jnp.sum(jnp.where(own, both, 0.0), axis=1, keepdims=True)
+    own = iota(both.shape, fronts_dim) == front
+    pair = jnp.sum(jnp.where(own, both, 0.0), axis=fronts_dim, keepdims=True)
     lane = iota((1, TILE), 1).astype(F32)
+    if fronts_dim == 0:
+        return [(lane < pair[:, i : i + 1]).astype(F32) for i in range(2)]
     return [(lane < pair[i : i + 1, :]).astype(F32) for i in range(2)]
 
 
@@ -294,8 +297,10 @@
     plan[2:3, :] = leaf_slots(row_onehot(dest, 64))
     plan[3:8, :] = jnp.zeros((5, 2 * TILE), F32)
     found = []
-    for ranks, groups in ((ranks_l, 1), (ranks_m, 16), (ranks_u, 32), (ranks_r, 64)):
-        found += mask_rows(ranks, groups)
+    for ranks, groups, dim in (
+        (ranks_l, 1, 1), (ranks_m, 16, 1), (ranks_u, 32, 0), (ranks_r, 64, 0),
+    ):
+        found += mask_rows(ranks, groups, dim)
     rows[...] = jnp.concatenate(found[0:7] + [piv[...]], axis=0)
     hold[LW:LQ, :] = w[...]
     hold[LQ:LV, :] = q[:, 0:TILE]
@@ -333,7 +338,9 @@
 
 
 def cross_kernel(*refs):
-    _, k1, k2 = refs[HELD_REFS:]
+    _, k1, k2, low, high, low_core, high_core = refs[HELD_REFS:]
+    for source, kept in zip(refs[3:5] + refs[8:10], (low, high, low_core, high_core)):
+        kept[...] = source[...]
     upper = Held(refs, END)
     root = Held(refs, END, END)
     k1[...] = cross(upper.all(PAT), upper.all(VAT))
@@ -594,7 +601,6 @@
         out_shape=outs[0] if len(outs) == 1 else outs,
         scratch_shapes=scratch,
         compiler_params=None if inputs else pltpu.CompilerParams(vmem_limit_bytes=16 << 20),
-        name=getattr(kernel, "func", kernel).__name__,
         **options,
     )(*args)
 
@@ -615,10 +621,6 @@
 
 def four(value, axis, unit):
     return [value] + [swap(value, axis, unit * m) for m in (1, 2, 3)]
-
-
-def add_four(values):
-    return (values[0] + values[1]) + (values[2] + values[3])
 
 
 def together(*values):
@@ -656,7 +658,7 @@
     src_u, w_u, p_u, q_u, piv_u, c_u, ranks_u, t_u,
     src_r, w_r, p_r, q_r, piv_r, ranks_r,
 ):
-    ranks_l, ranks_m, ranks_u, ranks_r = (r.T for r in (ranks_l, ranks_m, ranks_u, ranks_r))
+    ranks_l, ranks_m = ranks_l.T, ranks_m.T
     t_l, t_m, t_u = (t.reshape(1, -1) for t in (t_l, t_m, t_u))
     piv_l, piv_m, piv_u, piv_r = (v.reshape(1, -1) for v in (piv_l, piv_m, piv_u, piv_r))
     row = (RHS, TILE)
@@ -680,18 +682,18 @@
     )
     m_core, u_core = swap(pack_m, "leaf", 1), swap(pack_u, "leaf", 1)
     *sums, pack_m = together(*sums, pack_m)
-    m_prev, m_next = shift(pack_m, 1), shift(pack_m, -1)
+    m_prev = shift(pack_m, 1)
+    m_next = shift(pack_m, -1)
     out, z_l, zp_l, k_l = run(
         leaf_up_kernel,
         [(64 * HOLD, LANES), row, row, (TILE, TILE)],
         *sums, y_l, plan, rows, hold,
     )
-    m_prev, m_next = after(out, m_prev, m_next)
-    m_low, m_high, out = together(m_prev[:MISC], m_next[MISC:], out)
-    m_low, m_high = shift(m_low, 1), shift(m_high, -1)
     got_m = route_leaf(out)
+    m_prev, m_next, pack_u = after(got_m, m_prev, m_next, pack_u)
+    m_low, m_high = shift(m_prev[:MISC], 1), shift(m_next[MISC:], -1)
     m_prev_core, m_next_core = swap(m_prev, "leaf", 1), swap(m_next, "leaf", 1)
-    m_low, m_high, pack_u = after(got_m, m_low, m_high, pack_u)
+    m_low, m_high, pack_u = together(m_low, m_high, pack_u)
     u_prev, u_next = shift(pack_u, 1), shift(pack_u, -1)
     held_m = (
         pack_m, m_prev, m_next, m_low, m_high,
@@ -716,7 +718,10 @@
         u_core, u_prev_core, u_next_core, swap(u_low, "leaf", 1), swap(u_high, "leaf", 1),
     )
     red = between(part, 8)
-    k_u, k_r = run(cross_kernel, [(TILE, TILE)] * 2, *held_u, red)
+    k_u, k_r, *opposite = run(
+        cross_kernel, [(TILE, TILE)] * 2 + [(END, TILE), (REND, TILE)] * 2, *held_u, red
+    )
+    held_u = (*held_u[:3], *opposite[:2], *held_u[5:8], *opposite[2:])
     out, k_m = run(
         middle_up_kernel, [(16 * 2 * RHS, LANES), pair],
         *held_m, red, upd_m, rows, k_u, scratch=[(LANES, 128)], copied=PAT - MISC,

time: 237 us -> 232 us (0.979)
  Pallas kernels: 27.7 us -> 21.5 us
  local copies, waits for them, and re-layouts: 8.2 us -> 2.7 us
  blocking collectives: 128 us -> 131 us
  starting transfers between devices: 35.1 us -> 37.6 us
    pallas_call x17, Pallas kernels: 27.7 us -> 21.5 us  [run(): pl.pallas_call(kernel, out_shape=outs[0] if len(outs) == 1 else outs, scr...]
    unnamed x79 -> x60, local copies, waits for them, and re-layouts: 7.49 us -> 2.64 us
    ppermute x8, waiting for transfers between devices: 14.6 us -> 19.1 us  [shift(): lax.ppermute(value, 'grid', [(s, (s + step) % size) for s in range(size)])]
    all_to_all x1, waiting for transfers between devices: 3.39 us -> 0.01 us  [route_leaf(): lax.all_to_all(value, ('leaf', 'grid'), split_axis=0, concat_axis=0, tile...]
    ppermute x8, starting transfers between devices: 8.53 us -> 11.7 us  [shift(): lax.ppermute(value, 'grid', [(s, (s + step) % size) for s in range(size)])]
    all_to_all x10, blocking collectives: 128 us -> 131 us  [between(): lax.all_to_all(value, 'leaf', split_axis=0, concat_axis=0, tiled=True, ax...]
  transfers between devices with their start and end apart: 26 -> 26, of which waited for: 15 -> 14; matrix products, arithmetic and copies ran while one was open for 0% -> 0% of each run, Pallas kernels for 3% -> 3%
where the time goes in v3:
time: 232 us; the launch traced here: 231 us
  blocking collectives  131 us (56%)
  starting transfers between devices  37.6 us (16%)
  waiting for transfers between devices  37 us (16%)
  Pallas kernels  21.5 us (9%)
  local copies, waits for them, and re-layouts  2.7 us (1%)
    all_to_all x10, blocking collectives, between(): lax.all_to_all(value, 'leaf', split_axis=0, concat_axis=0, tiled=True, ax...  131 us
    pallas_call x17, Pallas kernels, run(): pl.pallas_call(kernel, out_shape=outs[0] if len(outs) == 1 else outs, scr...  21.5 us
    ppermute x8, waiting for transfers between devices, shift(): lax.ppermute(value, 'grid', [(s, (s + step) % size) for s in range(size)])  19.1 us
    ppermute x8, starting transfers between devices, shift(): lax.ppermute(value, 'grid', [(s, (s + step) % size) for s in range(size)])  11.7 us
    ppermute x16, starting transfers between devices, swap(): return lax.ppermute(value, axis, pairs)  11.6 us
    all_to_all x1, starting transfers between devices, route_leaf(): lax.all_to_all(value, ('leaf', 'grid'), split_axis=0, concat_axis=0, tile...  11 us
    ppermute x16, waiting for transfers between devices, swap(): return lax.ppermute(value, axis, pairs)  9.09 us
    all_to_all x1, waiting for transfers between devices, between(): lax.all_to_all(value, 'leaf', split_axis=0, concat_axis=0, tiled=True, ax...  8.77 us
  transfers between devices with their start and end apart: 26, of which 14 were waited for; matrix products, arithmetic and copies ran while one was open for 0% of the time, Pallas kernels for 3%

profile of v3, /device:TPU:2, one launch (start us, length us, event | category | flops | bytes accessed | tf_op | source)
XLA Modules:
  0.0 231.0 jit_solution(13412670542602892525)
XLA Ops:
  0.6 1.5 shard_map.309
  2.1 1.6 collective-permute-start.2
  3.7 2.8 %collective-permute-start.1 = (f32[144,128]{1,0:T(8,128)S(1)}, f32[144,128]{1,0:T(8,128)S(1)}, u32[]{:S(2)}, u32[]{:S(2)}) collective-permute-start(f32[144,128]{1,0:T(8,128)S(1)} %get-tuple-element.67.s0), channel_id=1, source_target_pairs={{0,2},{1,3},{2,0},{3,1},{4,6},{5,7},{6,4},{7,5},{8,10},{9,11},{10,... | collective-permute-start | bytes 221192 | tf_op jit(solution)/shard_map/ppermute | solution.py:614
  6.5 0.0 collective-permute-start
  6.5 1.3 shard_map.310
  7.9 2.0 collective-permute-done.1.s2
  9.8 1.0 collective-permute-done.s1
  10.9 1.2 shard_map.311
  12.1 0.6 copy-done.26
  12.7 0.6 copy-done.28
  13.3 11.0 %all-to-all-start = ((f32[64,8,128]{2,1,0:T(8,128)}), f32[64,8,128]{2,1,0:T(8,128)S(1)}, u32[]{:S(2)}, u32[]{:S(2)}) async-start(f32[64,8,128]{2,1,0:T(8,128)} %bitcast.9), calls=%async_computation | async-start | bytes 524288 | tf_op jit(solution)/shard_map/all_to_all | solution.py:645
  24.3 0.5 collective-permute-start.4
  24.8 1.6 collective-permute-start.3
  26.4 10.6 %collective-permute-done.4.refs_2_ = f32[656,128]{1,0:T(8,128)S(1)} collective-permute-done((f32[656,128]{1,0:T(8,128)S(1)}, f32[656,128]{1,0:T(8,128)S(1)}, u32[]{:S(2)}, u32[]{:S(2)}) %collective-permute-start.4) | collective-permute-done | bytes 335904 | tf_op jit(solution)/shard_map/ppermute | solution.py:619
  37.0 0.6 collective-permute-done.3.refs_1_
  37.6 0.9 collective-permute-start.5
  38.5 2.3 %collective-permute-start.6 = (f32[264,128]{1,0:T(8,128)S(1)}, f32[264,128]{1,0:T(8,128)S(1)}, u32[]{:S(2)}, u32[]{:S(2)}) collective-permute-start(f32[264,128]{1,0:T(8,128)S(1)} %slice.13), channel_id=1, source_target_pairs={{0,3},{1,0},{2,1},{3,2},{4,7},{5,4},{6,5},{7,6},{8,11},{9,8},{10,9... | collective-permute-start | bytes 405512 | tf_op jit(solution)/shard_map/ppermute | solution.py:619
  40.8 3.9 %collective-permute-done.6.refs_4_ = f32[264,128]{1,0:T(8,128)S(1)} collective-permute-done((f32[264,128]{1,0:T(8,128)S(1)}, f32[264,128]{1,0:T(8,128)S(1)}, u32[]{:S(2)}, u32[]{:S(2)}) %collective-permute-start.6) | collective-permute-done | bytes 135200 | tf_op jit(solution)/shard_map/ppermute | solution.py:619
  44.7 0.6 collective-permute-done.5.refs_3_
  45.3 3.0 %collective-permute-start.13 = (f32[1056,128]{1,0:T(8,128)S(1)}, f32[1056,128]{1,0:T(8,128)S(1)}, u32[]{:S(2)}, u32[]{:S(2)}) collective-permute-start(f32[1056,128]{1,0:T(8,128)S(1)} %get-tuple-element.81.refs_0_), channel_id=1, source_target_pairs={{0,3},{1,0},{2,1},{3,2},{4,7},{5,4},{6,5},{7,6},{8,11},{9,8},{10,9... | collective-permute-start | bytes 1622024 | tf_op jit(solution)/shard_map/ppermute | solution.py:619
  48.3 0.5 collective-permute-start.11
  48.8 0.2 collective-permute-start.9
  49.0 1.1 collective-permute-done.11.refs_9_
  50.1 0.1 collective-permute-start.10
  50.3 0.3 collective-permute-done.9.refs_7_
  50.6 1.0 collective-permute-done.10.refs_8_
  51.6 0.7 copy-done.14
  52.3 2.0 shard_map.312
  54.3 0.7 copy-done.22
  55.0 13.4 %all_to_all.132 = f32[8,8,128]{2,1,0:T(8,128)S(1)} all-to-all(f32[8,8,128]{2,1,0:T(8,128)S(1)} %bitcast.58), channel_id=1, replica_groups={{0,8,16,24,32,40,48,56},{4,12,20,28,36,44,52,60},{64,72,80,88,96,104,11..., dimensions={0} | all-to-all | bytes 65536 | tf_op jit(solution)/shard_map/all_to_all | solution.py:637
  68.5 2.8 %collective-permute-start.14 = (f32[656,128]{1,0:T(8,128)S(1)}, f32[656,128]{1,0:T(8,128)}, u32[]{:S(2)}, u32[]{:S(2)}) collective-permute-start(f32[656,128]{1,0:T(8,128)S(1)} %slice.14), channel_id=1, source_target_pairs={{0,1},{1,2},{2,3},{3,0},{4,5},{5,6},{6,7},{7,4},{8,9},{9,10},{10,1... | collective-permute-start | bytes 1007624 | tf_op jit(solution)/shard_map/ppermute | solution.py:619
  71.3 0.6 collective-permute-start.15
  72.0 0.5 collective-permute-start.17
  72.5 2.9 %shard_map.313 = (f32[192,128]{1,0:T(8,128)}, f32[8,1024]{1,0:T(8,128)S(1)}, f32[8,128]{1,0:T(8,128)S(1)}) custom-call(f32[656,128]{1,0:T(8,128)} %copy-done.4, f32[656,128]{1,0:T(8,128)} %copy-done, f32[656,128]{1,0:T(8,128)} %copy-done.2, f32[392,128]{1,0:T(8,128)} %copy-done.12, f32[264,128]{1,0:T(8,128)} %copy-done.18, f32[656,128]{1,0:T(8,128)} %copy-done.6, ...), custom_call_target="tpu_custom_call" | custom-call | tf_op jit(solution)/shard_map/pallas_call | solution.py:599
  75.3 3.1 %collective-permute-done.15.refs_4_ = f32[400,128]{1,0:T(8,128)} collective-permute-done((f32[400,128]{1,0:T(8,128)S(1)}, f32[400,128]{1,0:T(8,128)}, u32[]{:S(2)}, u32[]{:S(2)}) %collective-permute-start.15) | collective-permute-done | bytes 204832 | tf_op jit(solution)/shard_map/ppermute | solution.py:619
  78.4 0.4 collective-permute-done.14.refs_3_
  78.8 0.5 collective-permute-start.20
  79.3 3.4 %all-to-all-start.2 = ((f32[8,24,128]{2,1,0:T(8,128)}), f32[8,24,128]{2,1,0:T(8,128)S(1)}, u32[]{:S(2)}, u32[]{:S(2)}) async-start(f32[8,24,128]{2,1,0:T(8,128)} %bitcast.13), calls=%async_computation.2 | async-start | bytes 196608 | tf_op jit(solution)/shard_map/all_to_all | solution.py:637
  82.7 8.8 %all-to-all-done.2 = f32[8,24,128]{2,1,0:T(8,128)S(1)} async-done(((f32[8,24,128]{2,1,0:T(8,128)}), f32[8,24,128]{2,1,0:T(8,128)S(1)}, u32[]{:S(2)}, u32[]{:S(2)}) %all-to-all-start.2) | async-done | bytes 98336 | tf_op jit(solution)/shard_map/all_to_all | solution.py:637
  91.5 2.0 shard_map.314
  93.5 1.8 shard_map.315
  95.3 11.3 %all_to_all.133 = f32[16,16,128]{2,1,0:T(8,128)S(1)} all-to-all(f32[16,16,128]{2,1,0:T(8,128)S(1)} %bitcast.52), channel_id=1, replica_groups={{0,8,16,24,32,40,48,56,64,72,80,88,96,104,112,120},{4,12,20,28,36,44,52..., dimensions={0} | all-to-all | bytes 262144 | tf_op jit(solution)/shard_map/all_to_all | solution.py:637
  106.6 1.0 shard_map.316
  107.6 11.8 %all_to_all.134 = f32[16,24,128]{2,1,0:T(8,128)S(1)} all-to-all(f32[16,24,128]{2,1,0:T(8,128)S(1)} %bitcast.49), channel_id=1, replica_groups={{0,8,16,24,32,40,48,56,64,72,80,88,96,104,112,120},{4,12,20,28,36,44,52..., dimensions={0} | all-to-all | bytes 393216 | tf_op jit(solution)/shard_map/all_to_all | solution.py:637
  119.4 0.9 shard_map.317
  120.3 17.1 %all_to_all.135 = f32[32,16,128]{2,1,0:T(8,128)S(1)} all-to-all(f32[32,16,128]{2,1,0:T(8,128)S(1)} %bitcast.48), channel_id=1, replica_groups={{0,8,16,24,32,40,48,56,64,72,80,88,96,104,112,120,128,136,144,152,160,1..., dimensions={0} | all-to-all | bytes 524288 | tf_op jit(solution)/shard_map/all_to_all | solution.py:637
  137.4 0.8 shard_map.318
  138.2 15.9 %all_to_all.136 = f32[32,24,128]{2,1,0:T(8,128)S(1)} all-to-all(f32[32,24,128]{2,1,0:T(8,128)S(1)} %bitcast.46), channel_id=1, replica_groups={{0,8,16,24,32,40,48,56,64,72,80,88,96,104,112,120,128,136,144,152,160,1..., dimensions={0} | all-to-all | bytes 786432 | tf_op jit(solution)/shard_map/all_to_all | solution.py:637
  154.1 1.3 shard_map.319
  155.4 15.5 %all_to_all.137 = f32[32,8,128]{2,1,0:T(8,128)S(1)} all-to-all(f32[32,8,128]{2,1,0:T(8,128)S(1)} %bitcast.53), channel_id=1, replica_groups={{0,8,16,24,32,40,48,56,64,72,80,88,96,104,112,120,128,136,144,152,160,1..., dimensions={0} | all-to-all | bytes 262144 | tf_op jit(solution)/shard_map/all_to_all | solution.py:637
  170.9 0.4 shard_map.320
  171.4 11.2 %all_to_all.138 = f32[16,16,128]{2,1,0:T(8,128)S(1)} all-to-all(f32[16,16,128]{2,1,0:T(8,128)S(1)} %bitcast.55), channel_id=1, replica_groups={{0,8,16,24,32,40,48,56,64,72,80,88,96,104,112,120},{4,12,20,28,36,44,52..., dimensions={0} | all-to-all | bytes 262144 | tf_op jit(solution)/shard_map/all_to_all | solution.py:637
  182.6 1.4 shard_map.321
  184.0 11.7 %all_to_all.139 = f32[16,8,128]{2,1,0:T(8,128)S(1)} all-to-all(f32[16,8,128]{2,1,0:T(8,128)S(1)} %bitcast.56), channel_id=1, replica_groups={{0,8,16,24,32,40,48,56,64,72,80,88,96,104,112,120},{4,12,20,28,36,44,52..., dimensions={0} | all-to-all | bytes 131072 | tf_op jit(solution)/shard_map/all_to_all | solution.py:637
  195.8 0.4 shard_map.322
  196.2 12.8 %all_to_all.140 = f32[8,32,128]{2,1,0:T(8,128)S(1)} all-to-all(f32[8,32,128]{2,1,0:T(8,128)S(1)} %bitcast.54), channel_id=1, replica_groups={{0,8,16,24,32,40,48,56},{4,12,20,28,36,44,52,60},{64,72,80,88,96,104,11..., dimensions={0} | all-to-all | bytes 262144 | tf_op jit(solution)/shard_map/all_to_all | solution.py:637
  209.0 1.3 shard_map.323
  210.3 10.5 %all_to_all.141 = f32[8,8,128]{2,1,0:T(8,128)S(1)} all-to-all(f32[8,8,128]{2,1,0:T(8,128)S(1)} %bitcast.57), channel_id=1, replica_groups={{0,8,16,24,32,40,48,56},{4,12,20,28,36,44,52,60},{64,72,80,88,96,104,11..., dimensions={0} | all-to-all | bytes 65536 | tf_op jit(solution)/shard_map/all_to_all | solution.py:637
  220.8 0.3 shard_map.324.s0
  221.1 1.8 collective-permute-start.23
  222.9 3.5 %collective-permute-start.22 = (f32[16,128]{1,0:T(8,128)S(1)}, f32[16,128]{1,0:T(8,128)S(1)}, u32[]{:S(2)}, u32[]{:S(2)}) collective-permute-start(f32[16,128]{1,0:T(8,128)S(1)} %shard_map.324.s0), channel_id=1, source_target_pairs={{0,2},{1,3},{2,0},{3,1},{4,6},{5,7},{6,4},{7,5},{8,10},{9,11},{10,... | collective-permute-start | bytes 24584 | tf_op jit(solution)/shard_map/ppermute | solution.py:614
  226.4 1.6 collective-permute-done.22.s2
  228.1 2.0 collective-permute-done.21.s1
  230.1 0.9 shard_map.325
  (79 shorter events, 0.2 us)
Async XLA Ops:
  2.1 8.8 %copy-start.16 = (f32[768,128]{1,0:T(8,128)}, f32[768,128]{1,0:T(8,128)S(1)}, u32[]{:S(2)}) copy-start(f32[768,128]{1,0:T(8,128)S(1)} %get-tuple-element.74.hold) | copy-start | bytes 1179652
  2.1 5.8 %collective-permute-start.2 = (f32[144,128]{1,0:T(8,128)S(1)}, f32[144,128]{1,0:T(8,128)S(1)}, u32[]{:S(2)}, u32[]{:S(2)}) collective-permute-start(f32[144,128]{1,0:T(8,128)S(1)} %get-tuple-element.67.s0), channel_id=1, source_target_pairs={{0,3},{1,2},{2,1},{3,0},{4,7},{5,6},{6,5},{7,4},{8,11},{9,10},{10,... | collective-permute-start | bytes 221192 | tf_op jit(solution)/shard_map/ppermute | solution.py:614
  3.7 6.1 %collective-permute-start.1 = (f32[144,128]{1,0:T(8,128)S(1)}, f32[144,128]{1,0:T(8,128)S(1)}, u32[]{:S(2)}, u32[]{:S(2)}) collective-permute-start(f32[144,128]{1,0:T(8,128)S(1)} %get-tuple-element.67.s0), channel_id=1, source_target_pairs={{0,2},{1,3},{2,0},{3,1},{4,6},{5,7},{6,4},{7,5},{8,10},{9,11},{10,... | collective-permute-start | bytes 221192 | tf_op jit(solution)/shard_map/ppermute | solution.py:614
  6.5 4.4 %collective-permute-start = (f32[144,128]{1,0:T(8,128)S(1)}, f32[144,128]{1,0:T(8,128)S(1)}, u32[]{:S(2)}, u32[]{:S(2)}) collective-permute-start(f32[144,128]{1,0:T(8,128)S(1)} %get-tuple-element.67.s0), channel_id=1, source_target_pairs={{0,1},{1,0},{2,3},{3,2},{4,5},{5,4},{6,7},{7,6},{8,9},{9,8},{10,11... | collective-permute-start | bytes 221192 | tf_op jit(solution)/shard_map/ppermute | solution.py:614
  7.9 30.6 %copy-start.4 = (f32[656,128]{1,0:T(8,128)}, f32[656,128]{1,0:T(8,128)S(1)}, u32[]{:S(2)}) copy-start(f32[656,128]{1,0:T(8,128)S(1)} %get-tuple-element.65.refs_0_) | copy-start | bytes 1007620
  12.1 0.6 copy-start.26
  12.7 0.6 copy-start.28
  13.3 24.3 %all-to-all-start = ((f32[64,8,128]{2,1,0:T(8,128)}), f32[64,8,128]{2,1,0:T(8,128)S(1)}, u32[]{:S(2)}, u32[]{:S(2)}) async-start(f32[64,8,128]{2,1,0:T(8,128)} %bitcast.9), calls=%async_computation | async-start | bytes 524288 | tf_op jit(solution)/shard_map/all_to_all | solution.py:645
  24.3 12.7 %collective-permute-start.4 = (f32[656,128]{1,0:T(8,128)S(1)}, f32[656,128]{1,0:T(8,128)S(1)}, u32[]{:S(2)}, u32[]{:S(2)}) collective-permute-start(f32[656,128]{1,0:T(8,128)S(1)} %get-tuple-element.65.refs_0_), channel_id=1, source_target_pairs={{0,3},{1,0},{2,1},{3,2},{4,7},{5,4},{6,5},{7,6},{8,11},{9,8},{10,9... | collective-permute-start | bytes 1007624 | tf_op jit(solution)/shard_map/ppermute | solution.py:619
  24.8 12.8 %collective-permute-start.3 = (f32[656,128]{1,0:T(8,128)S(1)}, f32[656,128]{1,0:T(8,128)S(1)}, u32[]{:S(2)}, u32[]{:S(2)}) collective-permute-start(f32[656,128]{1,0:T(8,128)S(1)} %get-tuple-element.65.refs_0_), channel_id=1, source_target_pairs={{0,1},{1,2},{2,3},{3,0},{4,5},{5,6},{6,7},{7,4},{8,9},{9,10},{10,1... | collective-permute-start | bytes 1007624 | tf_op jit(solution)/shard_map/ppermute | solution.py:619
  37.0 11.8 %copy-start.2 = (f32[656,128]{1,0:T(8,128)}, f32[656,128]{1,0:T(8,128)S(1)}, u32[]{:S(2)}) copy-start(f32[656,128]{1,0:T(8,128)S(1)} %collective-permute-done.4.refs_2_) | copy-start | bytes 1007620
  37.6 10.7 %copy-start = (f32[656,128]{1,0:T(8,128)}, f32[656,128]{1,0:T(8,128)S(1)}, u32[]{:S(2)}) copy-start(f32[656,128]{1,0:T(8,128)S(1)} %collective-permute-done.3.refs_1_) | copy-start | bytes 1007620
  37.6 7.7 %collective-permute-start.5 = (f32[392,128]{1,0:T(8,128)S(1)}, f32[392,128]{1,0:T(8,128)S(1)}, u32[]{:S(2)}, u32[]{:S(2)}) collective-permute-start(f32[392,128]{1,0:T(8,128)S(1)} %slice.12), channel_id=1, source_target_pairs={{0,1},{1,2},{2,3},{3,0},{4,5},{5,6},{6,7},{7,4},{8,9},{9,10},{10,1... | collective-permute-start | bytes 602120 | tf_op jit(solution)/shard_map/ppermute | solution.py:619
  38.5 10.3 %collective-permute-start.7 = (f32[656,128]{1,0:T(8,128)S(1)}, f32[656,128]{1,0:T(8,128)S(1)}, u32[]{:S(2)}, u32[]{:S(2)}) collective-permute-start(f32[656,128]{1,0:T(8,128)S(1)} %get-tuple-element.65.refs_0_), channel_id=1, source_target_pairs={{0,4},{4,0},{8,12},{12,8},{16,20},{20,16},{24,28},{28,24},{32,36},... | collective-permute-start | bytes 1007624 | tf_op jit(solution)/shard_map/ppermute | solution.py:614
  38.5 6.2 %collective-permute-start.6 = (f32[264,128]{1,0:T(8,128)S(1)}, f32[264,128]{1,0:T(8,128)S(1)}, u32[]{:S(2)}, u32[]{:S(2)}) collective-permute-start(f32[264,128]{1,0:T(8,128)S(1)} %slice.13), channel_id=1, source_target_pairs={{0,3},{1,0},{2,1},{3,2},{4,7},{5,4},{6,5},{7,6},{8,11},{9,8},{10,9... | collective-permute-start | bytes 405512 | tf_op jit(solution)/shard_map/ppermute | solution.py:619
  44.7 6.9 %copy-start.18 = (f32[264,128]{1,0:T(8,128)}, f32[264,128]{1,0:T(8,128)S(1)}, u32[]{:S(2)}) copy-start(f32[264,128]{1,0:T(8,128)S(1)} %collective-permute-done.6.refs_4_) | copy-start | bytes 405508
  45.3 6.2 %copy-start.12 = (f32[392,128]{1,0:T(8,128)}, f32[392,128]{1,0:T(8,128)S(1)}, u32[]{:S(2)}) copy-start(f32[392,128]{1,0:T(8,128)S(1)} %collective-permute-done.5.refs_3_) | copy-start | bytes 602116
  45.3 23.1 %collective-permute-start.13 = (f32[1056,128]{1,0:T(8,128)S(1)}, f32[1056,128]{1,0:T(8,128)S(1)}, u32[]{:S(2)}, u32[]{:S(2)}) collective-permute-start(f32[1056,128]{1,0:T(8,128)S(1)} %get-tuple-element.81.refs_0_), channel_id=1, source_target_pairs={{0,3},{1,0},{2,1},{3,2},{4,7},{5,4},{6,5},{7,6},{8,11},{9,8},{10,9... | collective-permute-start | bytes 1622024 | tf_op jit(solution)/shard_map/ppermute | solution.py:619
  48.3 20.2 %collective-permute-start.12 = (f32[1056,128]{1,0:T(8,128)S(1)}, f32[1056,128]{1,0:T(8,128)S(1)}, u32[]{:S(2)}, u32[]{:S(2)}) collective-permute-start(f32[1056,128]{1,0:T(8,128)S(1)} %get-tuple-element.81.refs_0_), channel_id=1, source_target_pairs={{0,1},{1,2},{2,3},{3,0},{4,5},{5,6},{6,7},{7,4},{8,9},{9,10},{10,1... | collective-permute-start | bytes 1622024 | tf_op jit(solution)/shard_map/ppermute | solution.py:619
  48.3 2.0 collective-permute-start.8
  48.3 1.8 collective-permute-start.11
  48.8 2.8 %copy-start.6 = (f32[656,128]{1,0:T(8,128)}, f32[656,128]{1,0:T(8,128)S(1)}, u32[]{:S(2)}) copy-start(f32[656,128]{1,0:T(8,128)S(1)} %collective-permute-done.7.refs_5_) | copy-start | bytes 1007620
  48.8 1.8 collective-permute-start.9
  50.1 1.5 copy-start.20
  50.1 1.4 collective-permute-start.10
  50.3 1.3 copy-start.8
  50.6 1.0 copy-start.10
  51.6 0.7 copy-start.14
  54.3 0.7 copy-start.22
  55.0 13.4 %copy-start.24 = (f32[64,128]{1,0:T(8,128)}, f32[64,128]{1,0:T(8,128)S(1)}, u32[]{:S(2)}) copy-start(f32[64,128]{1,0:T(8,128)S(1)} %get-tuple-element.93.refs_11_) | copy-start | bytes 98308
  68.5 10.3 %collective-permute-start.14 = (f32[656,128]{1,0:T(8,128)S(1)}, f32[656,128]{1,0:T(8,128)}, u32[]{:S(2)}, u32[]{:S(2)}) collective-permute-start(f32[656,128]{1,0:T(8,128)S(1)} %slice.14), channel_id=1, source_target_pairs={{0,1},{1,2},{2,3},{3,0},{4,5},{5,6},{6,7},{7,4},{8,9},{9,10},{10,1... | collective-permute-start | bytes 1007624 | tf_op jit(solution)/shard_map/ppermute | solution.py:619
  71.3 7.1 %collective-permute-start.15 = (f32[400,128]{1,0:T(8,128)S(1)}, f32[400,128]{1,0:T(8,128)}, u32[]{:S(2)}, u32[]{:S(2)}) collective-permute-start(f32[400,128]{1,0:T(8,128)S(1)} %slice.15), channel_id=1, source_target_pairs={{0,3},{1,0},{2,1},{3,2},{4,7},{5,4},{6,5},{7,6},{8,11},{9,8},{10,9... | collective-permute-start | bytes 614408 | tf_op jit(solution)/shard_map/ppermute | solution.py:619
  71.9 10.7 %collective-permute-start.16 = (f32[1056,128]{1,0:T(8,128)S(1)}, f32[1056,128]{1,0:T(8,128)S(1)}, u32[]{:S(2)}, u32[]{:S(2)}) collective-permute-start(f32[1056,128]{1,0:T(8,128)S(1)} %get-tuple-element.81.refs_0_), channel_id=1, source_target_pairs={{0,4},{4,0},{8,12},{12,8},{16,20},{20,16},{24,28},{28,24},{32,36},... | collective-permute-start | bytes 1622024 | tf_op jit(solution)/shard_map/ppermute | solution.py:614
  72.0 19.5 %collective-permute-start.17 = (f32[1056,128]{1,0:T(8,128)S(1)}, f32[1056,128]{1,0:T(8,128)S(1)}, u32[]{:S(2)}, u32[]{:S(2)}) collective-permute-start(f32[1056,128]{1,0:T(8,128)S(1)} %collective-permute-done.12.refs_1_), channel_id=1, source_target_pairs={{0,4},{4,0},{8,12},{12,8},{16,20},{20,16},{24,28},{28,24},{32,36},... | collective-permute-start | bytes 1622024 | tf_op jit(solution)/shard_map/ppermute | solution.py:614
  72.5 19.0 %collective-permute-start.18 = (f32[1056,128]{1,0:T(8,128)S(1)}, f32[1056,128]{1,0:T(8,128)S(1)}, u32[]{:S(2)}, u32[]{:S(2)}) collective-permute-start(f32[1056,128]{1,0:T(8,128)S(1)} %collective-permute-done.13.refs_2_), channel_id=1, source_target_pairs={{0,4},{4,0},{8,12},{12,8},{16,20},{20,16},{24,28},{28,24},{32,36},... | collective-permute-start | bytes 1622024 | tf_op jit(solution)/shard_map/ppermute | solution.py:614
  78.8 12.7 %collective-permute-start.19 = (f32[656,128]{1,0:T(8,128)}, f32[656,128]{1,0:T(8,128)}, u32[]{:S(2)}, u32[]{:S(2)}) collective-permute-start(f32[656,128]{1,0:T(8,128)} %collective-permute-done.14.refs_3_), channel_id=1, source_target_pairs={{0,4},{4,0},{8,12},{12,8},{16,20},{20,16},{24,28},{28,24},{32,36},... | collective-permute-start | bytes 1007624 | tf_op jit(solution)/shard_map/ppermute | solution.py:614
  78.8 12.7 %collective-permute-start.20 = (f32[400,128]{1,0:T(8,128)}, f32[400,128]{1,0:T(8,128)}, u32[]{:S(2)}, u32[]{:S(2)}) collective-permute-start(f32[400,128]{1,0:T(8,128)} %collective-permute-done.15.refs_4_), channel_id=1, source_target_pairs={{0,4},{4,0},{8,12},{12,8},{16,20},{20,16},{24,28},{28,24},{32,36},... | collective-permute-start | bytes 614408 | tf_op jit(solution)/shard_map/ppermute | solution.py:614
  79.3 12.1 %all-to-all-start.2 = ((f32[8,24,128]{2,1,0:T(8,128)}), f32[8,24,128]{2,1,0:T(8,128)S(1)}, u32[]{:S(2)}, u32[]{:S(2)}) async-start(f32[8,24,128]{2,1,0:T(8,128)} %bitcast.13), calls=%async_computation.2 | async-start | bytes 196608 | tf_op jit(solution)/shard_map/all_to_all | solution.py:637
  91.5 2.0 copy-start.25
  182.6 13.1 %copy-start.1 = (f32[656,128]{1,0:T(8,128)S(1)}, f32[656,128]{1,0:T(8,128)}, u32[]{:S(2)}) copy-start(f32[656,128]{1,0:T(8,128)} %copy-done) | copy-start | bytes 1007620
  182.6 13.1 %copy-start.3 = (f32[656,128]{1,0:T(8,128)S(1)}, f32[656,128]{1,0:T(8,128)}, u32[]{:S(2)}) copy-start(f32[656,128]{1,0:T(8,128)} %copy-done.2) | copy-start | bytes 1007620
  182.6 13.1 %copy-start.5 = (f32[656,128]{1,0:T(8,128)S(1)}, f32[656,128]{1,0:T(8,128)}, u32[]{:S(2)}) copy-start(f32[656,128]{1,0:T(8,128)} %copy-done.4) | copy-start | bytes 1007620
  182.6 13.1 %copy-start.7 = (f32[656,128]{1,0:T(8,128)S(1)}, f32[656,128]{1,0:T(8,128)}, u32[]{:S(2)}) copy-start(f32[656,128]{1,0:T(8,128)} %copy-done.6) | copy-start | bytes 1007620
  182.6 13.1 %copy-start.9 = (f32[656,128]{1,0:T(8,128)S(1)}, f32[656,128]{1,0:T(8,128)}, u32[]{:S(2)}) copy-start(f32[656,128]{1,0:T(8,128)} %copy-done.8) | copy-start | bytes 1007620
  182.6 13.1 %copy-start.11 = (f32[656,128]{1,0:T(8,128)S(1)}, f32[656,128]{1,0:T(8,128)}, u32[]{:S(2)}) copy-start(f32[656,128]{1,0:T(8,128)} %copy-done.10) | copy-start | bytes 1007620
  182.6 13.1 %copy-start.13 = (f32[392,128]{1,0:T(8,128)S(1)}, f32[392,128]{1,0:T(8,128)}, u32[]{:S(2)}) copy-start(f32[392,128]{1,0:T(8,128)} %copy-done.12) | copy-start | bytes 602116
  182.6 13.1 %copy-start.15 = (f32[392,128]{1,0:T(8,128)S(1)}, f32[392,128]{1,0:T(8,128)}, u32[]{:S(2)}) copy-start(f32[392,128]{1,0:T(8,128)} %copy-done.14) | copy-start | bytes 602116
  182.6 13.1 %copy-start.21 = (f32[264,128]{1,0:T(8,128)S(1)}, f32[264,128]{1,0:T(8,128)}, u32[]{:S(2)}) copy-start(f32[264,128]{1,0:T(8,128)} %copy-done.20) | copy-start | bytes 405508
  184.0 11.8 %copy-start.19 = (f32[264,128]{1,0:T(8,128)S(1)}, f32[264,128]{1,0:T(8,128)}, u32[]{:S(2)}) copy-start(f32[264,128]{1,0:T(8,128)} %copy-done.18) | copy-start | bytes 405508
  196.2 12.8 %copy-start.23 = (f32[64,8,128]{2,1,0:T(8,128)S(1)}, f32[64,8,128]{2,1,0:T(8,128)}, u32[]{:S(2)}) copy-start(f32[64,8,128]{2,1,0:T(8,128)} %copy-done.22) | copy-start | bytes 786436
  209.0 11.8 %copy-start.17 = (f32[768,128]{1,0:T(8,128)S(1)}, f32[768,128]{1,0:T(8,128)}, u32[]{:S(2)}) copy-start(f32[768,128]{1,0:T(8,128)} %copy-done.16) | copy-start | bytes 1179652
  210.3 10.5 %copy-start.29 = (f32[8,128]{1,0:T(8,128)S(1)}, f32[8,128]{1,0:T(8,128)}, u32[]{:S(2)}) copy-start(f32[8,128]{1,0:T(8,128)} %copy-done.28) | copy-start | bytes 12292
  220.8 9.3 %copy-start.27 = (f32[8,128]{1,0:T(8,128)S(1)}, f32[8,128]{1,0:T(8,128)}, u32[]{:S(2)}) copy-start(f32[8,128]{1,0:T(8,128)} %copy-done.26) | copy-start | bytes 12292
  221.1 5.3 %collective-permute-start.23 = (f32[16,128]{1,0:T(8,128)S(1)}, f32[16,128]{1,0:T(8,128)S(1)}, u32[]{:S(2)}, u32[]{:S(2)}) collective-permute-start(f32[16,128]{1,0:T(8,128)S(1)} %shard_map.324.s0), channel_id=1, source_target_pairs={{0,3},{1,2},{2,1},{3,0},{4,7},{5,6},{6,5},{7,4},{8,11},{9,10},{10,... | collective-permute-start | bytes 24584 | tf_op jit(solution)/shard_map/ppermute | solution.py:614
  222.9 5.2 %collective-permute-start.22 = (f32[16,128]{1,0:T(8,128)S(1)}, f32[16,128]{1,0:T(8,128)S(1)}, u32[]{:S(2)}, u32[]{:S(2)}) collective-permute-start(f32[16,128]{1,0:T(8,128)S(1)} %shard_map.324.s0), channel_id=1, source_target_pairs={{0,2},{1,3},{2,0},{3,1},{4,6},{5,7},{6,4},{7,5},{8,10},{9,11},{10,... | collective-permute-start | bytes 24584 | tf_op jit(solution)/shard_map/ppermute | solution.py:614
  226.4 3.7 %collective-permute-start.21 = (f32[16,128]{1,0:T(8,128)S(1)}, f32[16,128]{1,0:T(8,128)S(1)}, u32[]{:S(2)}, u32[]{:S(2)}) collective-permute-start(f32[16,128]{1,0:T(8,128)S(1)} %shard_map.324.s0), channel_id=1, source_target_pairs={{0,1},{1,0},{2,3},{3,2},{4,5},{5,4},{6,7},{7,6},{8,9},{9,8},{10,11... | collective-permute-start | bytes 24584 | tf_op jit(solution)/shard_map/ppermute | solution.py:614
